TPU v7x, 32 devices: a whole 2x2x4 slice. The times are simulated.
32 devices in a mesh: grp: 2 (over x), dev: 16 (over z, y, core).
Axes of the slice: x: 2, y: 2, z: 4, core: 2. Of those that a mesh axis runs over, the one named last changes fastest.
Arguments:
- query: bfloat16 [64, 128, 4096], P(('grp', 'dev')), may hold values from -100 to 100
- grad_out: bfloat16 [64, 128, 4096], P(('grp', 'dev')), may hold values from -6 to 6
- branch_kv: bfloat16 [64, 128, 1024], P(('grp', 'dev')), may hold values from -6 to 6
- root_kv: bfloat16 [1024, 1024], P('dev'), may hold values from -24 to 24
- lengths: int32 [64], P(('grp', 'dev')), may hold values from 0 to 128, as said below
- segments: int32 [64], P(('grp', 'dev')), may hold values from 0 to 3
Outputs:
- query_grad: bfloat16 [64, 128, 4096], P(('grp', 'dev'))
- branch_grad: bfloat16 [64, 128, 1024], P(('grp', 'dev'))
- root_grad: float32 [1024, 1024], P('dev')
Inputs may be any that keep to these rules, and one draw needn't show every extreme that they name: `lengths`: A slot with length 0 holds no branch. A device's slots with live positions come before its empty slots. Within a group, device d and device d + 16/2 (d < 8) hold exactly 2 slots with live positions together; a quarter of a group's devices hold 2 such slots and a quarter hold none.
All inputs are finite; a program needn't handle non-finite values.
Results may differ from a plain program's by a relative error of at most 0.0069.
Values may be sent and summed in bfloat16 or wider, within the bound.
No kernel may reach another device: no remote copies, remote signals or barrier semaphores. Data moves between devices by JAX's collectives and lax.ppermute only.
A program may use at most 128 MiB of HBM per device.

v0:
```python
import jax
import jax.numpy as jnp
from jax import lax
from jax.sharding import PartitionSpec as P

H = 32
KVH = 4
DH = 128
SEGS = 4


def passed_along(block, axis, distance):
    devices = range(lax.axis_size(axis))
    route = [((i - distance) % len(devices), i) for i in devices]
    return lax.ppermute(block, axis, route)


def tile_grads(query, grad, branch, length, segment, root_keys):
    rows = query.shape[0]
    width = KVH * DH
    groups = H // KVH
    roots = root_keys.shape[0]
    everything = jnp.concatenate([root_keys, branch], axis=0)
    span = roots + rows
    scale = DH ** (-0.5)
    row_pos = lax.broadcasted_iota(jnp.int32, (rows, span), 0)
    col_pos = lax.broadcasted_iota(jnp.int32, (rows, span), 1)
    visible = jnp.where(
        col_pos < roots, col_pos < (segment + 1) * (roots // SEGS), col_pos - roots <= row_pos
    )
    live = lax.broadcasted_iota(jnp.int32, (rows, 1), 0) < length
    grad = jnp.where(live, grad, jnp.zeros_like(grad))
    dq_parts = []
    dk_parts = []
    dv_parts = []
    for head in range(KVH):
        q_head = query[:, head * groups * DH : (head + 1) * groups * DH].reshape(rows, groups, DH)
        g_head = grad[:, head * groups * DH : (head + 1) * groups * DH].reshape(rows, groups, DH)
        k_head = everything[:, head * DH : (head + 1) * DH]
        v_head = everything[:, width + head * DH : width + (head + 1) * DH]
        scores = (
            jnp.einsum("tgd,ld->gtl", q_head, k_head, preferred_element_type=jnp.float32) * scale
        )
        scores = jnp.where(visible[None], scores, jnp.float32(-1e30))
        peak = jnp.max(scores, axis=-1, keepdims=True)
        weights = jnp.exp(scores - peak)
        weights = weights / jnp.sum(weights, axis=-1, keepdims=True)
        probs = weights.astype(jnp.bfloat16)
        output = jnp.einsum("gtl,ld->tgd", probs, v_head, preferred_element_type=jnp.float32)
        delta = jnp.sum(g_head.astype(jnp.float32) * output, axis=-1)
        dv_parts.append(
            jnp.einsum("gtl,tgd->ld", probs, g_head, preferred_element_type=jnp.float32)
        )
        prob_grad = jnp.einsum("tgd,ld->gtl", g_head, v_head, preferred_element_type=jnp.float32)
        score_grad = (weights * (prob_grad - delta.T[:, :, None]) * scale).astype(jnp.bfloat16)
        dq_parts.append(
            jnp.einsum(
                "gtl,ld->tgd", score_grad, k_head, preferred_element_type=jnp.float32
            ).reshape(rows, groups * DH)
        )
        dk_parts.append(
            jnp.einsum("gtl,tgd->ld", score_grad, q_head, preferred_element_type=jnp.float32)
        )
    dq = jnp.concatenate(dq_parts, axis=1).astype(jnp.bfloat16)
    dkv = jnp.concatenate(dk_parts + dv_parts, axis=1)
    return (dq, dkv[roots:].astype(jnp.bfloat16), dkv[:roots])


def local(query, grad_out, branch_kv, root_kv, lengths, segments):
    root_keys = lax.all_gather(root_kv, "dev", axis=0, tiled=True)
    half = lax.axis_size("dev") // 2
    live_count = jnp.sum((lengths > 0).astype(jnp.int32))
    arrived = passed_along(
        (query[1], grad_out[1], branch_kv[1], lengths[1:], segments[1:]), "dev", half
    )
    resident = live_count > 0
    q_tile = jnp.where(resident, query[0], arrived[0])
    g_tile = jnp.where(resident, grad_out[0], arrived[1])
    b_tile = jnp.where(resident, branch_kv[0], arrived[2])
    length = jnp.where(resident, lengths[0], arrived[3][0])
    segment = jnp.where(resident, segments[0], arrived[4][0])
    dq, dbranch, total = tile_grads(q_tile, g_tile, b_tile, length, segment, root_keys)
    returned = passed_along((dq, dbranch), "dev", half)
    second = live_count > 1
    query_grad = jnp.stack(
        [
            jnp.where(resident, dq, jnp.zeros_like(dq)),
            jnp.where(second, returned[0], jnp.zeros_like(dq)),
        ]
    )
    branch_grad = jnp.stack(
        [
            jnp.where(resident, dbranch, jnp.zeros_like(dbranch)),
            jnp.where(second, returned[1], jnp.zeros_like(dbranch)),
        ]
    )
    within = lax.psum_scatter(total, "dev", scatter_dimension=0, tiled=True)
    root_grad = lax.psum(within, "grp")
    return (query_grad, branch_grad, root_grad)


def solution(mesh):
    placed = (
        P(("grp", "dev"), None, None),
        P(("grp", "dev"), None, None),
        P(("grp", "dev"), None, None),
        P("dev", None),
        P(("grp", "dev")),
        P(("grp", "dev")),
    )
    return jax.shard_map(
        local,
        mesh=mesh,
        in_specs=placed,
        out_specs=(P(("grp", "dev"), None, None), P(("grp", "dev"), None, None), P("dev", None)),
        check_vma=False,
    )
```

profile of v0, /device:TPU:0, one launch (start us, length us, event | category | flops | bytes accessed | tf_op | source)
XLA Modules:
  0.0 334.5 jit_solution(13698584150056525036)
XLA Ops:
  7.9 1.7 slice_bitcast_fusion
  9.6 4.1 %collective-permute-start = (bf16[128,1024]{1,0:T(8,128)(2,1)}, bf16[128,1024]{1,0:T(8,128)(2,1)}, u32[]{:S(2)}, u32[]{:S(2)}) collective-permute-start(bf16[128,1024]{1,0:T(8,128)(2,1)} %slice_bitcast_fusion), channel_id=1, source_target_pairs={{8,0},{9,1},{10,2},{11,3},{12,4},{13,5},{14,6},{15,7},{0,8},{1,9},... | collective-permute-start | bytes 786440 | tf_op jit(solution)/shard_map/ppermute | solution.py:15
  13.7 1.7 fusion.106
  15.4 1.3 copy.165
  17.3 2.9 collective-permute-start.3
  20.9 1.7 fusion.105
  22.6 1.3 copy.163
  23.9 2.9 collective-permute-start.2
  29.5 69.0 %collective-permute-done.1 = s32[1]{0:T(128)} collective-permute-done((s32[1]{0:T(128)}, s32[1]{0:T(128)}, u32[]{:S(2)}, u32[]{:S(2)}) %collective-permute-start.1) | collective-permute-done | bytes 36 | tf_op jit(solution)/shard_map/ppermute | solution.py:15
  99.8 1.2 fusion.45
  102.4 1.0 bitcast_select_fusion.10
  103.5 0.9 fusion.108
  104.4 15.7 %collective-permute-done.2 = bf16[128,4096]{0,1:T(8,128)(2,1)} collective-permute-done((bf16[128,4096]{0,1:T(8,128)(2,1)}, bf16[128,4096]{0,1:T(8,128)(2,1)}, u32[]{:S(2)}, u32[]{:S(2)}) %collective-permute-start.2) | collective-permute-done | bytes 1048608 | tf_op jit(solution)/shard_map/ppermute | solution.py:15
  120.2 0.9 fusion.107
  121.1 22.5 %all-gather.2.cloned.1.call-done = bf16[1024,1024]{1,0:T(8,128)(2,1)} async-done(((bf16[64,1024]{1,0:T(8,128)(2,1)}), bf16[1024,1024]{1,0:T(8,128)(2,1)}) %all-gather.2.cloned.1.call-update) | async-done | bytes 2097168 | tf_op jit(solution)/shard_map/all_gather | solution.py:70
  143.6 2.2 fusion.47
  145.9 3.8 %exponential_reduce_fusion.3 = (f32[8,128]{1,0:T(8,128)S(1)}, f32[8,128,1152]{1,2,0:T(8,128)}) fusion(pred[128,1152]{0,1:T(8,128)(4,1)S(1)} %fusion.45, bf16[128,8,128]{0,2,1:T(8,128)(2,1)S(1)} %bitcast.304, bf16[1152,128]{1,0:T(8,128)(2,1)S(1)} %get-tuple-element.8), kind=kOutput, calls=%fused_computation.50 | convolution fusion | flops 306709632 | bytes 5427200 | tf_op jit(solution)/shard_map/sub | solution.py:46
  149.7 3.1 fusion.40
  154.2 1.8 copy-done.16
  156.0 1.3 fusion.19
  157.3 1.7 fusion.31
  159.0 4.4 %exponential_reduce_fusion = (f32[8,128]{1,0:T(8,128)}, f32[8,128,1152]{1,2,0:T(8,128)}) fusion(pred[128,1152]{0,1:T(8,128)(4,1)S(1)} %fusion.45, bf16[128,8,128]{0,2,1:T(8,128)(2,1)S(1)} %bitcast.298, bf16[1152,128]{1,0:T(8,128)(2,1)S(1)} %get-tuple-element.12), kind=kOutput, calls=%fused_computation.44 | convolution fusion | flops 306709632 | bytes 5427200 | tf_op jit(solution)/shard_map/sub | solution.py:46
  163.4 3.1 fusion.43
  166.5 1.5 multiply_reduce_fusion
  168.1 2.7 fusion.10
  170.9 5.5 %exponential_reduce_fusion.1 = (f32[8,128]{1,0:T(8,128)}, f32[8,128,1152]{1,2,0:T(8,128)}) fusion(pred[128,1152]{0,1:T(8,128)(4,1)S(1)} %fusion.45, bf16[128,8,128]{0,2,1:T(8,128)(2,1)} %bitcast.300, bf16[1152,128]{1,0:T(8,128)(2,1)} %get-tuple-element.10), kind=kOutput, calls=%fused_computation.46 | convolution fusion | flops 306709632 | bytes 5427200 | tf_op jit(solution)/shard_map/sub | solution.py:46
  176.3 4.4 %fusion.42 = bf16[8,128,1152]{1,2,0:T(8,128)(2,1)} fusion(f32[8,128]{1,0:T(8,128)} %get-tuple-element.31, f32[8,128,1152]{1,2,0:T(8,128)} %get-tuple-element.32), kind=kLoop, calls=%fused_computation.78 | loop fusion | flops 2359296 | bytes 7081984 | tf_op jit(solution)/shard_map/convert_element_type | solution.py:48
  180.7 5.7 %exponential_reduce_fusion.2 = (f32[8,128]{1,0:T(8,128)}, f32[8,128,1152]{1,2,0:T(8,128)}) fusion(pred[128,1152]{0,1:T(8,128)(4,1)S(1)} %fusion.45, bf16[128,8,128]{0,2,1:T(8,128)(2,1)} %bitcast.302, bf16[1152,128]{1,0:T(8,128)(2,1)} %get-tuple-element.9), kind=kOutput, calls=%fused_computation.48 | convolution fusion | flops 306709632 | bytes 5427200 | tf_op jit(solution)/shard_map/sub | solution.py:46
  186.4 3.1 fusion.41
  190.8 1.3 fusion.16
  192.2 1.2 slice-done.1
  194.9 1.1 copy-done.2
  196.7 1.3 fusion.13
  198.0 1.4 copy-done.11
  200.3 0.9 copy-done.7
  201.9 0.9 copy-done.1
  206.1 2.1 copy-done.12
  208.2 2.3 slice.136
  212.8 2.4 convolution_convert_fusion.1
  217.2 1.1 select_bitcast_fusion.2
  218.3 2.4 collective-permute-start.6
  220.9 80.7 %collective-permute-done.6 = bf16[128,1024]{1,0:T(8,128)(2,1)S(1)} collective-permute-done((bf16[128,1024]{1,0:T(8,128)(2,1)S(1)}, bf16[128,1024]{1,0:T(8,128)(2,1)S(1)}, u32[]{:S(2)}, u32[]{:S(2)}) %collective-permute-start.6) | collective-permute-done | bytes 262176 | tf_op jit(solution)/shard_map/ppermute | solution.py:15
  301.6 0.8 pad_maximum_fusion.2
  302.4 1.0 select_bitcast_fusion
  303.5 1.4 pad_maximum_fusion
  304.9 2.7 copy.105
  307.6 18.6 %all-reduce.2.cloned.1.call-done = f32[64,1024]{1,0:T(8,128)} async-done(((f32[64,1024]{1,0:T(8,128)}), f32[64,1024]{1,0:T(8,128)}) %all-reduce.2.cloned.1.call-update) | async-done | bytes 262160 | tf_op jit(solution)/shard_map/psum | solution.py:98
  326.3 1.7 copy.174
  (113 shorter events, 17.4 us)
Async XLA Ops:
  7.2 136.5 %all-gather.2.cloned.1.call-start = ((), (), s32[]{:S(2)}) async-start(), calls=%async_computation.1 | async-start | bytes 2228224 | tf_op jit(solution)/shard_map/all_gather | solution.py:70
  7.9 295.6 %reduce-scatter.2.cloned.1.call-start = ((), (), s32[]{:S(2)}) async-start(), calls=%async_computation.2 | async-start | bytes 4456448 | tf_op jit(solution)/shard_map/reduce_scatter | solution.py:97
  9.6 7.1 %copy-start.34 = (s32[2]{0:T(128)S(1)}, s32[2]{0:T(128)}, u32[]{:S(2)}) copy-start(s32[2]{0:T(128)} %param.10) | copy-start | bytes 28
  9.6 10.6 %copy-start.33 = (s32[2]{0:T(128)S(1)}, s32[2]{0:T(128)}, u32[]{:S(2)}) copy-start(s32[2]{0:T(128)} %param.11) | copy-start | bytes 28
  9.6 92.8 %collective-permute-start = (bf16[128,1024]{1,0:T(8,128)(2,1)}, bf16[128,1024]{1,0:T(8,128)(2,1)}, u32[]{:S(2)}, u32[]{:S(2)}) collective-permute-start(bf16[128,1024]{1,0:T(8,128)(2,1)} %slice_bitcast_fusion), channel_id=1, source_target_pairs={{8,0},{9,1},{10,2},{11,3},{12,4},{13,5},{14,6},{15,7},{0,8},{1,9},... | collective-permute-start | bytes 786440 | tf_op jit(solution)/shard_map/ppermute | solution.py:15
  16.7 86.7 %collective-permute-start.4 = (bf16[128,4096]{0,1:T(8,128)(2,1)}, bf16[128,4096]{0,1:T(8,128)(2,1)}, u32[]{:S(2)}, u32[]{:S(2)}) collective-permute-start(bf16[128,4096]{0,1:T(8,128)(2,1)} %bitcast.14), channel_id=1, source_target_pairs={{8,0},{9,1},{10,2},{11,3},{12,4},{13,5},{14,6},{15,7},{0,8},{1,9},... | collective-permute-start | bytes 3145736 | tf_op jit(solution)/shard_map/ppermute | solution.py:15
  17.3 83.8 %collective-permute-start.3 = (s32[1]{0:T(128)}, s32[1]{0:T(128)}, u32[]{:S(2)}, u32[]{:S(2)}) collective-permute-start(s32[1]{0:T(128)} %get-tuple-element.27), channel_id=1, source_target_pairs={{8,0},{9,1},{10,2},{11,3},{12,4},{13,5},{14,6},{15,7},{0,8},{1,9},... | collective-permute-start | bytes 20 | tf_op jit(solution)/shard_map/ppermute | solution.py:15
  20.8 77.6 %collective-permute-start.1 = (s32[1]{0:T(128)}, s32[1]{0:T(128)}, u32[]{:S(2)}, u32[]{:S(2)}) collective-permute-start(s32[1]{0:T(128)} %get-tuple-element.25), channel_id=1, source_target_pairs={{8,0},{9,1},{10,2},{11,3},{12,4},{13,5},{14,6},{15,7},{0,8},{1,9},... | collective-permute-start | bytes 20 | tf_op jit(solution)/shard_map/ppermute | solution.py:15
  23.9 96.2 %collective-permute-start.2 = (bf16[128,4096]{0,1:T(8,128)(2,1)}, bf16[128,4096]{0,1:T(8,128)(2,1)}, u32[]{:S(2)}, u32[]{:S(2)}) collective-permute-start(bf16[128,4096]{0,1:T(8,128)(2,1)} %bitcast.295), channel_id=1, source_target_pairs={{8,0},{9,1},{10,2},{11,3},{12,4},{13,5},{14,6},{15,7},{0,8},{1,9},... | collective-permute-start | bytes 3145736 | tf_op jit(solution)/shard_map/ppermute | solution.py:15
  103.5 16.7 %copy-start.13 = (bf16[128,4096]{0,1:T(8,128)(2,1)}, bf16[128,4096]{0,1:T(8,128)(2,1)S(1)}, u32[]{:S(2)}) copy-start(bf16[128,4096]{0,1:T(8,128)(2,1)S(1)} %fusion.44) | copy-start | bytes 3145732
  121.1 37.9 %copy-start.26 = (bf16[128,1024]{0,1:T(8,128)(2,1)}, bf16[128,1024]{0,1:T(8,128)(2,1)S(1)}, u32[]{:S(2)}) copy-start(bf16[128,1024]{0,1:T(8,128)(2,1)S(1)} %get-tuple-element.18) | copy-start | bytes 786436
  145.9 3.8 %copy-start.17 = (bf16[1152,128]{1,0:T(8,128)(2,1)}, bf16[1152,128]{1,0:T(8,128)(2,1)S(1)}, u32[]{:S(2)}) copy-start(bf16[1152,128]{1,0:T(8,128)(2,1)S(1)} %get-tuple-element.8) | copy-start | bytes 884740
  145.9 13.1 %copy-start.21 = (bf16[1152,128]{1,0:T(8,128)(2,1)}, bf16[1152,128]{1,0:T(8,128)(2,1)S(1)}, u32[]{:S(2)}) copy-start(bf16[1152,128]{1,0:T(8,128)(2,1)S(1)} %get-tuple-element.12) | copy-start | bytes 884740
  149.7 3.1 copy-start.3
  152.8 1.4 copy-start
  152.8 3.2 copy-start.16
  157.3 1.7 copy-start.5
  163.4 3.1 copy-start.23
  163.4 4.7 %copy-start.14 = (f32[8,128,1152]{1,2,0:T(8,128)S(1)}, f32[8,128,1152]{1,2,0:T(8,128)}, u32[]{:S(2)}) copy-start(f32[8,128,1152]{1,2,0:T(8,128)} %get-tuple-element.30) | copy-start | bytes 14155780
  166.5 1.6 copy-start.24
  166.5 1.6 copy-start.31
  186.4 3.1 copy-start.4
  186.4 4.4 %copy-start.15 = (f32[8,128,1152]{1,2,0:T(8,128)S(1)}, f32[8,128,1152]{1,2,0:T(8,128)}, u32[]{:S(2)}) copy-start(f32[8,128,1152]{1,2,0:T(8,128)} %get-tuple-element.34) | copy-start | bytes 14155780
  186.4 4.4 %copy-start.32 = (f32[8,128]{1,0:T(8,128)S(1)}, f32[8,128]{1,0:T(8,128)}, u32[]{:S(2)}) copy-start(f32[8,128]{1,0:T(8,128)} %get-tuple-element.33) | copy-start | bytes 12292
  189.5 2.7 slice-start
  189.6 7.1 %slice-start.2 = ((s8[4718592]{0:T(1024)(128)(4,1)}), s8[4194304]{0:T(1024)(128)(4,1)S(1)}, s32[]{:S(2)}) async-start(s8[4718592]{0:T(1024)(128)(4,1)} %bitcast.276), calls=%async_computation.6 | async-start | bytes 8388608
  190.8 2.7 slice-start.1
  190.8 2.7 copy-start.29
  190.8 5.8 %slice-start.3 = ((s8[4718592]{0:T(1024)(128)(4,1)}), s8[524288]{0:T(1024)(128)(4,1)S(1)}, s32[]{:S(2)}) async-start(s8[4718592]{0:T(1024)(128)(4,1)} %bitcast.276), calls=%async_computation.7 | async-start | bytes 1048576
  193.5 1.4 copy-start.9
  193.5 2.5 copy-start.2
  196.7 2.8 copy-start.28
  198.0 1.4 copy-start.11
  199.5 1.7 copy-start.7
  199.5 1.7 copy-start.27
  201.1 1.7 copy-start.1
  204.4 1.0 copy-start.25
  206.1 2.1 copy-start.12
  210.5 1.7 copy-start.8
  210.5 1.7 copy-start.22
  210.6 2.2 copy-start.20
  210.6 115.7 %all-reduce.2.cloned.1.call-start = ((), (), s32[]{:S(2)}) async-start(), calls=%async_computation.3 | async-start | bytes 524288 | tf_op jit(solution)/shard_map/psum | solution.py:98
  212.2 3.0 copy-start.10
  212.2 3.0 copy-start.19
  212.8 3.1 copy-start.6
  212.8 3.1 copy-start.18
  216.5 85.9 %collective-permute-start.5 = (bf16[128,4096]{0,1:T(8,128)(2,1)S(1)}, bf16[128,4096]{0,1:T(8,128)(2,1)S(1)}, u32[]{:S(2)}, u32[]{:S(2)}) collective-permute-start(bf16[128,4096]{0,1:T(8,128)(2,1)S(1)} %pad_maximum_fusion.1), channel_id=1, source_target_pairs={{8,0},{9,1},{10,2},{11,3},{12,4},{13,5},{14,6},{15,7},{0,8},{1,9},... | collective-permute-start | bytes 3145736 | tf_op jit(solution)/shard_map/ppermute | solution.py:15
  218.3 83.3 %collective-permute-start.6 = (bf16[128,1024]{1,0:T(8,128)(2,1)S(1)}, bf16[128,1024]{1,0:T(8,128)(2,1)S(1)}, u32[]{:S(2)}, u32[]{:S(2)}) collective-permute-start(bf16[128,1024]{1,0:T(8,128)(2,1)S(1)} %get-tuple-element.7), channel_id=1, source_target_pairs={{8,0},{9,1},{10,2},{11,3},{12,4},{13,5},{14,6},{15,7},{0,8},{1,9},... | collective-permute-start | bytes 786440 | tf_op jit(solution)/shard_map/ppermute | solution.py:15
  (1 other events, 0.7 us)
Sparse Core Ops, SparseCore 0:
  10.1 133.4 all-gather.1
  210.7 85.1 reduce-scatter.1
  303.6 22.6 all-reduce.1
where the time goes:
time: 335 us; the launch traced here: 334 us
  waiting for transfers between devices  207 us (62%)
  matrix products  40.4 us (12%)
  local copies, waits for them, and re-layouts  31.2 us (9%)
  other arithmetic  23.9 us (7%)
  between operations  18.4 us (5%)
  starting transfers between devices  13.3 us (4%)
    ppermute x7, waiting for transfers between devices, passed_along(): return lax.ppermute(block, axis, route)  165 us
    all_gather x1, waiting for transfers between devices, local(): root_keys = lax.all_gather(root_kv, 'dev', axis=0, tiled=True)  22.5 us
    unnamed x84, local copies, waits for them, and re-layouts  20.9 us
    sub x4, matrix products, tile_grads(): weights = jnp.exp(scores - peak)  19.4 us
    psum x1, waiting for transfers between devices, local(): root_grad = lax.psum(within, 'grp')  18.6 us
    convert_element_type x4, other arithmetic, tile_grads(): probs = weights.astype(jnp.bfloat16)  13.7 us
    ppermute x7, starting transfers between devices, passed_along(): return lax.ppermute(block, axis, route)  12.9 us
    dot_general x4, matrix products, tile_grads(): jnp.einsum('tgd,ld->gtl', g_head, v_head, preferred_element_type=jnp.floa...  6.71 us
  transfers between devices with their start and end apart: 10, of which 5 were waited for; matrix products, arithmetic and copies ran while one was open for 8% of the time, Pallas kernels for 0%

commit v1 on v0

v1 whole, which is shorter than its diff:
```python
import functools
import math

import jax
import jax.numpy as jnp
from jax import lax
from jax.experimental import pallas as pl
from jax.experimental.pallas import tpu as pltpu
from jax.sharding import PartitionSpec as P

H = 32
KVH = 4
DH = 128
SEGS = 4
GROUPS = H // KVH
CORES = 2
HEADS = KVH // CORES
CHUNK = 32
NT = (((1,), (1,)), ((), ()))
NN = (((1,), (0,)), ((), ()))
F32 = jnp.float32
BF16 = jnp.bfloat16


def swapped(block, axis, bit):
    route = [(i ^ bit, i) for i in range(lax.axis_size(axis))]
    return lax.ppermute(block, axis, route)


def dot(a, b, dims):
    return lax.dot_general(a, b, dims, preferred_element_type=F32)


def head_kernel(
    offsets,
    tiles,
    info,
    q_own,
    q_far,
    g_own,
    g_far,
    bk_own,
    bk_far,
    bv_own,
    bv_far,
    kv_near,
    kv_next,
    dq_own,
    dq_far,
    db_own,
    db_far,
    keep,
    send,
    keys,
    values,
    keys_t,
    bkeys,
    bvalues,
    bkeys_t,
    s_scr,
    dp_scr,
    dk_acc,
    dv_acc,
    dbk_acc,
    dbv_acc,
    dq_scr,
):
    t = pl.program_id(0)
    me = info[1]
    rr = kv_near.shape[2]
    rows = q_own.shape[1]
    roots = keys.shape[0]
    width = roots // SEGS
    qrows = GROUPS * CHUNK
    scale = DH ** (-0.5)
    sharp = scale * math.log2(math.e)

    def places():
        for side, bit in ((0, 0), (1, 2)):
            for j, off in enumerate(offsets):
                for b0 in range(CORES):
                    rel = b0 + bit + off
                    yield side, j, b0, pl.multiple_of((me ^ rel) * rr, rr)

    @pl.when(t == 0)
    def _():
        for side, j, b0, at in places():
            block = (kv_near, kv_next)[side][j, b0]
            keys[pl.ds(at, rr), :] = block[:, :DH]
            values[pl.ds(at, rr), :] = block[:, DH:]
        dk_acc[...] = jnp.zeros_like(dk_acc)
        dv_acc[...] = jnp.zeros_like(dv_acc)
        for b in range(0, roots, DH):
            keys_t[:, b : b + DH] = keys[b : b + DH, :].T

    own = t < tiles
    length = info[2 + t]
    segment = info[2 + 2 * tiles + t]

    bkeys[...] = jnp.where(own, bk_own[0], bk_far[0])
    bvalues[...] = jnp.where(own, bv_own[0], bv_far[0])
    bkeys_t[...] = bkeys[...].T
    dbk_acc[...] = jnp.zeros_like(dbk_acc)
    dbv_acc[...] = jnp.zeros_like(dbv_acc)
    dq_scr[...] = jnp.zeros_like(dq_scr)

    def fold(x, op):
        return op(x.reshape(x.shape[0] // 8, 8, x.shape[1]), axis=0)

    def chunk(c, segs):
        r0 = pl.multiple_of(c * CHUNK, CHUNK)

        def taken(near, far):
            x = jnp.where(own, near[0, pl.ds(r0, CHUNK), :], far[0, pl.ds(r0, CHUNK), :])
            return x

        def stacked(x):
            return jnp.concatenate([x[:, j * DH : (j + 1) * DH] for j in range(GROUPS)], axis=0)

        q = stacked(taken(q_own, q_far))
        g = stacked(taken(g_own, g_far))
        row = lax.broadcasted_iota(jnp.int32, (qrows, DH), 0) % CHUNK + r0
        g = jnp.where(row < length, g.astype(F32), 0.0).astype(BF16)

        spans = [(b * width, width) for b in range(segs)] + [(roots, rows)]

        def k_of(b):
            return keys[spans[b][0] : spans[b][0] + width, :] if b < segs else bkeys[...]

        def v_of(b):
            return values[spans[b][0] : spans[b][0] + width, :] if b < segs else bvalues[...]

        def kt_of(b):
            return keys_t[:, spans[b][0] : spans[b][0] + width] if b < segs else bkeys_t[...]

        top = None
        for b in range(segs + 1):
            s = dot(k_of(b), q, NT)
            if b == segs:
                key = lax.broadcasted_iota(jnp.int32, s.shape, 0)
                pos = lax.broadcasted_iota(jnp.int32, s.shape, 1) % CHUNK + r0
                s = jnp.where(key <= pos, s, F32(-1e30))
            s_scr[spans[b][0] : spans[b][0] + spans[b][1], :] = s
            part = fold(s, jnp.max)
            top = part if top is None else jnp.maximum(top, part)
        peak = jnp.max(top, axis=0, keepdims=True)

        total = jnp.zeros((8, qrows), F32)
        for b in range(segs + 1):
            at = slice(spans[b][0], spans[b][0] + spans[b][1])
            dp_scr[at, :] = dot(v_of(b), g, NT)
            e = jnp.exp2((s_scr[at, :] - peak) * sharp)
            s_scr[at, :] = e
            total = total + fold(e, jnp.sum)
        inv = 1.0 / jnp.sum(total, axis=0, keepdims=True)

        delta = jnp.zeros((8, qrows), F32)
        for b in range(segs + 1):
            at = slice(spans[b][0], spans[b][0] + spans[b][1])
            probs = (s_scr[at, :] * inv).astype(BF16)
            delta = delta + fold(probs.astype(F32) * dp_scr[at, :], jnp.sum)
            dv = dot(probs, g, NN)
            if b < segs:
                dv_acc[at, :] += dv
            else:
                dbv_acc[...] += dv
        delta = jnp.sum(delta, axis=0, keepdims=True)
        invs = inv * scale

        dq_t = jnp.zeros((DH, qrows), F32)
        for b in range(segs + 1):
            at = slice(spans[b][0], spans[b][0] + spans[b][1])
            ds = ((s_scr[at, :] * invs) * (dp_scr[at, :] - delta)).astype(BF16)
            dk = dot(ds, q, NN)
            if b < segs:
                dk_acc[at, :] += dk
            else:
                dbk_acc[...] += dk
            dq_t = dq_t + dot(kt_of(b), ds, NN)
        dq = dq_t.T.astype(BF16)
        for j in range(GROUPS):
            dq_scr[pl.ds(r0, CHUNK), j * DH : (j + 1) * DH] = dq[j * CHUNK : (j + 1) * CHUNK, :]

    count = (length + (CHUNK - 1)) // CHUNK
    for s in range(SEGS):

        @pl.when(segment == s)
        def _():
            def step(c, carry):
                chunk(c, s + 1)
                return carry

            lax.fori_loop(0, count, step, 0)

    for mine, dq_ref, db_ref in ((own, dq_own, db_own), (jnp.logical_not(own), dq_far, db_far)):

        @pl.when(mine)
        def _():
            dq_ref[0] = dq_scr[...]
            db_ref[0, :, :DH] = dbk_acc[...].astype(BF16)
            db_ref[0, :, DH:] = dbv_acc[...].astype(BF16)

    @pl.when(t == 2 * tiles - 1)
    def _():
        for side, j, b0, at in places():
            out = (keep, send)[side]
            out[j, b0, :, :DH] = dk_acc[pl.ds(at, rr), :].astype(out.dtype)
            out[j, b0, :, DH:] = dv_acc[pl.ds(at, rr), :].astype(out.dtype)


def head_grads(head, offsets, info, q, q_far, g, g_far, b, b_far, near, nxt):
    tiles, rows, _ = q.shape
    half = near.shape[0]
    rr = near.shape[2]
    roots = 2 * half * CORES * rr
    qw = GROUPS * DH
    qrows = GROUPS * CHUNK

    def low(t):
        return jnp.minimum(t, tiles - 1)

    def high(t):
        return jnp.maximum(t - tiles, 0)

    def col(info):
        return info[0] * HEADS + head

    whole = pl.BlockSpec(near.shape, lambda t, info: (0, 0, 0, 0))
    q_near_spec = pl.BlockSpec((1, rows, qw), lambda t, info: (low(t), 0, col(info)))
    q_far_spec = pl.BlockSpec((1, rows, qw), lambda t, info: (high(t), 0, head))
    in_specs = [
        q_near_spec,
        q_far_spec,
        q_near_spec,
        q_far_spec,
        pl.BlockSpec((1, rows, DH), lambda t, info: (low(t), 0, col(info))),
        pl.BlockSpec((1, rows, DH), lambda t, info: (high(t), 0, head)),
        pl.BlockSpec((1, rows, DH), lambda t, info: (low(t), 0, KVH + col(info))),
        pl.BlockSpec((1, rows, DH), lambda t, info: (high(t), 0, HEADS + head)),
        whole,
        whole,
    ]
    out_specs = [
        pl.BlockSpec((1, rows, qw), lambda t, info: (low(t), 0, 0)),
        pl.BlockSpec((1, rows, qw), lambda t, info: (high(t), 0, 0)),
        pl.BlockSpec((1, rows, 2 * DH), lambda t, info: (low(t), 0, 0)),
        pl.BlockSpec((1, rows, 2 * DH), lambda t, info: (high(t), 0, 0)),
        whole,
        whole,
    ]
    out_shape = [
        jax.ShapeDtypeStruct((tiles, rows, qw), BF16),
        jax.ShapeDtypeStruct((tiles, rows, qw), BF16),
        jax.ShapeDtypeStruct((tiles, rows, 2 * DH), BF16),
        jax.ShapeDtypeStruct((tiles, rows, 2 * DH), BF16),
        jax.ShapeDtypeStruct(near.shape, F32),
        jax.ShapeDtypeStruct(near.shape, BF16),
    ]
    span = roots + rows
    scratch = [
        pltpu.VMEM((roots, DH), BF16),
        pltpu.VMEM((roots, DH), BF16),
        pltpu.VMEM((DH, roots), BF16),
        pltpu.VMEM((rows, DH), BF16),
        pltpu.VMEM((rows, DH), BF16),
        pltpu.VMEM((DH, rows), BF16),
        pltpu.VMEM((span, qrows), F32),
        pltpu.VMEM((span, qrows), F32),
        pltpu.VMEM((roots, DH), F32),
        pltpu.VMEM((roots, DH), F32),
        pltpu.VMEM((rows, DH), F32),
        pltpu.VMEM((rows, DH), F32),
        pltpu.VMEM((rows, qw), BF16),
    ]
    flops = 2 * 5 * tiles * rows * GROUPS * span * DH
    return pl.pallas_call(
        functools.partial(head_kernel, offsets, tiles),
        grid_spec=pltpu.PrefetchScalarGridSpec(
            num_scalar_prefetch=1,
            grid=(2 * tiles,),
            in_specs=in_specs,
            out_specs=out_specs,
            scratch_shapes=scratch,
        ),
        out_shape=out_shape,
        cost_estimate=pl.CostEstimate(
            flops=flops, bytes_accessed=8 * tiles * rows * qw, transcendentals=0
        ),
        compiler_params=pltpu.CompilerParams(dimension_semantics=("arbitrary",)),
        name=f"grads_{head}",
    )(info, q, q_far, g, g_far, b, b_far, b, b_far, near, nxt)


def local(query, grad_out, branch_kv, root_kv, lengths, segments):
    n_dev = lax.axis_size("dev")
    n_grp = lax.axis_size("grp")
    me = lax.axis_index("dev")
    core = me % CORES
    tiles, rows, _ = query.shape
    rr = root_kv.shape[0]
    bits = []
    while (4 << len(bits)) < n_dev:
        bits.append(4 << len(bits))

    def halves(x, parts):
        x = x.reshape(x.shape[:-1] + (parts, CORES, x.shape[-1] // (parts * CORES)))
        axis = x.ndim - 2
        mine = lax.dynamic_index_in_dim(x, core, axis, keepdims=False)
        other = lax.dynamic_index_in_dim(x, 1 - core, axis, keepdims=False)
        flat = x.shape[:-3] + (-1,)
        return mine.reshape(flat), other.reshape(flat)

    mine, other = halves(root_kv, 2)
    block = jnp.stack([mine, swapped(other, "dev", 1)])
    block = block.reshape(1, CORES, rr, 2, HEADS, DH)
    gathered = []
    for head in range(HEADS):
        x = block[:, :, :, :, head, :].reshape(1, CORES, rr, 2 * DH)
        for bit in reversed(bits):
            x = jnp.concatenate([x, swapped(x, "dev", bit)], axis=0)
        gathered.append((x, swapped(x, "dev", 2)))
    offsets = [0]
    for bit in reversed(bits):
        offsets = offsets + [off + bit for off in offsets]

    q_far = swapped(halves(query, 1)[1], "dev", 1)
    g_far = swapped(halves(grad_out, 1)[1], "dev", 1)
    b_far = swapped(halves(branch_kv, 2)[1], "dev", 1)
    meta = jnp.concatenate([lengths, segments]).reshape(2, tiles)
    meta_far = swapped(meta, "dev", 1)
    info = jnp.concatenate(
        [jnp.stack([core, me]), jnp.concatenate([meta, meta_far], axis=1).reshape(-1)]
    )

    q_parts, b_parts, root_parts = [], [], []
    for head in range(HEADS):
        near, nxt = gathered[head]
        dq_own, dq_far, db_own, db_far, keep, send = head_grads(
            head, tuple(offsets), info, query, q_far, grad_out, g_far, branch_kv, b_far, near, nxt
        )
        x = keep + swapped(send, "dev", 2)
        for bit in bits:
            half = x.shape[0] // 2
            x = x[:half] + swapped(x[half:].astype(BF16), "dev", bit)
        x = x[0]
        hop = 1
        while hop < n_grp:
            x = x.astype(BF16)
            x = x.astype(F32) + swapped(x, "grp", hop).astype(F32)
            hop *= 2
        root_parts.append((x[0], swapped(x[1], "dev", 1)))
        q_parts.append((dq_own, swapped(dq_far, "dev", 1)))
        b_parts.append((db_own, swapped(db_far, "dev", 1)))

    def joined(parts, kinds):
        def laid(side):
            x = jnp.stack([p[side].reshape(p[side].shape[:-1] + (kinds, -1)) for p in parts], -2)
            return x.reshape(x.shape[:-2] + (-1,))

        near, far = laid(0), laid(1)
        first = jnp.where(core == 0, near, far)
        second = jnp.where(core == 0, far, near)
        x = jnp.stack([first, second], axis=-2)
        return x.reshape(x.shape[:-3] + (-1,))

    return (joined(q_parts, 1), joined(b_parts, 2), joined(root_parts, 2))


def solution(mesh):
    placed = (
        P(("grp", "dev"), None, None),
        P(("grp", "dev"), None, None),
        P(("grp", "dev"), None, None),
        P("dev", None),
        P(("grp", "dev")),
        P(("grp", "dev")),
    )
    return jax.shard_map(
        local,
        mesh=mesh,
        in_specs=placed,
        out_specs=(P(("grp", "dev"), None, None), P(("grp", "dev"), None, None), P("dev", None)),
        check_vma=False,
    )
```

time: 335 us -> 116 us (0.35)
  waiting for transfers between devices: 207 us -> 18.5 us
  matrix products: 40.4 us -> 0 us
  starting transfers between devices: 13.3 us -> 51.3 us
  other arithmetic: 23.9 us -> 2.83 us
  between operations: 18.4 us -> 1.29 us
  Pallas kernels: 0 us -> 15.8 us
    ppermute x7 -> x25, waiting for transfers between devices: 165 us -> 18.5 us  [swapped(): return lax.ppermute(block, axis, route)]
    ppermute x7 -> x25, starting transfers between devices: 12.9 us -> 51.3 us  [swapped(): return lax.ppermute(block, axis, route)]
    all_gather x1 -> x0, waiting for transfers between devices: 22.5 us -> none  [local(): root_keys = lax.all_gather(root_kv, 'dev', axis=0, tiled=True)]
    dot_general x20 -> x0, matrix products: 21.1 us -> none  [the longest x4 6.71 us: tile_grads(): jnp.einsum('tgd,ld->gtl', g_head, v_head, preferred_element_type=jnp.floa...]
    sub x4 -> x0, matrix products: 19.4 us -> none  [tile_grads(): weights = jnp.exp(scores - peak)]
    psum x1 -> x0, waiting for transfers between devices: 18.6 us -> none  [local(): root_grad = lax.psum(within, 'grp')]
    pallas_call x0 -> x2, Pallas kernels: none -> 15.8 us  [head_grads(): pl.pallas_call(functools.partial(head_kernel, offsets, tiles), grid_spec=...]
    unnamed x84 -> x38, local copies, waits for them, and re-layouts: 20.9 us -> 6.57 us
  transfers between devices with their start and end apart: 10 -> 25, of which waited for: 5 -> 7; matrix products, arithmetic and copies ran while one was open for 8% -> 22% of each run, Pallas kernels for 0% -> 13%
where the time goes in v1:
time: 116 us; the launch traced here: 118 us
  starting transfers between devices  51.3 us (44%)
  local copies, waits for them, and re-layouts  28.5 us (25%)
  waiting for transfers between devices  18.5 us (16%)
  Pallas kernels  15.8 us (14%)
  other arithmetic  2.83 us (2%)
  between operations  1.29 us (1%)
    ppermute x25, starting transfers between devices, swapped(): return lax.ppermute(block, axis, route)  51.3 us
    ppermute x25, waiting for transfers between devices, swapped(): return lax.ppermute(block, axis, route)  18.5 us
    pallas_call x2, Pallas kernels, head_grads(): pl.pallas_call(functools.partial(head_kernel, offsets, tiles), grid_spec=...  15.8 us
    reshape x4, local copies, waits for them, and re-layouts, halves(): x = x.reshape(x.shape[:-1] + (parts, CORES, x.shape[-1] // (parts * CORES)))  7.96 us
    dynamic_slice x4, local copies, waits for them, and re-layouts, halves(): other = lax.dynamic_index_in_dim(x, 1 - core, axis, keepdims=False)  7.01 us
    unnamed x38, local copies, waits for them, and re-layouts  6.57 us
  transfers between devices with their start and end apart: 25, of which 7 were waited for; matrix products, arithmetic and copies ran while one was open for 22% of the time, Pallas kernels for 13%

profile of v1, /device:TPU:0, one launch (start us, length us, event | category | flops | bytes accessed | tf_op | source)
XLA Modules:
  0.0 118.1 jit_solution(10034463688723191834)
XLA Ops:
  0.6 1.0 reshape.195
  1.6 0.9 dynamic-slice_reduce_fusion.1
  2.6 0.6 collective-permute-start.4
  3.1 3.3 %reshape.191 = bf16[2,128,1,2,2048]{4,3,1,0,2:T(2,128)(2,1)S(1)} reshape(bf16[2,128,4096]{2,1,0:T(8,128)(2,1)} %g_own.3) | data formatting | bytes 4194304 | tf_op jit(solution)/shard_map/reshape | solution.py:306
  6.4 2.2 %constant_dynamic-slice_fusion = bf16[2,128,1,1,2048]{4,3,1,0,2:T(2,128)(2,1)S(1)} fusion(bf16[2,128,1,2,2048]{4,3,1,0,2:T(2,128)(2,1)S(1)} %reshape.191, s32[]{:T(128)S(6)} %select_n.121), kind=kLoop, calls=%fused_computation.50 | loop fusion | bytes 2097156 | tf_op jit(solution)/shard_map/jit(dynamic_index_in_dim)/dynamic_slice | solution.py:309
  8.6 0.6 copy.71
  9.3 3.3 %reshape.189 = bf16[2,128,1,2,2048]{4,3,1,0,2:T(2,128)(2,1)S(1)} reshape(bf16[2,128,4096]{2,1,0:T(8,128)(2,1)} %q_own.3) | data formatting | bytes 4194304 | tf_op jit(solution)/shard_map/reshape | solution.py:306
  12.6 2.2 %constant_dynamic-slice_fusion.1 = bf16[2,128,1,1,2048]{4,3,1,0,2:T(2,128)(2,1)S(1)} fusion(bf16[2,128,1,2,2048]{4,3,1,0,2:T(2,128)(2,1)S(1)} %reshape.189, s32[]{:T(128)S(6)} %select_n.121), kind=kLoop, calls=%fused_computation.51 | loop fusion | bytes 2097156 | tf_op jit(solution)/shard_map/jit(dynamic_index_in_dim)/dynamic_slice | solution.py:309
  14.8 0.6 copy.72
  15.4 0.6 collective-permute-start.1
  16.0 0.4 reshape.193
  16.4 1.8 %dynamic-slice_reduce_fusion = bf16[2,128,2,256]{3,2,1,0:T(2,128)(2,1)S(1)} fusion(bf16[2,128,2,2,256]{4,3,2,1,0:T(2,128)(2,1)S(1)} %reshape.193, s32[]{:T(128)S(6)} %select_n.121), kind=kLoop, calls=%fused_computation.10 | loop fusion | bytes 524292 | tf_op jit(solution)/shard_map/jit(dynamic_index_in_dim)/dynamic_slice | solution.py:309
  18.3 0.4 collective-permute-start.3
  19.2 0.9 collective-permute-done
  20.2 0.6 pad_add_fusion.2.info
  20.8 0.9 stack.50
  21.8 0.8 slice_reduce_fusion.1
  22.6 3.8 %collective-permute-start.5 = (bf16[1,2,64,256]{3,2,1,0:T(8,128)(2,1)S(1)}, bf16[1,2,64,256]{3,2,1,0:T(8,128)(2,1)S(1)}, u32[]{:S(2)}, u32[]{:S(2)}) collective-permute-start(bf16[1,2,64,256]{3,2,1,0:T(8,128)(2,1)S(1)} %reshape_squeeze.6), channel_id=1, source_target_pairs={{8,0},{9,1},{10,2},{11,3},{12,4},{13,5},{14,6},{15,7},{0,8},{1,9},... | collective-permute-start | bytes 196616 | tf_op jit(solution)/shard_map/ppermute | solution.py:27
  26.6 4.1 %collective-permute-done.5 = bf16[1,2,64,256]{3,2,1,0:T(8,128)(2,1)S(1)} collective-permute-done((bf16[1,2,64,256]{3,2,1,0:T(8,128)(2,1)S(1)}, bf16[1,2,64,256]{3,2,1,0:T(8,128)(2,1)S(1)}, u32[]{:S(2)}, u32[]{:S(2)}) %collective-permute-start.5) | collective-permute-done | bytes 65568 | tf_op jit(solution)/shard_map/ppermute | solution.py:27
  30.7 2.0 %collective-permute-start.6 = (bf16[2,2,64,256]{3,2,1,0:T(8,128)(2,1)S(1)}, bf16[2,2,64,256]{3,2,1,0:T(8,128)(2,1)S(1)}, u32[]{:S(2)}, u32[]{:S(2)}) collective-permute-start(bf16[2,2,64,256]{3,2,1,0:T(8,128)(2,1)S(1)} %pad_maximum_fusion.7), channel_id=1, source_target_pairs={{4,0},{5,1},{6,2},{7,3},{0,4},{1,5},{2,6},{3,7},{12,8},{13,9},{14,... | collective-permute-start | bytes 393224 | tf_op jit(solution)/shard_map/ppermute | solution.py:27
  32.7 0.5 collective-permute-done.8
  33.3 0.8 collective-permute-start.9
  34.1 3.1 %collective-permute-done.6 = bf16[2,2,64,256]{3,2,1,0:T(8,128)(2,1)S(1)} collective-permute-done((bf16[2,2,64,256]{3,2,1,0:T(8,128)(2,1)S(1)}, bf16[2,2,64,256]{3,2,1,0:T(8,128)(2,1)S(1)}, u32[]{:S(2)}, u32[]{:S(2)}) %collective-permute-start.6) | collective-permute-done | bytes 131104 | tf_op jit(solution)/shard_map/ppermute | solution.py:27
  37.2 1.7 %collective-permute-start.7 = (bf16[4,2,64,256]{3,2,1,0:T(8,128)(2,1)S(1)}, bf16[4,2,64,256]{3,2,1,0:T(8,128)(2,1)S(1)}, u32[]{:S(2)}, u32[]{:S(2)}) collective-permute-start(bf16[4,2,64,256]{3,2,1,0:T(8,128)(2,1)S(1)} %constant_dynamic-update-slice_fusion.2.kv_near), channel_id=1, source_target_pairs={{2,0},{3,1},{0,2},{1,3},{6,4},{7,5},{4,6},{5,7},{10,8},{11,9},{8,1... | collective-permute-start | bytes 786440 | tf_op jit(solution)/shard_map/ppermute | solution.py:27
  39.2 1.6 %collective-permute-start.10 = (bf16[4,2,64,256]{3,2,1,0:T(8,128)(2,1)S(1)}, bf16[4,2,64,256]{3,2,1,0:T(8,128)(2,1)}, u32[]{:S(2)}, u32[]{:S(2)}) collective-permute-start(bf16[4,2,64,256]{3,2,1,0:T(8,128)(2,1)S(1)} %constant_dynamic-update-slice_fusion.5.kv_near), channel_id=1, source_target_pairs={{2,0},{3,1},{0,2},{1,3},{6,4},{7,5},{4,6},{5,7},{10,8},{11,9},{8,1... | collective-permute-start | bytes 786440 | tf_op jit(solution)/shard_map/ppermute | solution.py:27
  40.8 5.6 %collective-permute-done.7.kv_next = bf16[4,2,64,256]{3,2,1,0:T(8,128)(2,1)S(1)} collective-permute-done((bf16[4,2,64,256]{3,2,1,0:T(8,128)(2,1)S(1)}, bf16[4,2,64,256]{3,2,1,0:T(8,128)(2,1)S(1)}, u32[]{:S(2)}, u32[]{:S(2)}) %collective-permute-start.7) | collective-permute-done | bytes 262176 | tf_op jit(solution)/shard_map/ppermute | solution.py:27
  46.4 0.7 copy-done.11
  47.1 7.9 %grads_0.1 = (bf16[2,128,1024]{2,1,0:T(8,128)(2,1)}, bf16[2,128,1024]{2,1,0:T(8,128)(2,1)}, bf16[2,128,256]{2,1,0:T(8,128)(2,1)}, bf16[2,128,256]{2,1,0:T(8,128)...) custom-call(s32[10]{0:T(128)} %pad_add_fusion.2.info, bf16[2,128,4096]{2,1,0:T(8,128)(2,1)} %q_own.3, ...), custom_call_target="tpu_custom_call" | custom-call | flops 3019898880 | bytes 2097152 | tf_op jit(solution)/shard_map/grads_0/pallas_call | solution.py:276
  55.2 7.8 %grads_1.1 = (bf16[2,128,1024]{2,1,0:T(8,128)(2,1)}, bf16[2,128,1024]{2,1,0:T(8,128)(2,1)}, bf16[2,128,256]{2,1,0:T(8,128)(2,1)}, bf16[2,128,256]{2,1,0:T(8,128)...) custom-call(s32[10]{0:T(128)} %pad_add_fusion.2.info, bf16[2,128,4096]{2,1,0:T(8,128)(2,1)} %q_own.3, ...), custom_call_target="tpu_custom_call" | custom-call | flops 3019898880 | bytes 2097152 | tf_op jit(solution)/shard_map/grads_1/pallas_call | solution.py:276
  63.1 1.3 %collective-permute-start.15 = (bf16[4,2,64,256]{3,2,1,0:T(8,128)(2,1)S(1)}, bf16[4,2,64,256]{3,2,1,0:T(8,128)(2,1)S(1)}, u32[]{:S(2)}, u32[]{:S(2)}) collective-permute-start(bf16[4,2,64,256]{3,2,1,0:T(8,128)(2,1)S(1)} %copy-done.10), channel_id=1, source_target_pairs={{2,0},{3,1},{0,2},{1,3},{6,4},{7,5},{4,6},{5,7},{10,8},{11,9},{8,1... | collective-permute-start | bytes 786440 | tf_op jit(solution)/shard_map/ppermute | solution.py:27
  64.4 0.8 collective-permute-start.19
  65.3 1.0 copy.54
  66.4 0.5 collective-permute-start.12
  67.4 1.0 copy.52
  68.4 4.0 %collective-permute-done.15 = bf16[4,2,64,256]{3,2,1,0:T(8,128)(2,1)S(1)} collective-permute-done((bf16[4,2,64,256]{3,2,1,0:T(8,128)(2,1)S(1)}, bf16[4,2,64,256]{3,2,1,0:T(8,128)(2,1)S(1)}, u32[]{:S(2)}, u32[]{:S(2)}) %collective-permute-start.15) | collective-permute-done | bytes 262176 | tf_op jit(solution)/shard_map/ppermute | solution.py:27
  72.4 6.6 %collective-permute-start.16 = (bf16[2,2,64,256]{3,2,1,0:T(8,128)(2,1)S(1)}, bf16[2,2,64,256]{3,2,1,0:T(8,128)(2,1)S(1)}, u32[]{:S(2)}, u32[]{:S(2)}) collective-permute-start(bf16[2,2,64,256]{3,2,1,0:T(8,128)(2,1)S(1)} %slice.95), channel_id=1, source_target_pairs={{4,0},{5,1},{6,2},{7,3},{0,4},{1,5},{2,6},{3,7},{12,8},{13,9},{14,... | collective-permute-start | bytes 393224 | tf_op jit(solution)/shard_map/ppermute | solution.py:27
  79.1 4.7 %collective-permute-start.20 = (bf16[2,2,64,256]{3,2,1,0:T(8,128)(2,1)S(1)}, bf16[2,2,64,256]{3,2,1,0:T(8,128)(2,1)S(1)}, u32[]{:S(2)}, u32[]{:S(2)}) collective-permute-start(bf16[2,2,64,256]{3,2,1,0:T(8,128)(2,1)S(1)} %slice.94), channel_id=1, source_target_pairs={{4,0},{5,1},{6,2},{7,3},{0,4},{1,5},{2,6},{3,7},{12,8},{13,9},{14,... | collective-permute-start | bytes 393224 | tf_op jit(solution)/shard_map/ppermute | solution.py:27
  83.9 10.1 %collective-permute-start.17 = (bf16[1,2,64,256]{3,2,1,0:T(8,128)(2,1)S(1)}, bf16[1,2,64,256]{3,2,1,0:T(8,128)(2,1)S(1)}, u32[]{:S(2)}, u32[]{:S(2)}) collective-permute-start(bf16[1,2,64,256]{3,2,1,0:T(8,128)(2,1)S(1)} %slice.97), channel_id=1, source_target_pairs={{8,0},{9,1},{10,2},{11,3},{12,4},{13,5},{14,6},{15,7},{0,8},{1,9},... | collective-permute-start | bytes 196616 | tf_op jit(solution)/shard_map/ppermute | solution.py:27
  94.0 6.0 %collective-permute-start.21 = (bf16[1,2,64,256]{3,2,1,0:T(8,128)(2,1)S(1)}, bf16[1,2,64,256]{3,2,1,0:T(8,128)(2,1)S(1)}, u32[]{:S(2)}, u32[]{:S(2)}) collective-permute-start(bf16[1,2,64,256]{3,2,1,0:T(8,128)(2,1)S(1)} %slice.96), channel_id=1, source_target_pairs={{8,0},{9,1},{10,2},{11,3},{12,4},{13,5},{14,6},{15,7},{0,8},{1,9},... | collective-permute-start | bytes 196616 | tf_op jit(solution)/shard_map/ppermute | solution.py:27
  100.1 5.5 %collective-permute-start.18 = (bf16[2,64,256]{2,1,0:T(8,128)(2,1)S(1)}, bf16[2,64,256]{2,1,0:T(8,128)(2,1)S(1)}, u32[]{:S(2)}, u32[]{:S(2)}) collective-permute-start(bf16[2,64,256]{2,1,0:T(8,128)(2,1)S(1)} %fusion.2), channel_id=1, source_target_pairs={{16,0},{0,16},{17,1},{1,17},{18,2},{2,18},{19,3},{3,19},{20,4},{4,... | collective-permute-start | bytes 196616 | tf_op jit(solution)/shard_map/ppermute | solution.py:27
  105.6 3.2 %collective-permute-start.22 = (bf16[2,64,256]{2,1,0:T(8,128)(2,1)S(1)}, bf16[2,64,256]{2,1,0:T(8,128)(2,1)S(1)}, u32[]{:S(2)}, u32[]{:S(2)}) collective-permute-start(bf16[2,64,256]{2,1,0:T(8,128)(2,1)S(1)} %fusion.3), channel_id=1, source_target_pairs={{16,0},{0,16},{17,1},{1,17},{18,2},{2,18},{19,3},{3,19},{20,4},{4,... | collective-permute-start | bytes 196616 | tf_op jit(solution)/shard_map/ppermute | solution.py:27
  108.8 0.8 copy-done.2
  109.6 1.2 %broadcast_select_fusion.1 = (bf16[2,128,1,2,1024]{4,1,0,3,2:T(8,128)(2,1)S(1)}, bf16[2,128,1,2,1024]{4,1,0,3,2:T(8,128)(2,1)S(1)}) fusion(pred[]{:T(512)S(6)} %eq.4, bf16[2,128,1,1,1024]{4,1,0,3,2:T(8,128)(2,1)} %bitcast.47, bf16[2,128,1,1,1024]{4,1,0,3,2:T(8,128)(2,1)S(1)} %bitcast.46, bf16[2,128,1,1,1024]{4,1,0,3,2:T(8,128)(2,1)S(1)} %bitcast.45, ...), kind=kLoop, calls=%fused_computation.6 | loop fusion | flops 2097152 | bytes 4194305 | tf_op jit(solution)/shard_map/jit(_where)/select_n | solution.py:361
  110.9 0.7 copy.38
  111.5 0.7 copy.39
  112.4 0.5 collective-permute-start.24
  113.3 2.7 %copy.51 = bf16[2,128,4096]{2,1,0:T(8,128)(2,1)} copy(bf16[2,128,4096]{1,2,0:T(8,128)(2,1)S(1)} %bitcast.36) | data formatting | bytes 4194304
  117.2 0.9 reshape.199
  (106 shorter events, 4.1 us)
Async XLA Ops:
  2.6 18.3 %collective-permute-start.4 = (bf16[64,512]{1,0:T(8,128)(2,1)S(1)}, bf16[64,512]{1,0:T(8,128)(2,1)}, u32[]{:S(2)}, u32[]{:S(2)}) collective-permute-start(bf16[64,512]{1,0:T(8,128)(2,1)S(1)} %bitcast.53), channel_id=1, source_target_pairs={{1,0},{0,1},{3,2},{2,3},{5,4},{4,5},{7,6},{6,7},{9,8},{8,9},{11,10... | collective-permute-start | bytes 196616 | tf_op jit(solution)/shard_map/ppermute | solution.py:27
  9.2 37.2 %collective-permute-start.2 = (bf16[2,128,2048]{2,1,0:T(8,128)(2,1)S(1)}, bf16[2,128,2048]{2,1,0:T(8,128)(2,1)}, u32[]{:S(2)}, u32[]{:S(2)}) collective-permute-start(bf16[2,128,2048]{2,1,0:T(8,128)(2,1)S(1)} %bitcast.40), channel_id=1, source_target_pairs={{1,0},{0,1},{3,2},{2,3},{5,4},{4,5},{7,6},{6,7},{9,8},{8,9},{11,10... | collective-permute-start | bytes 3145736 | tf_op jit(solution)/shard_map/ppermute | solution.py:27
  14.8 1.2 %copy-start.3 = (bf16[2,128,1024]{2,1,0:T(8,128)(2,1)S(1)}, bf16[2,128,1024]{2,1,0:T(8,128)(2,1)}, u32[]{:S(2)}) copy-start(bf16[2,128,1024]{2,1,0:T(8,128)(2,1)} %bv_own.3) | copy-start | bytes 1572868
  14.8 3.9 %copy-start.12 = (s32[2]{0:T(128)S(1)}, s32[2]{0:T(128)}, u32[]{:S(2)}) copy-start(s32[2]{0:T(128)} %param.11) | copy-start | bytes 28
  14.8 3.9 %copy-start.13 = (s32[2]{0:T(128)S(1)}, s32[2]{0:T(128)}, u32[]{:S(2)}) copy-start(s32[2]{0:T(128)} %param.10) | copy-start | bytes 28
  15.4 31.7 %collective-permute-start.1 = (bf16[2,128,2048]{2,1,0:T(8,128)(2,1)S(1)}, bf16[2,128,2048]{2,1,0:T(8,128)(2,1)}, u32[]{:S(2)}, u32[]{:S(2)}) collective-permute-start(bf16[2,128,2048]{2,1,0:T(8,128)(2,1)S(1)} %bitcast.41), channel_id=1, source_target_pairs={{1,0},{0,1},{3,2},{2,3},{5,4},{4,5},{7,6},{6,7},{9,8},{8,9},{11,10... | collective-permute-start | bytes 3145736 | tf_op jit(solution)/shard_map/ppermute | solution.py:27
  18.3 22.4 %collective-permute-start.3 = (bf16[2,128,512]{2,1,0:T(8,128)(2,1)S(1)}, bf16[2,128,512]{2,1,0:T(8,128)(2,1)S(1)}, u32[]{:S(2)}, u32[]{:S(2)}) collective-permute-start(bf16[2,128,512]{2,1,0:T(8,128)(2,1)S(1)} %reshape.194), channel_id=1, source_target_pairs={{1,0},{0,1},{3,2},{2,3},{5,4},{4,5},{7,6},{6,7},{9,8},{8,9},{11,10... | collective-permute-start | bytes 786440 | tf_op jit(solution)/shard_map/ppermute | solution.py:27
  18.9 1.2 collective-permute-start
  22.6 8.1 %collective-permute-start.5 = (bf16[1,2,64,256]{3,2,1,0:T(8,128)(2,1)S(1)}, bf16[1,2,64,256]{3,2,1,0:T(8,128)(2,1)S(1)}, u32[]{:S(2)}, u32[]{:S(2)}) collective-permute-start(bf16[1,2,64,256]{3,2,1,0:T(8,128)(2,1)S(1)} %reshape_squeeze.6), channel_id=1, source_target_pairs={{8,0},{9,1},{10,2},{11,3},{12,4},{13,5},{14,6},{15,7},{0,8},{1,9},... | collective-permute-start | bytes 196616 | tf_op jit(solution)/shard_map/ppermute | solution.py:27
  26.5 6.7 %collective-permute-start.8 = (bf16[1,2,64,256]{3,2,1,0:T(8,128)(2,1)S(1)}, bf16[1,2,64,256]{3,2,1,0:T(8,128)(2,1)S(1)}, u32[]{:S(2)}, u32[]{:S(2)}) collective-permute-start(bf16[1,2,64,256]{3,2,1,0:T(8,128)(2,1)S(1)} %reshape_squeeze.7), channel_id=1, source_target_pairs={{8,0},{9,1},{10,2},{11,3},{12,4},{13,5},{14,6},{15,7},{0,8},{1,9},... | collective-permute-start | bytes 196616 | tf_op jit(solution)/shard_map/ppermute | solution.py:27
  30.7 6.4 %collective-permute-start.6 = (bf16[2,2,64,256]{3,2,1,0:T(8,128)(2,1)S(1)}, bf16[2,2,64,256]{3,2,1,0:T(8,128)(2,1)S(1)}, u32[]{:S(2)}, u32[]{:S(2)}) collective-permute-start(bf16[2,2,64,256]{3,2,1,0:T(8,128)(2,1)S(1)} %pad_maximum_fusion.7), channel_id=1, source_target_pairs={{4,0},{5,1},{6,2},{7,3},{0,4},{1,5},{2,6},{3,7},{12,8},{13,9},{14,... | collective-permute-start | bytes 393224 | tf_op jit(solution)/shard_map/ppermute | solution.py:27
  33.3 5.9 %collective-permute-start.9 = (bf16[2,2,64,256]{3,2,1,0:T(8,128)(2,1)S(1)}, bf16[2,2,64,256]{3,2,1,0:T(8,128)(2,1)S(1)}, u32[]{:S(2)}, u32[]{:S(2)}) collective-permute-start(bf16[2,2,64,256]{3,2,1,0:T(8,128)(2,1)S(1)} %pad_maximum_fusion.8), channel_id=1, source_target_pairs={{4,0},{5,1},{6,2},{7,3},{0,4},{1,5},{2,6},{3,7},{12,8},{13,9},{14,... | collective-permute-start | bytes 393224 | tf_op jit(solution)/shard_map/ppermute | solution.py:27
  37.1 10.0 %copy-start.7 = (bf16[4,2,64,256]{3,2,1,0:T(8,128)(2,1)}, bf16[4,2,64,256]{3,2,1,0:T(8,128)(2,1)S(1)}, u32[]{:S(2)}) copy-start(bf16[4,2,64,256]{3,2,1,0:T(8,128)(2,1)S(1)} %constant_dynamic-update-slice_fusion.2.kv_near) | copy-start | bytes 786436
  37.2 9.2 %collective-permute-start.7 = (bf16[4,2,64,256]{3,2,1,0:T(8,128)(2,1)S(1)}, bf16[4,2,64,256]{3,2,1,0:T(8,128)(2,1)S(1)}, u32[]{:S(2)}, u32[]{:S(2)}) collective-permute-start(bf16[4,2,64,256]{3,2,1,0:T(8,128)(2,1)S(1)} %constant_dynamic-update-slice_fusion.2.kv_near), channel_id=1, source_target_pairs={{2,0},{3,1},{0,2},{1,3},{6,4},{7,5},{4,6},{5,7},{10,8},{11,9},{8,1... | collective-permute-start | bytes 786440 | tf_op jit(solution)/shard_map/ppermute | solution.py:27
  39.2 15.9 %copy-start.8 = (bf16[4,2,64,256]{3,2,1,0:T(8,128)(2,1)}, bf16[4,2,64,256]{3,2,1,0:T(8,128)(2,1)S(1)}, u32[]{:S(2)}) copy-start(bf16[4,2,64,256]{3,2,1,0:T(8,128)(2,1)S(1)} %constant_dynamic-update-slice_fusion.5.kv_near) | copy-start | bytes 786436
  39.2 16.0 %collective-permute-start.10 = (bf16[4,2,64,256]{3,2,1,0:T(8,128)(2,1)S(1)}, bf16[4,2,64,256]{3,2,1,0:T(8,128)(2,1)}, u32[]{:S(2)}, u32[]{:S(2)}) collective-permute-start(bf16[4,2,64,256]{3,2,1,0:T(8,128)(2,1)S(1)} %constant_dynamic-update-slice_fusion.5.kv_near), channel_id=1, source_target_pairs={{2,0},{3,1},{0,2},{1,3},{6,4},{7,5},{4,6},{5,7},{10,8},{11,9},{8,1... | collective-permute-start | bytes 786440 | tf_op jit(solution)/shard_map/ppermute | solution.py:27
  40.8 6.3 %copy-start.9 = (bf16[2,128,512]{2,1,0:T(8,128)(2,1)}, bf16[2,128,512]{2,1,0:T(8,128)(2,1)S(1)}, u32[]{:S(2)}) copy-start(bf16[2,128,512]{2,1,0:T(8,128)(2,1)S(1)} %collective-permute-done.3.bk_far.bv_far) | copy-start | bytes 786436
  46.4 0.7 copy-start.11
  55.1 8.0 %copy-start.10 = (bf16[4,2,64,256]{3,2,1,0:T(8,128)(2,1)S(1)}, bf16[4,2,64,256]{3,2,1,0:T(8,128)(2,1)}, u32[]{:S(2)}) copy-start(bf16[4,2,64,256]{3,2,1,0:T(8,128)(2,1)} %get-tuple-element.24) | copy-start | bytes 786436
  55.1 10.1 %copy-start.6 = (bf16[2,128,256]{2,1,0:T(8,128)(2,1)S(1)}, bf16[2,128,256]{2,1,0:T(8,128)(2,1)}, u32[]{:S(2)}) copy-start(bf16[2,128,256]{2,1,0:T(8,128)(2,1)} %get-tuple-element.19) | copy-start | bytes 393220
  55.1 11.3 %collective-permute-start.13 = (bf16[2,128,256]{2,1,0:T(8,128)(2,1)}, bf16[2,128,256]{2,1,0:T(8,128)(2,1)S(1)}, u32[]{:S(2)}, u32[]{:S(2)}) collective-permute-start(bf16[2,128,256]{2,1,0:T(8,128)(2,1)} %get-tuple-element.21), channel_id=1, source_target_pairs={{1,0},{0,1},{3,2},{2,3},{5,4},{4,5},{7,6},{6,7},{9,8},{8,9},{11,10... | collective-permute-start | bytes 393224 | tf_op jit(solution)/shard_map/ppermute | solution.py:27
  63.0 4.0 %collective-permute-start.14 = (bf16[2,128,256]{2,1,0:T(8,128)(2,1)}, bf16[2,128,256]{2,1,0:T(8,128)(2,1)S(1)}, u32[]{:S(2)}, u32[]{:S(2)}) collective-permute-start(bf16[2,128,256]{2,1,0:T(8,128)(2,1)} %get-tuple-element.22), channel_id=1, source_target_pairs={{1,0},{0,1},{3,2},{2,3},{5,4},{4,5},{7,6},{6,7},{9,8},{8,9},{11,10... | collective-permute-start | bytes 393224 | tf_op jit(solution)/shard_map/ppermute | solution.py:27
  63.1 9.2 %collective-permute-start.15 = (bf16[4,2,64,256]{3,2,1,0:T(8,128)(2,1)S(1)}, bf16[4,2,64,256]{3,2,1,0:T(8,128)(2,1)S(1)}, u32[]{:S(2)}, u32[]{:S(2)}) collective-permute-start(bf16[4,2,64,256]{3,2,1,0:T(8,128)(2,1)S(1)} %copy-done.10), channel_id=1, source_target_pairs={{2,0},{3,1},{0,2},{1,3},{6,4},{7,5},{4,6},{5,7},{10,8},{11,9},{8,1... | collective-permute-start | bytes 786440 | tf_op jit(solution)/shard_map/ppermute | solution.py:27
  64.4 14.7 %collective-permute-start.19 = (bf16[4,2,64,256]{3,2,1,0:T(8,128)(2,1)}, bf16[4,2,64,256]{3,2,1,0:T(8,128)(2,1)S(1)}, u32[]{:S(2)}, u32[]{:S(2)}) collective-permute-start(bf16[4,2,64,256]{3,2,1,0:T(8,128)(2,1)} %get-tuple-element.26), channel_id=1, source_target_pairs={{2,0},{3,1},{0,2},{1,3},{6,4},{7,5},{4,6},{5,7},{10,8},{11,9},{8,1... | collective-permute-start | bytes 786440 | tf_op jit(solution)/shard_map/ppermute | solution.py:27
  66.3 42.5 %collective-permute-start.11 = (bf16[2,128,1024]{2,1,0:T(8,128)(2,1)}, bf16[2,128,1024]{2,1,0:T(8,128)(2,1)S(1)}, u32[]{:S(2)}, u32[]{:S(2)}) collective-permute-start(bf16[2,128,1024]{2,1,0:T(8,128)(2,1)} %get-tuple-element.17), channel_id=1, source_target_pairs={{1,0},{0,1},{3,2},{2,3},{5,4},{4,5},{7,6},{6,7},{9,8},{8,9},{11,10... | collective-permute-start | bytes 1572872 | tf_op jit(solution)/shard_map/ppermute | solution.py:27
  66.4 42.4 %collective-permute-start.12 = (bf16[2,128,1024]{2,1,0:T(8,128)(2,1)}, bf16[2,128,1024]{2,1,0:T(8,128)(2,1)S(1)}, u32[]{:S(2)}, u32[]{:S(2)}) collective-permute-start(bf16[2,128,1024]{2,1,0:T(8,128)(2,1)} %get-tuple-element.18), channel_id=1, source_target_pairs={{1,0},{0,1},{3,2},{2,3},{5,4},{4,5},{7,6},{6,7},{9,8},{8,9},{11,10... | collective-permute-start | bytes 1572872 | tf_op jit(solution)/shard_map/ppermute | solution.py:27
  67.2 5.2 %copy-start.4 = (f32[4,2,64,256]{3,2,1,0:T(8,128)S(1)}, f32[4,2,64,256]{3,2,1,0:T(8,128)}, u32[]{:S(2)}) copy-start(f32[4,2,64,256]{3,2,1,0:T(8,128)} %get-tuple-element.23) | copy-start | bytes 1572868
  67.3 11.7 %copy-start.5 = (f32[4,2,64,256]{3,2,1,0:T(8,128)S(1)}, f32[4,2,64,256]{3,2,1,0:T(8,128)}, u32[]{:S(2)}) copy-start(f32[4,2,64,256]{3,2,1,0:T(8,128)} %get-tuple-element.25) | copy-start | bytes 1572868
  72.4 37.2 %copy-start = (bf16[2,128,1024]{2,1,0:T(8,128)(2,1)S(1)}, bf16[2,128,1024]{2,1,0:T(8,128)(2,1)}, u32[]{:S(2)}) copy-start(bf16[2,128,1024]{2,1,0:T(8,128)(2,1)} %get-tuple-element.15) | copy-start | bytes 1572868
  72.4 37.2 %copy-start.1 = (bf16[2,128,1024]{2,1,0:T(8,128)(2,1)S(1)}, bf16[2,128,1024]{2,1,0:T(8,128)(2,1)}, u32[]{:S(2)}) copy-start(bf16[2,128,1024]{2,1,0:T(8,128)(2,1)} %get-tuple-element.16) | copy-start | bytes 1572868
  72.4 11.4 %collective-permute-start.16 = (bf16[2,2,64,256]{3,2,1,0:T(8,128)(2,1)S(1)}, bf16[2,2,64,256]{3,2,1,0:T(8,128)(2,1)S(1)}, u32[]{:S(2)}, u32[]{:S(2)}) collective-permute-start(bf16[2,2,64,256]{3,2,1,0:T(8,128)(2,1)S(1)} %slice.95), channel_id=1, source_target_pairs={{4,0},{5,1},{6,2},{7,3},{0,4},{1,5},{2,6},{3,7},{12,8},{13,9},{14,... | collective-permute-start | bytes 393224 | tf_op jit(solution)/shard_map/ppermute | solution.py:27
  79.1 14.8 %collective-permute-start.20 = (bf16[2,2,64,256]{3,2,1,0:T(8,128)(2,1)S(1)}, bf16[2,2,64,256]{3,2,1,0:T(8,128)(2,1)S(1)}, u32[]{:S(2)}, u32[]{:S(2)}) collective-permute-start(bf16[2,2,64,256]{3,2,1,0:T(8,128)(2,1)S(1)} %slice.94), channel_id=1, source_target_pairs={{4,0},{5,1},{6,2},{7,3},{0,4},{1,5},{2,6},{3,7},{12,8},{13,9},{14,... | collective-permute-start | bytes 393224 | tf_op jit(solution)/shard_map/ppermute | solution.py:27
  83.9 16.2 %collective-permute-start.17 = (bf16[1,2,64,256]{3,2,1,0:T(8,128)(2,1)S(1)}, bf16[1,2,64,256]{3,2,1,0:T(8,128)(2,1)S(1)}, u32[]{:S(2)}, u32[]{:S(2)}) collective-permute-start(bf16[1,2,64,256]{3,2,1,0:T(8,128)(2,1)S(1)} %slice.97), channel_id=1, source_target_pairs={{8,0},{9,1},{10,2},{11,3},{12,4},{13,5},{14,6},{15,7},{0,8},{1,9},... | collective-permute-start | bytes 196616 | tf_op jit(solution)/shard_map/ppermute | solution.py:27
  94.0 11.6 %collective-permute-start.21 = (bf16[1,2,64,256]{3,2,1,0:T(8,128)(2,1)S(1)}, bf16[1,2,64,256]{3,2,1,0:T(8,128)(2,1)S(1)}, u32[]{:S(2)}, u32[]{:S(2)}) collective-permute-start(bf16[1,2,64,256]{3,2,1,0:T(8,128)(2,1)S(1)} %slice.96), channel_id=1, source_target_pairs={{8,0},{9,1},{10,2},{11,3},{12,4},{13,5},{14,6},{15,7},{0,8},{1,9},... | collective-permute-start | bytes 196616 | tf_op jit(solution)/shard_map/ppermute | solution.py:27
  100.1 12.1 %collective-permute-start.18 = (bf16[2,64,256]{2,1,0:T(8,128)(2,1)S(1)}, bf16[2,64,256]{2,1,0:T(8,128)(2,1)S(1)}, u32[]{:S(2)}, u32[]{:S(2)}) collective-permute-start(bf16[2,64,256]{2,1,0:T(8,128)(2,1)S(1)} %fusion.2), channel_id=1, source_target_pairs={{16,0},{0,16},{17,1},{1,17},{18,2},{2,18},{19,3},{3,19},{20,4},{4,... | collective-permute-start | bytes 196616 | tf_op jit(solution)/shard_map/ppermute | solution.py:27
  105.6 6.7 %collective-permute-start.22 = (bf16[2,64,256]{2,1,0:T(8,128)(2,1)S(1)}, bf16[2,64,256]{2,1,0:T(8,128)(2,1)S(1)}, u32[]{:S(2)}, u32[]{:S(2)}) collective-permute-start(bf16[2,64,256]{2,1,0:T(8,128)(2,1)S(1)} %fusion.3), channel_id=1, source_target_pairs={{16,0},{0,16},{17,1},{1,17},{18,2},{2,18},{19,3},{3,19},{20,4},{4,... | collective-permute-start | bytes 196616 | tf_op jit(solution)/shard_map/ppermute | solution.py:27
  108.8 0.8 copy-start.2
  112.2 4.0 %collective-permute-start.23 = (f32[64,256]{1,0:T(8,128)S(1)}, f32[64,256]{1,0:T(8,128)S(1)}, u32[]{:S(2)}, u32[]{:S(2)}) collective-permute-start(f32[64,256]{1,0:T(8,128)S(1)} %get-tuple-element.41), channel_id=1, source_target_pairs={{1,0},{0,1},{3,2},{2,3},{5,4},{4,5},{7,6},{6,7},{9,8},{8,9},{11,10... | collective-permute-start | bytes 196616 | tf_op jit(solution)/shard_map/ppermute | solution.py:27
  112.4 4.0 %collective-permute-start.24 = (f32[64,256]{1,0:T(8,128)S(1)}, f32[64,256]{1,0:T(8,128)S(1)}, u32[]{:S(2)}, u32[]{:S(2)}) collective-permute-start(f32[64,256]{1,0:T(8,128)S(1)} %get-tuple-element.43), channel_id=1, source_target_pairs={{1,0},{0,1},{3,2},{2,3},{5,4},{4,5},{7,6},{6,7},{9,8},{8,9},{11,10... | collective-permute-start | bytes 196616 | tf_op jit(solution)/shard_map/ppermute | solution.py:27

commit v2 on v1

--- a/solution.py
+++ b/solution.py
@@ -7,6 +7,7 @@
 from jax.experimental import pallas as pl
 from jax.experimental.pallas import tpu as pltpu
 from jax.sharding import PartitionSpec as P
+
 
 H = 32
 KVH = 4
@@ -31,40 +32,12 @@
     return lax.dot_general(a, b, dims, preferred_element_type=F32)
 
 
-def head_kernel(
-    offsets,
-    tiles,
-    info,
-    q_own,
-    q_far,
-    g_own,
-    g_far,
-    bk_own,
-    bk_far,
-    bv_own,
-    bv_far,
-    kv_near,
-    kv_next,
-    dq_own,
-    dq_far,
-    db_own,
-    db_far,
-    keep,
-    send,
-    keys,
-    values,
-    keys_t,
-    bkeys,
-    bvalues,
-    bkeys_t,
-    s_scr,
-    dp_scr,
-    dk_acc,
-    dv_acc,
-    dbk_acc,
-    dbv_acc,
-    dq_scr,
-):
+def head_kernel(head, offsets, tiles, info, *refs):
+    ins, refs = refs[:-19], refs[-19:]
+    q_own, q_far, g_own, g_far, bk_own, bk_far, bv_own, bv_far, kv_near, kv_next = ins[:10]
+    dq_own, dq_far, db_own, db_far, keep, send = refs[:6]
+    keys, values, keys_t, bkeys, bvalues, bkeys_t, s_scr, dp_scr = refs[6:14]
+    dk_acc, dv_acc, dbk_acc, dbv_acc, dq_scr = refs[14:]
     t = pl.program_id(0)
     me = info[1]
     rr = kv_near.shape[2]
@@ -192,13 +165,18 @@
 
             lax.fori_loop(0, count, step, 0)
 
-    for mine, dq_ref, db_ref in ((own, dq_own, db_own), (jnp.logical_not(own), dq_far, db_far)):
+    for side, (mine, dq_ref, db_ref) in enumerate(
+        ((own, dq_own, db_own), (jnp.logical_not(own), dq_far, db_far))
+    ):
 
         @pl.when(mine)
         def _():
             dq_ref[0] = dq_scr[...]
-            db_ref[0, :, :DH] = dbk_acc[...].astype(BF16)
-            db_ref[0, :, DH:] = dbv_acc[...].astype(BF16)
+            if len(ins) > 10:
+                db_ref[0] = ins[12 + side][0]
+            at = pl.multiple_of((info[0] * HEADS + head) * DH, DH)
+            db_ref[0, :, pl.ds(at, DH)] = dbk_acc[...].astype(BF16)
+            db_ref[0, :, pl.ds(at + KVH * DH, DH)] = dbv_acc[...].astype(BF16)
 
     @pl.when(t == 2 * tiles - 1)
     def _():
@@ -208,13 +186,14 @@
             out[j, b0, :, DH:] = dv_acc[pl.ds(at, rr), :].astype(out.dtype)
 
 
-def head_grads(head, offsets, info, q, q_far, g, g_far, b, b_far, near, nxt):
+def head_grads(head, offsets, info, q, q_far, g, g_far, b, b_far, near, nxt, earlier):
     tiles, rows, _ = q.shape
     half = near.shape[0]
     rr = near.shape[2]
     roots = 2 * half * CORES * rr
     qw = GROUPS * DH
     qrows = GROUPS * CHUNK
+    first = earlier is None
 
     def low(t):
         return jnp.minimum(t, tiles - 1)
@@ -228,6 +207,8 @@
     whole = pl.BlockSpec(near.shape, lambda t, info: (0, 0, 0, 0))
     q_near_spec = pl.BlockSpec((1, rows, qw), lambda t, info: (low(t), 0, col(info)))
     q_far_spec = pl.BlockSpec((1, rows, qw), lambda t, info: (high(t), 0, head))
+    db_near_spec = pl.BlockSpec((1, rows, b.shape[2]), lambda t, info: (low(t), 0, 0))
+    db_far_spec = pl.BlockSpec((1, rows, b.shape[2]), lambda t, info: (high(t), 0, 0))
     in_specs = [
         q_near_spec,
         q_far_spec,
@@ -240,19 +221,19 @@
         whole,
         whole,
     ]
-    out_specs = [
-        pl.BlockSpec((1, rows, qw), lambda t, info: (low(t), 0, 0)),
-        pl.BlockSpec((1, rows, qw), lambda t, info: (high(t), 0, 0)),
-        pl.BlockSpec((1, rows, 2 * DH), lambda t, info: (low(t), 0, 0)),
-        pl.BlockSpec((1, rows, 2 * DH), lambda t, info: (high(t), 0, 0)),
-        whole,
-        whole,
-    ]
+    args = [q, q_far, g, g_far, b, b_far, b, b_far, near, nxt]
+    aliases = {}
+    if not first:
+        any_spec = pl.BlockSpec(memory_space=pl.ANY)
+        in_specs += [any_spec, any_spec, db_near_spec, db_far_spec]
+        aliases = {1 + len(args) + i: i for i in range(4)}
+        args += earlier
+    out_specs = [q_near_spec, q_far_spec, db_near_spec, db_far_spec, whole, whole]
     out_shape = [
-        jax.ShapeDtypeStruct((tiles, rows, qw), BF16),
-        jax.ShapeDtypeStruct((tiles, rows, qw), BF16),
-        jax.ShapeDtypeStruct((tiles, rows, 2 * DH), BF16),
-        jax.ShapeDtypeStruct((tiles, rows, 2 * DH), BF16),
+        jax.ShapeDtypeStruct(q.shape, BF16),
+        jax.ShapeDtypeStruct((tiles, rows, HEADS * qw), BF16),
+        jax.ShapeDtypeStruct(b.shape, BF16),
+        jax.ShapeDtypeStruct(b.shape, BF16),
         jax.ShapeDtypeStruct(near.shape, F32),
         jax.ShapeDtypeStruct(near.shape, BF16),
     ]
@@ -273,8 +254,8 @@
         pltpu.VMEM((rows, qw), BF16),
     ]
     flops = 2 * 5 * tiles * rows * GROUPS * span * DH
-    return pl.pallas_call(
-        functools.partial(head_kernel, offsets, tiles),
+    outs = pl.pallas_call(
+        functools.partial(head_kernel, head, offsets, tiles),
         grid_spec=pltpu.PrefetchScalarGridSpec(
             num_scalar_prefetch=1,
             grid=(2 * tiles,),
@@ -283,12 +264,13 @@
             scratch_shapes=scratch,
         ),
         out_shape=out_shape,
+        input_output_aliases=aliases,
         cost_estimate=pl.CostEstimate(
             flops=flops, bytes_accessed=8 * tiles * rows * qw, transcendentals=0
         ),
         compiler_params=pltpu.CompilerParams(dimension_semantics=("arbitrary",)),
-        name=f"grads_{head}",
-    )(info, q, q_far, g, g_far, b, b_far, b, b_far, near, nxt)
+    )(info, *args)
+    return list(outs[:4]), outs[4], outs[5]
 
 
 def local(query, grad_out, branch_kv, root_kv, lengths, segments):
@@ -296,74 +278,86 @@
     n_grp = lax.axis_size("grp")
     me = lax.axis_index("dev")
     core = me % CORES
-    tiles, rows, _ = query.shape
-    rr = root_kv.shape[0]
-    bits = []
-    while (4 << len(bits)) < n_dev:
-        bits.append(4 << len(bits))
-
-    def halves(x, parts):
-        x = x.reshape(x.shape[:-1] + (parts, CORES, x.shape[-1] // (parts * CORES)))
-        axis = x.ndim - 2
-        mine = lax.dynamic_index_in_dim(x, core, axis, keepdims=False)
-        other = lax.dynamic_index_in_dim(x, 1 - core, axis, keepdims=False)
-        flat = x.shape[:-3] + (-1,)
-        return mine.reshape(flat), other.reshape(flat)
-
-    mine, other = halves(root_kv, 2)
-    block = jnp.stack([mine, swapped(other, "dev", 1)])
-    block = block.reshape(1, CORES, rr, 2, HEADS, DH)
+    tiles, _, qcols = query.shape
+    kcols = root_kv.shape[1] // 2
+    offsets = tuple(range(0, n_dev, 2 * CORES))
+
+    def cols(x, which, parts):
+        part = x.shape[-1] // parts
+        wide = part // CORES
+        axis = x.ndim - 1
+        pieces = [
+            lax.dynamic_slice_in_dim(x, p * part + which * wide, wide, axis) for p in range(parts)
+        ]
+        return pieces
+
+    mine = cols(root_kv, core, 2)
+    other = jnp.concatenate(cols(root_kv, 1 - core, 2), axis=1)
+    got = swapped(other, "dev", 1)
+    got = [got[:, : kcols // CORES], got[:, kcols // CORES :]]
     gathered = []
     for head in range(HEADS):
-        x = block[:, :, :, :, head, :].reshape(1, CORES, rr, 2 * DH)
-        for bit in reversed(bits):
-            x = jnp.concatenate([x, swapped(x, "dev", bit)], axis=0)
-        gathered.append((x, swapped(x, "dev", 2)))
-    offsets = [0]
-    for bit in reversed(bits):
-        offsets = offsets + [off + bit for off in offsets]
-
-    q_far = swapped(halves(query, 1)[1], "dev", 1)
-    g_far = swapped(halves(grad_out, 1)[1], "dev", 1)
-    b_far = swapped(halves(branch_kv, 2)[1], "dev", 1)
+        at = slice(head * DH, (head + 1) * DH)
+        x = jnp.stack(
+            [
+                jnp.concatenate([mine[0][:, at], mine[1][:, at]], axis=1),
+                jnp.concatenate([got[0][:, at], got[1][:, at]], axis=1),
+            ]
+        )[None]
+        arrived = [swapped(x, "dev", off) for off in offsets[1:]]
+        x = jnp.concatenate([x] + arrived, axis=0)
+        nxt = swapped(x, "dev", CORES)
+        gathered.append((x, nxt))
+
+    q_far = swapped(cols(query, 1 - core, 1)[0], "dev", 1)
+    g_far = swapped(cols(grad_out, 1 - core, 1)[0], "dev", 1)
+    b_far = swapped(jnp.concatenate(cols(branch_kv, 1 - core, 2), axis=2), "dev", 1)
     meta = jnp.concatenate([lengths, segments]).reshape(2, tiles)
     meta_far = swapped(meta, "dev", 1)
     info = jnp.concatenate(
         [jnp.stack([core, me]), jnp.concatenate([meta, meta_far], axis=1).reshape(-1)]
     )
 
-    q_parts, b_parts, root_parts = [], [], []
+    outs = None
+    sums = []
     for head in range(HEADS):
         near, nxt = gathered[head]
-        dq_own, dq_far, db_own, db_far, keep, send = head_grads(
-            head, tuple(offsets), info, query, q_far, grad_out, g_far, branch_kv, b_far, near, nxt
+        outs, keep, send = head_grads(
+            head, offsets, info, query, q_far, grad_out, g_far, branch_kv, b_far, near, nxt, outs
         )
-        x = keep + swapped(send, "dev", 2)
-        for bit in bits:
-            half = x.shape[0] // 2
-            x = x[:half] + swapped(x[half:].astype(BF16), "dev", bit)
+        back = swapped(send, "dev", CORES)
+        x = keep + back
+        arrived = [swapped(x[j].astype(BF16), "dev", offsets[j]) for j in range(1, len(offsets))]
         x = x[0]
-        hop = 1
-        while hop < n_grp:
-            x = x.astype(BF16)
-            x = x.astype(F32) + swapped(x, "grp", hop).astype(F32)
-            hop *= 2
-        root_parts.append((x[0], swapped(x[1], "dev", 1)))
-        q_parts.append((dq_own, swapped(dq_far, "dev", 1)))
-        b_parts.append((db_own, swapped(db_far, "dev", 1)))
-
-    def joined(parts, kinds):
-        def laid(side):
-            x = jnp.stack([p[side].reshape(p[side].shape[:-1] + (kinds, -1)) for p in parts], -2)
-            return x.reshape(x.shape[:-2] + (-1,))
-
-        near, far = laid(0), laid(1)
-        first = jnp.where(core == 0, near, far)
-        second = jnp.where(core == 0, far, near)
-        x = jnp.stack([first, second], axis=-2)
-        return x.reshape(x.shape[:-3] + (-1,))
-
-    return (joined(q_parts, 1), joined(b_parts, 2), joined(root_parts, 2))
+        for part in arrived:
+            x = x + part
+        sums.append(x)
+    x = jnp.concatenate(sums, axis=2)
+    hop = 1
+    while hop < n_grp:
+        x = x.astype(BF16)
+        back = swapped(x, "grp", hop)
+        x = x.astype(F32) + back.astype(F32)
+        hop *= 2
+    far = swapped(x[1], "dev", 1)
+    near = x[0]
+    pieces = []
+    for part in range(2):
+        for side in range(CORES):
+            for head in range(HEADS):
+                at = (head * 2 + part) * DH
+                pieces.append(
+                    jnp.where(core == side, near[:, at : at + DH], far[:, at : at + DH])
+                )
+    root_grad = jnp.concatenate(pieces, axis=1)
+
+    dq, dq_far, db, db_far = outs
+    dq_got = swapped(dq_far, "dev", 1)
+    db_got = swapped(db_far, "dev", 1)
+    query_grad = lax.dynamic_update_slice_in_dim(dq, dq_got, (1 - core) * (qcols // CORES), 2)
+    col = lax.broadcasted_iota(jnp.int32, db.shape, 2)
+    branch_grad = jnp.where(col // (HEADS * DH) % CORES == core, db, db_got)
+    return (query_grad, branch_grad, root_grad)
 
 
 def solution(mesh):
@@ -375,6 +369,7 @@
         P(("grp", "dev")),
         P(("grp", "dev")),
     )
+
     return jax.shard_map(
         local,
         mesh=mesh,

time: 116 us -> 90.8 us (0.78); the launches traced: 118 us -> 90.5 us
  local copies, waits for them, and re-layouts: 28.5 us -> 9.06 us
  starting transfers between devices: 51.3 us -> 42.1 us
  Pallas kernels: 15.8 us -> 22.1 us
  waiting for transfers between devices: 18.5 us -> 13.8 us
    ppermute x25, starting transfers between devices: 51.3 us -> 42.1 us  [swapped(): return lax.ppermute(block, axis, route)]
    reshape x6 -> x0, local copies, waits for them, and re-layouts: 9.04 us -> none  [the longest x4 7.96 us: halves(): x = x.reshape(x.shape[:-1] + (parts, CORES, x.shape[-1] // (parts * CORES)))]
    pallas_call x2, Pallas kernels: 15.8 us -> 22.1 us  [head_grads(): pl.pallas_call(functools.partial(head_kernel, head, offsets, tiles), grid...]
    ppermute x25, waiting for transfers between devices: 18.5 us -> 13.8 us  [swapped(): return lax.ppermute(block, axis, route)]
    another operation x20 -> x0, local copies, waits for them, and re-layouts: 3.24 us -> none  [the longest x12 1.8 us: laid(): jnp.stack([p[side].reshape(p[side].shape[:-1] + (kinds, -1)) for p in par...]
    dynamic_slice x4, local copies, waits for them, and re-layouts: 7.01 us -> 4.36 us  [cols(): lax.dynamic_slice_in_dim(x, p * part + which * wide, wide, axis)]
    unnamed x38 -> x34, local copies, waits for them, and re-layouts: 6.57 us -> 4.31 us
    select_n x4 -> x0, local copies, waits for them, and re-layouts: 1.54 us -> none  [the longest x2 0.77 us: joined(): first = jnp.where(core == 0, near, far)]
  transfers between devices with their start and end apart: 25 -> 25, of which waited for: 7 -> 10; matrix products, arithmetic and copies ran while one was open for 22% -> 7% of each run, Pallas kernels for 13% -> 24%
where the time goes in v2:
time: 90.8 us; the launch traced here: 90.5 us
  starting transfers between devices  42.1 us (46%)
  Pallas kernels  22.1 us (24%)
  waiting for transfers between devices  13.8 us (15%)
  local copies, waits for them, and re-layouts  9.06 us (10%)
  other arithmetic  2.33 us (3%)
  between operations  1.06 us (1%)
    ppermute x25, starting transfers between devices, swapped(): return lax.ppermute(block, axis, route)  42.1 us
    pallas_call x2, Pallas kernels, head_grads(): pl.pallas_call(functools.partial(head_kernel, head, offsets, tiles), grid...  22.1 us
    ppermute x25, waiting for transfers between devices, swapped(): return lax.ppermute(block, axis, route)  13.8 us
    dynamic_slice x4, local copies, waits for them, and re-layouts, cols(): lax.dynamic_slice_in_dim(x, p * part + which * wide, wide, axis)  4.36 us
    unnamed x34, local copies, waits for them, and re-layouts  4.31 us
  transfers between devices with their start and end apart: 25, of which 10 were waited for; matrix products, arithmetic and copies ran while one was open for 7% of the time, Pallas kernels for 24%

profile of v2, /device:TPU:0, one launch (start us, length us, event | category | flops | bytes accessed | tf_op | source)
XLA Modules:
  0.0 90.5 jit_solution(11610549383826570360)
XLA Ops:
  0.7 0.9 %constant_dynamic-slice_fusion.3 = (bf16[64,256]{1,0:T(8,128)(2,1)S(1)}, bf16[64,256]{1,0:T(8,128)(2,1)S(1)}) fusion(bf16[64,1024]{1,0:T(8,128)(2,1)} %param.9, s32[]{:T(128)S(6)} %select_n.81, s32[]{:T(128)S(6)} %select_n.82), kind=kLoop, calls=%fused_computation.58 | loop fusion | bytes 131080 | tf_op jit(solution)/shard_map/dynamic_slice | solution.py:290
  1.6 0.6 collective-permute-start.4
  2.2 2.4 %constant_dynamic-slice_fusion.9 = bf16[2,128,2048]{2,1,0:T(8,128)(2,1)} fusion(bf16[2,128,4096]{2,1,0:T(8,128)(2,1)} %refs_0_.3, s32[]{:T(128)S(6)} %select_n.80), kind=kLoop, calls=%fused_computation.64 | loop fusion | bytes 2097156 | tf_op jit(solution)/shard_map/dynamic_slice | solution.py:290
  4.6 1.0 %constant_dynamic-slice_fusion.8 = bf16[2,128,2048]{2,1,0:T(8,128)(2,1)} fusion(bf16[2,128,4096]{2,1,0:T(8,128)(2,1)S(1)} %copy-done, s32[]{:T(128)S(6)} %select_n.80), kind=kLoop, calls=%fused_computation.63 | loop fusion | bytes 2097156 | tf_op jit(solution)/shard_map/dynamic_slice | solution.py:290
  5.6 0.5 collective-permute-start.2
  6.1 0.1 pad_add_fusion.1
  6.2 0.1 reshape.18
  6.4 3.7 %collective-permute-start.10 = (bf16[1,2,64,256]{3,2,1,0:T(8,128)(2,1)S(1)}, bf16[1,2,64,256]{3,2,1,0:T(8,128)(2,1)S(1)}, u32[]{:S(2)}, u32[]{:S(2)}) collective-permute-start(bf16[1,2,64,256]{3,2,1,0:T(8,128)(2,1)S(1)} %maximum_bitcast_fusion.1), channel_id=1, source_target_pairs={{8,0},{9,1},{10,2},{11,3},{12,4},{13,5},{14,6},{15,7},{0,8},{1,9},... | collective-permute-start | bytes 196616 | tf_op jit(solution)/shard_map/ppermute | solution.py:28
  10.1 1.3 %collective-permute-start.11 = (bf16[1,2,64,256]{3,2,1,0:T(8,128)(2,1)S(1)}, bf16[1,2,64,256]{3,2,1,0:T(8,128)(2,1)S(1)}, u32[]{:S(2)}, u32[]{:S(2)}) collective-permute-start(bf16[1,2,64,256]{3,2,1,0:T(8,128)(2,1)S(1)} %maximum_bitcast_fusion.1), channel_id=1, source_target_pairs={{12,0},{13,1},{14,2},{15,3},{8,4},{9,5},{10,6},{11,7},{4,8},{5,9},... | collective-permute-start | bytes 196616 | tf_op jit(solution)/shard_map/ppermute | solution.py:28
  11.5 0.2 collective-permute-start.9
  11.7 2.7 %collective-permute-done.10 = bf16[1,2,64,256]{3,2,1,0:T(8,128)(2,1)S(1)} collective-permute-done((bf16[1,2,64,256]{3,2,1,0:T(8,128)(2,1)S(1)}, bf16[1,2,64,256]{3,2,1,0:T(8,128)(2,1)S(1)}, u32[]{:S(2)}, u32[]{:S(2)}) %collective-permute-start.10) | collective-permute-done | bytes 65568 | tf_op jit(solution)/shard_map/ppermute | solution.py:28
  14.5 2.3 %collective-permute-done.11 = bf16[1,2,64,256]{3,2,1,0:T(8,128)(2,1)S(1)} collective-permute-done((bf16[1,2,64,256]{3,2,1,0:T(8,128)(2,1)S(1)}, bf16[1,2,64,256]{3,2,1,0:T(8,128)(2,1)S(1)}, u32[]{:S(2)}, u32[]{:S(2)}) %collective-permute-start.11) | collective-permute-done | bytes 65568 | tf_op jit(solution)/shard_map/ppermute | solution.py:28
  16.8 0.2 collective-permute-done.9
  17.0 0.9 collective-permute-start.5
  18.0 3.1 %collective-permute-start.6 = (bf16[1,2,64,256]{3,2,1,0:T(8,128)(2,1)S(1)}, bf16[1,2,64,256]{3,2,1,0:T(8,128)(2,1)S(1)}, u32[]{:S(2)}, u32[]{:S(2)}) collective-permute-start(bf16[1,2,64,256]{3,2,1,0:T(8,128)(2,1)S(1)} %maximum_bitcast_fusion), channel_id=1, source_target_pairs={{8,0},{9,1},{10,2},{11,3},{12,4},{13,5},{14,6},{15,7},{0,8},{1,9},... | collective-permute-start | bytes 196616 | tf_op jit(solution)/shard_map/ppermute | solution.py:28
  21.1 0.2 collective-permute-done.5
  21.3 1.6 %collective-permute-start.12 = (bf16[4,2,64,256]{3,2,1,0:T(8,128)(2,1)S(1)}, bf16[4,2,64,256]{3,2,1,0:T(8,128)(2,1)S(1)}, u32[]{:S(2)}, u32[]{:S(2)}) collective-permute-start(bf16[4,2,64,256]{3,2,1,0:T(8,128)(2,1)S(1)} %pad_maximum_fusion.2.refs_8_), channel_id=1, source_target_pairs={{2,0},{3,1},{0,2},{1,3},{6,4},{7,5},{4,6},{5,7},{10,8},{11,9},{8,1... | collective-permute-start | bytes 786440 | tf_op jit(solution)/shard_map/ppermute | solution.py:28
  22.9 0.1 pad_add_fusion
  23.0 0.1 reshape.19
  23.0 0.5 collective-permute-done.6
  23.5 4.3 %collective-permute-start.7 = (bf16[1,2,64,256]{3,2,1,0:T(8,128)(2,1)S(1)}, bf16[1,2,64,256]{3,2,1,0:T(8,128)(2,1)S(1)}, u32[]{:S(2)}, u32[]{:S(2)}) collective-permute-start(bf16[1,2,64,256]{3,2,1,0:T(8,128)(2,1)S(1)} %maximum_bitcast_fusion), channel_id=1, source_target_pairs={{12,0},{13,1},{14,2},{15,3},{8,4},{9,5},{10,6},{11,7},{4,8},{5,9},... | collective-permute-start | bytes 196616 | tf_op jit(solution)/shard_map/ppermute | solution.py:28
  27.9 0.6 pad_add_fusion.2.info
  28.5 1.6 %collective-permute-done.7 = bf16[1,2,64,256]{3,2,1,0:T(8,128)(2,1)S(1)} collective-permute-done((bf16[1,2,64,256]{3,2,1,0:T(8,128)(2,1)S(1)}, bf16[1,2,64,256]{3,2,1,0:T(8,128)(2,1)S(1)}, u32[]{:S(2)}, u32[]{:S(2)}) %collective-permute-start.7) | collective-permute-done | bytes 65568 | tf_op jit(solution)/shard_map/ppermute | solution.py:28
  30.2 1.6 %collective-permute-start.8 = (bf16[4,2,64,256]{3,2,1,0:T(8,128)(2,1)S(1)}, bf16[4,2,64,256]{3,2,1,0:T(8,128)(2,1)S(1)}, u32[]{:S(2)}, u32[]{:S(2)}) collective-permute-start(bf16[4,2,64,256]{3,2,1,0:T(8,128)(2,1)S(1)} %pad_maximum_fusion.1.refs_8_), channel_id=1, source_target_pairs={{2,0},{3,1},{0,2},{1,3},{6,4},{7,5},{4,6},{5,7},{10,8},{11,9},{8,1... | collective-permute-start | bytes 786440 | tf_op jit(solution)/shard_map/ppermute | solution.py:28
  31.8 0.7 copy-done.6
  32.4 0.1 copy-done.14
  32.5 1.0 %copy-done.5 = bf16[2,128,2048]{2,1,0:T(8,128)(2,1)} copy-done((bf16[2,128,2048]{2,1,0:T(8,128)(2,1)}, bf16[2,128,2048]{2,1,0:T(8,128)(2,1)S(1)}, u32[]{:S(2)}) %copy-start.5) | copy-done | bytes 1048600
  33.5 10.9 %shard_map.85 = (bf16[2,128,4096]{2,1,0:T(8,128)(2,1)}, bf16[2,128,2048]{2,1,0:T(8,128)(2,1)}, bf16[2,128,1024]{2,1,0:T(8,128)(2,1)}, bf16[2,128,1024]{2,1,0:T(8...) custom-call(s32[10]{0:T(128)} %pad_add_fusion.2.info, bf16[2,128,4096]{2,1,0:T(8,128)(2,1)} %refs_0_.3, ...), custom_call_target="tpu_custom_call" | custom-call | flops 3019898880 | bytes 2097152 | tf_op jit(solution)/shard_map/pallas_call | solution.py:257
  44.4 5.7 %collective-permute-start.15 = (bf16[4,2,64,256]{3,2,1,0:T(8,128)(2,1)}, bf16[4,2,64,256]{3,2,1,0:T(8,128)(2,1)S(1)}, u32[]{:S(2)}, u32[]{:S(2)}) collective-permute-start(bf16[4,2,64,256]{3,2,1,0:T(8,128)(2,1)} %get-tuple-element.24), channel_id=1, source_target_pairs={{2,0},{3,1},{0,2},{1,3},{6,4},{7,5},{4,6},{5,7},{10,8},{11,9},{8,1... | collective-permute-start | bytes 786440 | tf_op jit(solution)/shard_map/ppermute | solution.py:28
  50.1 0.7 copy-done.10
  50.8 11.2 %shard_map.86 = (bf16[2,128,4096]{2,1,0:T(8,128)(2,1)}, bf16[2,128,2048]{2,1,0:T(8,128)(2,1)}, bf16[2,128,1024]{2,1,0:T(8,128)(2,1)}, bf16[2,128,1024]{2,1,0:T(8...) custom-call(s32[10]{0:T(128)} %pad_add_fusion.2.info, ...), custom_call_target="tpu_custom_call", output_to_operand_aliasing={{0}: (11, {}), {1}: (12, {}), {2}: (13, {}), {3}: (14, {})} | custom-call | flops 3019898880 | bytes 2097152 | tf_op jit(solution)/shard_map/pallas_call | solution.py:257
  62.1 5.2 %collective-permute-start.19 = (bf16[4,2,64,256]{3,2,1,0:T(8,128)(2,1)}, bf16[4,2,64,256]{3,2,1,0:T(8,128)(2,1)S(1)}, u32[]{:S(2)}, u32[]{:S(2)}) collective-permute-start(bf16[4,2,64,256]{3,2,1,0:T(8,128)(2,1)} %get-tuple-element.26), channel_id=1, source_target_pairs={{2,0},{3,1},{0,2},{1,3},{6,4},{7,5},{4,6},{5,7},{10,8},{11,9},{8,1... | collective-permute-start | bytes 786440 | tf_op jit(solution)/shard_map/ppermute | solution.py:28
  67.4 0.4 collective-permute-start.16
  67.8 4.1 %collective-permute-start.18 = (bf16[2,64,256]{2,1,0:T(8,128)(2,1)S(1)}, bf16[2,64,256]{2,1,0:T(8,128)(2,1)S(1)}, u32[]{:S(2)}, u32[]{:S(2)}) collective-permute-start(bf16[2,64,256]{2,1,0:T(8,128)(2,1)S(1)} %get-tuple-element.36), channel_id=1, source_target_pairs={{12,0},{13,1},{14,2},{15,3},{8,4},{9,5},{10,6},{11,7},{4,8},{5,9},... | collective-permute-start | bytes 196616 | tf_op jit(solution)/shard_map/ppermute | solution.py:28
  72.0 0.3 collective-permute-start.20
  72.3 0.3 collective-permute-start.21
  72.6 3.8 %collective-permute-start.22 = (bf16[2,64,256]{2,1,0:T(8,128)(2,1)S(1)}, bf16[2,64,256]{2,1,0:T(8,128)(2,1)S(1)}, u32[]{:S(2)}, u32[]{:S(2)}) collective-permute-start(bf16[2,64,256]{2,1,0:T(8,128)(2,1)S(1)} %get-tuple-element.39), channel_id=1, source_target_pairs={{12,0},{13,1},{14,2},{15,3},{8,4},{9,5},{10,6},{11,7},{4,8},{5,9},... | collective-permute-start | bytes 196616 | tf_op jit(solution)/shard_map/ppermute | solution.py:28
  76.5 1.2 %collective-permute-done.20 = bf16[2,64,256]{2,1,0:T(8,128)(2,1)S(1)} collective-permute-done((bf16[2,64,256]{2,1,0:T(8,128)(2,1)S(1)}, bf16[2,64,256]{2,1,0:T(8,128)(2,1)S(1)}, u32[]{:S(2)}, u32[]{:S(2)}) %collective-permute-start.20) | collective-permute-done | bytes 65568 | tf_op jit(solution)/shard_map/ppermute | solution.py:28
  77.8 2.2 %collective-permute-done.21 = bf16[2,64,256]{2,1,0:T(8,128)(2,1)S(1)} collective-permute-done((bf16[2,64,256]{2,1,0:T(8,128)(2,1)S(1)}, bf16[2,64,256]{2,1,0:T(8,128)(2,1)S(1)}, u32[]{:S(2)}, u32[]{:S(2)}) %collective-permute-start.21) | collective-permute-done | bytes 65568 | tf_op jit(solution)/shard_map/ppermute | solution.py:28
  80.0 3.9 %collective-permute-start.23 = (bf16[2,64,512]{2,1,0:T(8,128)(2,1)S(1)}, bf16[2,64,512]{2,1,0:T(8,128)(2,1)S(1)}, u32[]{:S(2)}, u32[]{:S(2)}) collective-permute-start(bf16[2,64,512]{2,1,0:T(8,128)(2,1)S(1)} %pad_maximum_fusion.3), channel_id=1, source_target_pairs={{16,0},{0,16},{17,1},{1,17},{18,2},{2,18},{19,3},{3,19},{20,4},{4,... | collective-permute-start | bytes 393224 | tf_op jit(solution)/shard_map/ppermute | solution.py:28
  84.0 0.5 collective-permute-start.13
  84.5 2.4 %collective-permute-done.23 = bf16[2,64,512]{2,1,0:T(8,128)(2,1)S(1)} collective-permute-done((bf16[2,64,512]{2,1,0:T(8,128)(2,1)S(1)}, bf16[2,64,512]{2,1,0:T(8,128)(2,1)S(1)}, u32[]{:S(2)}, u32[]{:S(2)}) %collective-permute-start.23) | collective-permute-done | bytes 131104 | tf_op jit(solution)/shard_map/ppermute | solution.py:28
  86.9 0.1 collective-permute-start.24
  87.0 1.1 %fusion.2 = bf16[2,128,1024]{2,1,0:T(8,128)(2,1)} fusion(bf16[2,128,1024]{2,1,0:T(8,128)(2,1)S(1)} %copy-done.4, bf16[2,128,1024]{2,1,0:T(8,128)(2,1)S(1)} %collective-permute-done.14, s32[]{:T(128)} %select_n.79, s32[1024]{0:T(1024)S(1)} %get-tuple-element.55, s32[1024]{0:T(1024)S(1)} %get-tuple-element.56, pred[1024]{0:T(1024)(128)(4,1)S(1)} %fusion.13), kind=kLoop, calls=%fused_computation.7 | loop fusion | flops 3670016 | bytes 1582084 | tf_op jit(solution)/shard_map/jit(_where)/select_n | solution.py:359
  88.1 0.2 collective-permute-done.24
  88.5 0.1 constant_dynamic-update-slice_fusion
  88.7 0.5 copy-done.13
  89.2 1.3 %copy-done.3 = bf16[2,128,4096]{2,1,0:T(8,128)(2,1)} copy-done((bf16[2,128,4096]{2,1,0:T(8,128)(2,1)}, bf16[2,128,4096]{2,1,0:T(8,128)(2,1)S(1)}, u32[]{:S(2)}) %copy-start.3) | copy-done | bytes 2097176
  (78 shorter events, 0.8 us)
Async XLA Ops:
  0.6 4.0 %copy-start = (bf16[2,128,4096]{2,1,0:T(8,128)(2,1)S(1)}, bf16[2,128,4096]{2,1,0:T(8,128)(2,1)}, u32[]{:S(2)}) copy-start(bf16[2,128,4096]{2,1,0:T(8,128)(2,1)} %refs_2_.3) | copy-start | bytes 6291460
  1.6 4.8 %collective-permute-start.4 = (bf16[64,512]{1,0:T(8,128)(2,1)S(1)}, bf16[64,512]{1,0:T(8,128)(2,1)S(1)}, u32[]{:S(2)}, u32[]{:S(2)}) collective-permute-start(bf16[64,512]{1,0:T(8,128)(2,1)S(1)} %pad_maximum_fusion.4), channel_id=1, source_target_pairs={{1,0},{0,1},{3,2},{2,3},{5,4},{4,5},{7,6},{6,7},{9,8},{8,9},{11,10... | collective-permute-start | bytes 196616 | tf_op jit(solution)/shard_map/ppermute | solution.py:28
  2.2 3.9 %copy-start.1 = (bf16[2,128,1024]{2,1,0:T(8,128)(2,1)S(1)}, bf16[2,128,1024]{2,1,0:T(8,128)(2,1)}, u32[]{:S(2)}) copy-start(bf16[2,128,1024]{2,1,0:T(8,128)(2,1)} %refs_6_.3) | copy-start | bytes 1572868
  2.2 4.0 %copy-start.15 = (s32[2]{0:T(128)S(1)}, s32[2]{0:T(128)}, u32[]{:S(2)}) copy-start(s32[2]{0:T(128)} %param.11) | copy-start | bytes 28
  2.2 4.0 %copy-start.16 = (s32[2]{0:T(128)S(1)}, s32[2]{0:T(128)}, u32[]{:S(2)}) copy-start(s32[2]{0:T(128)} %param.10) | copy-start | bytes 28
  4.5 1.8 %copy-start.12 = (bf16[64,1024]{1,0:T(8,128)(2,1)S(1)}, bf16[64,1024]{1,0:T(8,128)(2,1)}, u32[]{:S(2)}) copy-start(bf16[64,1024]{1,0:T(8,128)(2,1)} %param.9) | copy-start | bytes 393220
  4.5 27.2 %collective-permute-start.1 = (bf16[2,128,2048]{2,1,0:T(8,128)(2,1)}, bf16[2,128,2048]{2,1,0:T(8,128)(2,1)}, u32[]{:S(2)}, u32[]{:S(2)}) collective-permute-start(bf16[2,128,2048]{2,1,0:T(8,128)(2,1)} %constant_dynamic-slice_fusion.9), channel_id=1, source_target_pairs={{1,0},{0,1},{3,2},{2,3},{5,4},{4,5},{7,6},{6,7},{9,8},{8,9},{11,10... | collective-permute-start | bytes 3145736 | tf_op jit(solution)/shard_map/ppermute | solution.py:28
  5.6 26.2 %collective-permute-start.2 = (bf16[2,128,2048]{2,1,0:T(8,128)(2,1)}, bf16[2,128,2048]{2,1,0:T(8,128)(2,1)S(1)}, u32[]{:S(2)}, u32[]{:S(2)}) collective-permute-start(bf16[2,128,2048]{2,1,0:T(8,128)(2,1)} %constant_dynamic-slice_fusion.8), channel_id=1, source_target_pairs={{1,0},{0,1},{3,2},{2,3},{5,4},{4,5},{7,6},{6,7},{9,8},{8,9},{11,10... | collective-permute-start | bytes 3145736 | tf_op jit(solution)/shard_map/ppermute | solution.py:28
  6.4 8.0 %collective-permute-start.10 = (bf16[1,2,64,256]{3,2,1,0:T(8,128)(2,1)S(1)}, bf16[1,2,64,256]{3,2,1,0:T(8,128)(2,1)S(1)}, u32[]{:S(2)}, u32[]{:S(2)}) collective-permute-start(bf16[1,2,64,256]{3,2,1,0:T(8,128)(2,1)S(1)} %maximum_bitcast_fusion.1), channel_id=1, source_target_pairs={{8,0},{9,1},{10,2},{11,3},{12,4},{13,5},{14,6},{15,7},{0,8},{1,9},... | collective-permute-start | bytes 196616 | tf_op jit(solution)/shard_map/ppermute | solution.py:28
  10.1 6.7 %collective-permute-start.11 = (bf16[1,2,64,256]{3,2,1,0:T(8,128)(2,1)S(1)}, bf16[1,2,64,256]{3,2,1,0:T(8,128)(2,1)S(1)}, u32[]{:S(2)}, u32[]{:S(2)}) collective-permute-start(bf16[1,2,64,256]{3,2,1,0:T(8,128)(2,1)S(1)} %maximum_bitcast_fusion.1), channel_id=1, source_target_pairs={{12,0},{13,1},{14,2},{15,3},{8,4},{9,5},{10,6},{11,7},{4,8},{5,9},... | collective-permute-start | bytes 196616 | tf_op jit(solution)/shard_map/ppermute | solution.py:28
  11.5 5.6 %collective-permute-start.9 = (bf16[1,2,64,256]{3,2,1,0:T(8,128)(2,1)S(1)}, bf16[1,2,64,256]{3,2,1,0:T(8,128)(2,1)S(1)}, u32[]{:S(2)}, u32[]{:S(2)}) collective-permute-start(bf16[1,2,64,256]{3,2,1,0:T(8,128)(2,1)S(1)} %maximum_bitcast_fusion.1), channel_id=1, source_target_pairs={{4,0},{5,1},{6,2},{7,3},{0,4},{1,5},{2,6},{3,7},{12,8},{13,9},{14,... | collective-permute-start | bytes 196616 | tf_op jit(solution)/shard_map/ppermute | solution.py:28
  14.5 17.3 %collective-permute-start.3 = (bf16[2,128,512]{2,1,0:T(8,128)(2,1)S(1)}, bf16[2,128,512]{2,1,0:T(8,128)(2,1)S(1)}, u32[]{:S(2)}, u32[]{:S(2)}) collective-permute-start(bf16[2,128,512]{2,1,0:T(8,128)(2,1)S(1)} %pad_maximum_fusion), channel_id=1, source_target_pairs={{1,0},{0,1},{3,2},{2,3},{5,4},{4,5},{7,6},{6,7},{9,8},{8,9},{11,10... | collective-permute-start | bytes 786440 | tf_op jit(solution)/shard_map/ppermute | solution.py:28
  16.8 1.2 %collective-permute-start = (s32[2,2]{1,0:T(2,128)S(1)}, s32[2,2]{1,0:T(2,128)S(1)}, u32[]{:S(2)}, u32[]{:S(2)}) collective-permute-start(s32[2,2]{1,0:T(2,128)S(1)} %reshape.18), channel_id=1, source_target_pairs={{1,0},{0,1},{3,2},{2,3},{5,4},{4,5},{7,6},{6,7},{9,8},{8,9},{11,10... | collective-permute-start | bytes 56 | tf_op jit(solution)/shard_map/ppermute | solution.py:28
  17.0 4.3 %collective-permute-start.5 = (bf16[1,2,64,256]{3,2,1,0:T(8,128)(2,1)S(1)}, bf16[1,2,64,256]{3,2,1,0:T(8,128)(2,1)S(1)}, u32[]{:S(2)}, u32[]{:S(2)}) collective-permute-start(bf16[1,2,64,256]{3,2,1,0:T(8,128)(2,1)S(1)} %maximum_bitcast_fusion), channel_id=1, source_target_pairs={{4,0},{5,1},{6,2},{7,3},{0,4},{1,5},{2,6},{3,7},{12,8},{13,9},{14,... | collective-permute-start | bytes 196616 | tf_op jit(solution)/shard_map/ppermute | solution.py:28
  17.9 13.9 %copy-start.11 = (bf16[4,2,64,256]{3,2,1,0:T(8,128)(2,1)}, bf16[4,2,64,256]{3,2,1,0:T(8,128)(2,1)S(1)}, u32[]{:S(2)}) copy-start(bf16[4,2,64,256]{3,2,1,0:T(8,128)(2,1)S(1)} %pad_maximum_fusion.2.refs_8_) | copy-start | bytes 786436
  18.0 5.6 %collective-permute-start.6 = (bf16[1,2,64,256]{3,2,1,0:T(8,128)(2,1)S(1)}, bf16[1,2,64,256]{3,2,1,0:T(8,128)(2,1)S(1)}, u32[]{:S(2)}, u32[]{:S(2)}) collective-permute-start(bf16[1,2,64,256]{3,2,1,0:T(8,128)(2,1)S(1)} %maximum_bitcast_fusion), channel_id=1, source_target_pairs={{8,0},{9,1},{10,2},{11,3},{12,4},{13,5},{14,6},{15,7},{0,8},{1,9},... | collective-permute-start | bytes 196616 | tf_op jit(solution)/shard_map/ppermute | solution.py:28
  21.3 10.4 %collective-permute-start.12 = (bf16[4,2,64,256]{3,2,1,0:T(8,128)(2,1)S(1)}, bf16[4,2,64,256]{3,2,1,0:T(8,128)(2,1)S(1)}, u32[]{:S(2)}, u32[]{:S(2)}) collective-permute-start(bf16[4,2,64,256]{3,2,1,0:T(8,128)(2,1)S(1)} %pad_maximum_fusion.2.refs_8_), channel_id=1, source_target_pairs={{2,0},{3,1},{0,2},{1,3},{6,4},{7,5},{4,6},{5,7},{10,8},{11,9},{8,1... | collective-permute-start | bytes 786440 | tf_op jit(solution)/shard_map/ppermute | solution.py:28
  23.5 6.6 %collective-permute-start.7 = (bf16[1,2,64,256]{3,2,1,0:T(8,128)(2,1)S(1)}, bf16[1,2,64,256]{3,2,1,0:T(8,128)(2,1)S(1)}, u32[]{:S(2)}, u32[]{:S(2)}) collective-permute-start(bf16[1,2,64,256]{3,2,1,0:T(8,128)(2,1)S(1)} %maximum_bitcast_fusion), channel_id=1, source_target_pairs={{12,0},{13,1},{14,2},{15,3},{8,4},{9,5},{10,6},{11,7},{4,8},{5,9},... | collective-permute-start | bytes 196616 | tf_op jit(solution)/shard_map/ppermute | solution.py:28
  30.1 20.0 %copy-start.7 = (bf16[4,2,64,256]{3,2,1,0:T(8,128)(2,1)}, bf16[4,2,64,256]{3,2,1,0:T(8,128)(2,1)S(1)}, u32[]{:S(2)}) copy-start(bf16[4,2,64,256]{3,2,1,0:T(8,128)(2,1)S(1)} %pad_maximum_fusion.1.refs_8_) | copy-start | bytes 786436
  30.2 20.0 %collective-permute-start.8 = (bf16[4,2,64,256]{3,2,1,0:T(8,128)(2,1)S(1)}, bf16[4,2,64,256]{3,2,1,0:T(8,128)(2,1)S(1)}, u32[]{:S(2)}, u32[]{:S(2)}) collective-permute-start(bf16[4,2,64,256]{3,2,1,0:T(8,128)(2,1)S(1)} %pad_maximum_fusion.1.refs_8_), channel_id=1, source_target_pairs={{2,0},{3,1},{0,2},{1,3},{6,4},{7,5},{4,6},{5,7},{10,8},{11,9},{8,1... | collective-permute-start | bytes 786440 | tf_op jit(solution)/shard_map/ppermute | solution.py:28
  31.7 0.7 copy-start.6
  31.8 0.8 copy-start.14
  32.5 1.0 %copy-start.5 = (bf16[2,128,2048]{2,1,0:T(8,128)(2,1)}, bf16[2,128,2048]{2,1,0:T(8,128)(2,1)S(1)}, u32[]{:S(2)}) copy-start(bf16[2,128,2048]{2,1,0:T(8,128)(2,1)S(1)} %collective-permute-done.2.refs_3_) | copy-start | bytes 3145732
  44.4 22.9 %collective-permute-start.15 = (bf16[4,2,64,256]{3,2,1,0:T(8,128)(2,1)}, bf16[4,2,64,256]{3,2,1,0:T(8,128)(2,1)S(1)}, u32[]{:S(2)}, u32[]{:S(2)}) collective-permute-start(bf16[4,2,64,256]{3,2,1,0:T(8,128)(2,1)} %get-tuple-element.24), channel_id=1, source_target_pairs={{2,0},{3,1},{0,2},{1,3},{6,4},{7,5},{4,6},{5,7},{10,8},{11,9},{8,1... | collective-permute-start | bytes 786440 | tf_op jit(solution)/shard_map/ppermute | solution.py:28
  50.1 0.7 copy-start.10
  50.8 16.5 %copy-start.9 = (f32[4,2,64,256]{3,2,1,0:T(8,128)S(1)}, f32[4,2,64,256]{3,2,1,0:T(8,128)}, u32[]{:S(2)}) copy-start(f32[4,2,64,256]{3,2,1,0:T(8,128)} %get-tuple-element.23) | copy-start | bytes 1572868
  62.0 9.9 %copy-start.8 = (f32[4,2,64,256]{3,2,1,0:T(8,128)S(1)}, f32[4,2,64,256]{3,2,1,0:T(8,128)}, u32[]{:S(2)}) copy-start(f32[4,2,64,256]{3,2,1,0:T(8,128)} %get-tuple-element.25) | copy-start | bytes 1572868
  62.1 9.8 %collective-permute-start.19 = (bf16[4,2,64,256]{3,2,1,0:T(8,128)(2,1)}, bf16[4,2,64,256]{3,2,1,0:T(8,128)(2,1)S(1)}, u32[]{:S(2)}, u32[]{:S(2)}) collective-permute-start(bf16[4,2,64,256]{3,2,1,0:T(8,128)(2,1)} %get-tuple-element.26), channel_id=1, source_target_pairs={{2,0},{3,1},{0,2},{1,3},{6,4},{7,5},{4,6},{5,7},{10,8},{11,9},{8,1... | collective-permute-start | bytes 786440 | tf_op jit(solution)/shard_map/ppermute | solution.py:28
  67.4 19.6 %copy-start.4 = (bf16[2,128,1024]{2,1,0:T(8,128)(2,1)S(1)}, bf16[2,128,1024]{2,1,0:T(8,128)(2,1)}, u32[]{:S(2)}) copy-start(bf16[2,128,1024]{2,1,0:T(8,128)(2,1)} %get-tuple-element.21) | copy-start | bytes 1572868
  67.4 5.2 %collective-permute-start.16 = (bf16[2,64,256]{2,1,0:T(8,128)(2,1)S(1)}, bf16[2,64,256]{2,1,0:T(8,128)(2,1)S(1)}, u32[]{:S(2)}, u32[]{:S(2)}) collective-permute-start(bf16[2,64,256]{2,1,0:T(8,128)(2,1)S(1)} %get-tuple-element.35), channel_id=1, source_target_pairs={{4,0},{5,1},{6,2},{7,3},{0,4},{1,5},{2,6},{3,7},{12,8},{13,9},{14,... | collective-permute-start | bytes 196616 | tf_op jit(solution)/shard_map/ppermute | solution.py:28
  67.8 8.7 %collective-permute-start.17 = (bf16[2,64,256]{2,1,0:T(8,128)(2,1)S(1)}, bf16[2,64,256]{2,1,0:T(8,128)(2,1)S(1)}, u32[]{:S(2)}, u32[]{:S(2)}) collective-permute-start(bf16[2,64,256]{2,1,0:T(8,128)(2,1)S(1)} %get-tuple-element.37), channel_id=1, source_target_pairs={{8,0},{9,1},{10,2},{11,3},{12,4},{13,5},{14,6},{15,7},{0,8},{1,9},... | collective-permute-start | bytes 196616 | tf_op jit(solution)/shard_map/ppermute | solution.py:28
  67.8 8.7 %collective-permute-start.18 = (bf16[2,64,256]{2,1,0:T(8,128)(2,1)S(1)}, bf16[2,64,256]{2,1,0:T(8,128)(2,1)S(1)}, u32[]{:S(2)}, u32[]{:S(2)}) collective-permute-start(bf16[2,64,256]{2,1,0:T(8,128)(2,1)S(1)} %get-tuple-element.36), channel_id=1, source_target_pairs={{12,0},{13,1},{14,2},{15,3},{8,4},{9,5},{10,6},{11,7},{4,8},{5,9},... | collective-permute-start | bytes 196616 | tf_op jit(solution)/shard_map/ppermute | solution.py:28
  72.0 5.8 %collective-permute-start.20 = (bf16[2,64,256]{2,1,0:T(8,128)(2,1)S(1)}, bf16[2,64,256]{2,1,0:T(8,128)(2,1)S(1)}, u32[]{:S(2)}, u32[]{:S(2)}) collective-permute-start(bf16[2,64,256]{2,1,0:T(8,128)(2,1)S(1)} %get-tuple-element.38), channel_id=1, source_target_pairs={{4,0},{5,1},{6,2},{7,3},{0,4},{1,5},{2,6},{3,7},{12,8},{13,9},{14,... | collective-permute-start | bytes 196616 | tf_op jit(solution)/shard_map/ppermute | solution.py:28
  72.3 7.6 %collective-permute-start.21 = (bf16[2,64,256]{2,1,0:T(8,128)(2,1)S(1)}, bf16[2,64,256]{2,1,0:T(8,128)(2,1)S(1)}, u32[]{:S(2)}, u32[]{:S(2)}) collective-permute-start(bf16[2,64,256]{2,1,0:T(8,128)(2,1)S(1)} %get-tuple-element.40), channel_id=1, source_target_pairs={{8,0},{9,1},{10,2},{11,3},{12,4},{13,5},{14,6},{15,7},{0,8},{1,9},... | collective-permute-start | bytes 196616 | tf_op jit(solution)/shard_map/ppermute | solution.py:28
  72.6 7.3 %collective-permute-start.22 = (bf16[2,64,256]{2,1,0:T(8,128)(2,1)S(1)}, bf16[2,64,256]{2,1,0:T(8,128)(2,1)S(1)}, u32[]{:S(2)}, u32[]{:S(2)}) collective-permute-start(bf16[2,64,256]{2,1,0:T(8,128)(2,1)S(1)} %get-tuple-element.39), channel_id=1, source_target_pairs={{12,0},{13,1},{14,2},{15,3},{8,4},{9,5},{10,6},{11,7},{4,8},{5,9},... | collective-permute-start | bytes 196616 | tf_op jit(solution)/shard_map/ppermute | solution.py:28
  76.5 12.0 %copy-start.2 = (bf16[2,128,4096]{2,1,0:T(8,128)(2,1)S(1)}, bf16[2,128,4096]{2,1,0:T(8,128)(2,1)}, u32[]{:S(2)}) copy-start(bf16[2,128,4096]{2,1,0:T(8,128)(2,1)} %get-tuple-element.19) | copy-start | bytes 6291460
  80.0 6.9 %collective-permute-start.23 = (bf16[2,64,512]{2,1,0:T(8,128)(2,1)S(1)}, bf16[2,64,512]{2,1,0:T(8,128)(2,1)S(1)}, u32[]{:S(2)}, u32[]{:S(2)}) collective-permute-start(bf16[2,64,512]{2,1,0:T(8,128)(2,1)S(1)} %pad_maximum_fusion.3), channel_id=1, source_target_pairs={{16,0},{0,16},{17,1},{1,17},{18,2},{2,18},{19,3},{3,19},{20,4},{4,... | collective-permute-start | bytes 393224 | tf_op jit(solution)/shard_map/ppermute | solution.py:28
  83.9 3.1 %collective-permute-start.14 = (bf16[2,128,1024]{2,1,0:T(8,128)(2,1)}, bf16[2,128,1024]{2,1,0:T(8,128)(2,1)S(1)}, u32[]{:S(2)}, u32[]{:S(2)}) collective-permute-start(bf16[2,128,1024]{2,1,0:T(8,128)(2,1)} %get-tuple-element.22), channel_id=1, source_target_pairs={{1,0},{0,1},{3,2},{2,3},{5,4},{4,5},{7,6},{6,7},{9,8},{8,9},{11,10... | collective-permute-start | bytes 1572872 | tf_op jit(solution)/shard_map/ppermute | solution.py:28
  84.0 4.6 %collective-permute-start.13 = (bf16[2,128,2048]{2,1,0:T(8,128)(2,1)}, bf16[2,128,2048]{2,1,0:T(8,128)(2,1)S(1)}, u32[]{:S(2)}, u32[]{:S(2)}) collective-permute-start(bf16[2,128,2048]{2,1,0:T(8,128)(2,1)} %get-tuple-element.20), channel_id=1, source_target_pairs={{1,0},{0,1},{3,2},{2,3},{5,4},{4,5},{7,6},{6,7},{9,8},{8,9},{11,10... | collective-permute-start | bytes 3145736 | tf_op jit(solution)/shard_map/ppermute | solution.py:28
  86.9 1.4 %collective-permute-start.24 = (f32[64,512]{1,0:T(8,128)S(1)}, f32[64,512]{1,0:T(8,128)S(1)}, u32[]{:S(2)}, u32[]{:S(2)}) collective-permute-start(f32[64,512]{1,0:T(8,128)S(1)} %get-tuple-element.34), channel_id=1, source_target_pairs={{1,0},{0,1},{3,2},{2,3},{5,4},{4,5},{7,6},{6,7},{9,8},{8,9},{11,10... | collective-permute-start | bytes 393224 | tf_op jit(solution)/shard_map/ppermute | solution.py:28
  88.5 0.7 copy-start.13
  89.2 1.3 %copy-start.3 = (bf16[2,128,4096]{2,1,0:T(8,128)(2,1)}, bf16[2,128,4096]{2,1,0:T(8,128)(2,1)S(1)}, u32[]{:S(2)}) copy-start(bf16[2,128,4096]{2,1,0:T(8,128)(2,1)S(1)} %constant_dynamic-update-slice_fusion) | copy-start | bytes 6291460

commit v3 on v2

v3 whole, which is shorter than its diff:
```python
import functools
import math

import jax
import jax.numpy as jnp
from jax import lax
from jax.experimental import pallas as pl
from jax.experimental.pallas import tpu as pltpu
from jax.sharding import PartitionSpec as P


H = 32
KVH = 4
DH = 128
SEGS = 4
GROUPS = H // KVH
CORES = 2
HEADS = KVH // CORES
CHUNK = 32
NT = (((1,), (1,)), ((), ()))
NN = (((1,), (0,)), ((), ()))
F32 = jnp.float32
BF16 = jnp.bfloat16


def swapped(block, axis, bit):
    route = [(i ^ bit, i) for i in range(lax.axis_size(axis))]
    return lax.ppermute(block, axis, route)


def dot(a, b, dims):
    return lax.dot_general(a, b, dims, preferred_element_type=F32)


def head_kernel(head, offsets, info, *refs):
    ins, refs = refs[:8], refs[-24:]
    q_own, q_far, g_own, g_far, b_own, b_far, kv_near, kv_next = ins
    dq_own, dq_far, db_own, db_far, keep, send = refs[:6]
    keys, values, keys_t, bkeys, bvalues, bkeys_t, s_scr, dp_scr = refs[6:14]
    dk_acc, dv_acc, dbk_acc, dbv_acc, q_buf, g_buf, dq_buf, db_buf = refs[14:22]
    in_sem, kv_sem = refs[22:]
    tiles, rows, _ = q_own.shape
    me = info[1]
    rr = kv_near.shape[2]
    roots = keys.shape[0]
    width = roots // SEGS
    qw = GROUPS * DH
    scale = DH ** (-0.5)
    sharp = scale * math.log2(math.e)
    at_own = pl.multiple_of((info[0] * HEADS + head) * qw, qw)
    k_own = pl.multiple_of((info[0] * HEADS + head) * DH, DH)

    def places():
        n = 0
        for side in range(2):
            for j, off in enumerate(offsets):
                for b0 in range(CORES):
                    rel = b0 + side * CORES + off
                    yield n, side, j, b0, pl.multiple_of((me ^ rel) * rr, rr)
                    n += 1

    def kv_copies():
        for n, side, j, b0, at in places():
            block = (kv_near, kv_next)[side].at[j, b0]
            for i, ref in enumerate((keys, values)):
                yield pltpu.make_async_copy(
                    block.at[:, pl.ds(i * DH, DH)], ref.at[pl.ds(at, rr)], kv_sem.at[n, i]
                )

    def tile_copies(t, out):
        if t < tiles:
            wide, narrow, at = pl.ds(at_own, qw), pl.ds(k_own, DH), t
            q_ref, g_ref, b_ref, dq_ref, db_ref = q_own, g_own, b_own, dq_own, db_own
            v_at = k_own + KVH * DH
        else:
            wide, narrow, at = pl.ds(head * qw, qw), pl.ds(head * DH, DH), t - tiles
            q_ref, g_ref, b_ref, dq_ref, db_ref = q_far, g_far, b_far, dq_far, db_far
            v_at = (HEADS + head) * DH
        v_narrow = pl.ds(v_at, DH)
        reads = (
            (q_ref.at[at, :, wide], q_buf.at[t]),
            (g_ref.at[at, :, wide], g_buf.at[t]),
            (b_ref.at[at, :, narrow], bkeys.at[t]),
            (b_ref.at[at, :, v_narrow], bvalues.at[t]),
        )
        writes = (
            (dq_buf.at[t], dq_ref.at[at, :, wide]),
            (db_buf.at[t, 0], db_ref.at[at, :, narrow]),
            (db_buf.at[t, 1], db_ref.at[at, :, v_narrow]),
        )
        picked = writes if out else reads
        return [
            pltpu.make_async_copy(src, dst, in_sem.at[t, i + (len(reads) if out else 0)])
            for i, (src, dst) in enumerate(picked)
        ]

    for copy in kv_copies():
        copy.start()
    for t in range(2 * tiles):

        @pl.when(info[2 + t] > 0)
        def _():
            for copy in tile_copies(t, False):
                copy.start()

    dk_acc[...] = jnp.zeros_like(dk_acc)
    dv_acc[...] = jnp.zeros_like(dv_acc)
    for copy in kv_copies():
        copy.wait()
    for b in range(0, roots, DH):
        keys_t[:, b : b + DH] = keys[b : b + DH, :].T

    def fold(x, op):
        return op(x.reshape(x.shape[0] // 8, 8, x.shape[1]), axis=0)

    def tile(t, carry):
        length = info[2 + t]
        segment = info[2 + 2 * tiles + t]

        dbk_acc[...] = jnp.zeros_like(dbk_acc)
        dbv_acc[...] = jnp.zeros_like(dbv_acc)

        for at in range(2 * tiles):

            @pl.when((t == at) & (length > 0))
            def _():
                for copy in tile_copies(at, False):
                    copy.wait()

        bkeys_t[...] = bkeys[t].T

        def piece(r0, size, segs):
            qrows = GROUPS * size
            lanes = slice(0, qrows)

            def stacked(ref):
                x = ref[t, pl.ds(r0, size), :]
                return jnp.concatenate([x[:, j * DH : (j + 1) * DH] for j in range(GROUPS)], axis=0)

            q = stacked(q_buf)
            g = stacked(g_buf)
            row = lax.broadcasted_iota(jnp.int32, (qrows, DH), 0) % size + r0
            g = jnp.where(row < length, g.astype(F32), 0.0).astype(BF16)

            spans = [(b * width, width) for b in range(segs)] + [(roots, rows)]
            ats = [slice(lo, lo + n) for lo, n in spans]

            def k_of(b):
                return keys[ats[b], :] if b < segs else bkeys[t]

            def v_of(b):
                return values[ats[b], :] if b < segs else bvalues[t]

            def kt_of(b):
                return keys_t[:, ats[b]] if b < segs else bkeys_t[...]

            top = None
            for b in range(segs + 1):
                s = dot(k_of(b), q, NT)
                if b == segs:
                    key = lax.broadcasted_iota(jnp.int32, s.shape, 0)
                    pos = lax.broadcasted_iota(jnp.int32, s.shape, 1) % size + r0
                    s = jnp.where(key <= pos, s, F32(-1e30))
                s_scr[ats[b], lanes] = s
                part = fold(s, jnp.max)
                top = part if top is None else jnp.maximum(top, part)
            peak = jnp.max(top, axis=0, keepdims=True)

            total = jnp.zeros((8, qrows), F32)
            for b in range(segs + 1):
                dp_scr[ats[b], lanes] = dot(v_of(b), g, NT)
                e = jnp.exp2((s_scr[ats[b], lanes] - peak) * sharp)
                s_scr[ats[b], lanes] = e
                total = total + fold(e, jnp.sum)
            inv = 1.0 / jnp.sum(total, axis=0, keepdims=True)

            delta = jnp.zeros((8, qrows), F32)
            for b in range(segs + 1):
                probs = (s_scr[ats[b], lanes] * inv).astype(BF16)
                delta = delta + fold(probs.astype(F32) * dp_scr[ats[b], lanes], jnp.sum)
                dv = dot(probs, g, NN)
                if b < segs:
                    dv_acc[ats[b], :] += dv
                else:
                    dbv_acc[...] += dv
            delta = jnp.sum(delta, axis=0, keepdims=True)
            invs = inv * scale

            dq_t = jnp.zeros((DH, qrows), F32)
            for b in range(segs + 1):
                ds = ((s_scr[ats[b], lanes] * invs) * (dp_scr[ats[b], lanes] - delta)).astype(BF16)
                dk = dot(ds, q, NN)
                if b < segs:
                    dk_acc[ats[b], :] += dk
                else:
                    dbk_acc[...] += dk
                dq_t = dq_t + dot(kt_of(b), ds, NN)
            dq = dq_t.T.astype(BF16)
            for j in range(GROUPS):
                dq_buf[t, pl.ds(r0, size), j * DH : (j + 1) * DH] = dq[j * size : (j + 1) * size, :]

        count = (length + (CHUNK - 1)) // CHUNK
        for s in range(SEGS):

            @pl.when(segment == s)
            def _():
                def step(c, carry):
                    piece(pl.multiple_of(c * (2 * CHUNK), 2 * CHUNK), 2 * CHUNK, s + 1)
                    return carry

                lax.fori_loop(0, count // 2, step, 0)

                @pl.when(count % 2 == 1)
                def _():
                    piece(pl.multiple_of((count - 1) * CHUNK, CHUNK), CHUNK, s + 1)

        def clear(c, carry):
            at = pl.multiple_of(c * CHUNK, CHUNK)
            dq_buf[t, pl.ds(at, CHUNK), :] = jnp.zeros((CHUNK, qw), BF16)
            return carry

        lax.fori_loop(count, rows // CHUNK, clear, 0)
        db_buf[t, 0] = dbk_acc[...].astype(BF16)
        db_buf[t, 1] = dbv_acc[...].astype(BF16)
        for at in range(2 * tiles):

            @pl.when(t == at)
            def _():
                for copy in tile_copies(at, True):
                    copy.start()

        return carry

    lax.fori_loop(0, 2 * tiles, tile, 0)

    for _, side, j, b0, at in places():
        out = (keep, send)[side]
        out[j, b0, :, :DH] = dk_acc[pl.ds(at, rr), :].astype(out.dtype)
        out[j, b0, :, DH:] = dv_acc[pl.ds(at, rr), :].astype(out.dtype)
    for t in range(2 * tiles):
        for copy in tile_copies(t, True):
            copy.wait()


def head_grads(head, offsets, info, q, q_far, g, g_far, b, b_far, near, nxt, earlier):
    tiles, rows, _ = q.shape
    half = near.shape[0]
    rr = near.shape[2]
    roots = 2 * half * CORES * rr
    qw = GROUPS * DH
    span = roots + rows
    vmem = pl.BlockSpec(memory_space=pltpu.VMEM)
    hbm = pl.BlockSpec(memory_space=pltpu.HBM)
    args = [q, q_far, g, g_far, b, b_far, near, nxt]
    in_specs = [pl.BlockSpec(memory_space=pltpu.SMEM)] + [hbm] * len(args)
    aliases = {}
    if earlier is not None:
        in_specs += [hbm] * 4
        aliases = {1 + len(args) + i: i for i in range(4)}
        args += earlier
    out_shape = [
        jax.ShapeDtypeStruct(q.shape, BF16),
        jax.ShapeDtypeStruct((tiles, rows, HEADS * qw), BF16),
        jax.ShapeDtypeStruct(b.shape, BF16),
        jax.ShapeDtypeStruct(b_far.shape, BF16),
        jax.ShapeDtypeStruct(near.shape, F32),
        jax.ShapeDtypeStruct(near.shape, BF16),
    ]
    scratch = [
        pltpu.VMEM((roots, DH), BF16),
        pltpu.VMEM((roots, DH), BF16),
        pltpu.VMEM((DH, roots), BF16),
        pltpu.VMEM((2 * tiles, rows, DH), BF16),
        pltpu.VMEM((2 * tiles, rows, DH), BF16),
        pltpu.VMEM((DH, rows), BF16),
        pltpu.VMEM((span, 2 * CHUNK * GROUPS), F32),
        pltpu.VMEM((span, 2 * CHUNK * GROUPS), F32),
        pltpu.VMEM((roots, DH), F32),
        pltpu.VMEM((roots, DH), F32),
        pltpu.VMEM((rows, DH), F32),
        pltpu.VMEM((rows, DH), F32),
        pltpu.VMEM((2 * tiles, rows, qw), BF16),
        pltpu.VMEM((2 * tiles, rows, qw), BF16),
        pltpu.VMEM((2 * tiles, rows, qw), BF16),
        pltpu.VMEM((2 * tiles, 2, rows, DH), BF16),
        pltpu.SemaphoreType.DMA((2 * tiles, 7)),
        pltpu.SemaphoreType.DMA((2 * half * CORES, 2)),
    ]
    flops = 2 * 5 * tiles * rows * GROUPS * span * DH
    outs = pl.pallas_call(
        functools.partial(head_kernel, head, offsets),
        in_specs=in_specs,
        out_specs=[hbm] * 4 + [vmem] * 2,
        scratch_shapes=scratch,
        out_shape=out_shape,
        input_output_aliases=aliases,
        cost_estimate=pl.CostEstimate(
            flops=flops, bytes_accessed=8 * tiles * rows * qw, transcendentals=0
        ),
        compiler_params=pltpu.CompilerParams(vmem_limit_bytes=32 * 2**20),
    )(info, *args)
    return list(outs[:4]), outs[4], outs[5]


def local(query, grad_out, branch_kv, root_kv, lengths, segments):
    n_dev = lax.axis_size("dev")
    n_grp = lax.axis_size("grp")
    me = lax.axis_index("dev")
    core = me % CORES
    tiles, _, qcols = query.shape
    kcols = root_kv.shape[1] // 2
    offsets = tuple(range(0, n_dev, 2 * CORES))

    def cols(x, which, parts):
        part = x.shape[-1] // parts
        wide = part // CORES
        axis = x.ndim - 1
        pieces = [
            lax.dynamic_slice_in_dim(x, p * part + which * wide, wide, axis) for p in range(parts)
        ]
        return pieces

    mine = cols(root_kv, core, 2)
    other = jnp.concatenate(cols(root_kv, 1 - core, 2), axis=1)
    got = swapped(other, "dev", 1)
    got = [got[:, : kcols // CORES], got[:, kcols // CORES :]]
    gathered = []
    for head in range(HEADS):
        at = slice(head * DH, (head + 1) * DH)
        x = jnp.stack(
            [
                jnp.concatenate([mine[0][:, at], mine[1][:, at]], axis=1),
                jnp.concatenate([got[0][:, at], got[1][:, at]], axis=1),
            ]
        )[None]
        arrived = [swapped(x, "dev", off) for off in offsets[1:]]
        x = jnp.concatenate([x] + arrived, axis=0)
        nxt = swapped(x, "dev", CORES)
        gathered.append((x, nxt))

    q_far = swapped(cols(query, 1 - core, 1)[0], "dev", 1)
    g_far = swapped(cols(grad_out, 1 - core, 1)[0], "dev", 1)
    b_far = swapped(jnp.concatenate(cols(branch_kv, 1 - core, 2), axis=2), "dev", 1)
    meta = jnp.concatenate([lengths, segments]).reshape(2, tiles)
    meta_far = swapped(meta, "dev", 1)
    info = jnp.concatenate(
        [jnp.stack([core, me]), jnp.concatenate([meta, meta_far], axis=1).reshape(-1)]
    )

    outs = None
    sums = []
    for head in range(HEADS):
        near, nxt = gathered[head]
        outs, keep, send = head_grads(
            head, offsets, info, query, q_far, grad_out, g_far, branch_kv, b_far, near, nxt, outs
        )
        back = swapped(send, "dev", CORES)
        x = keep + back
        arrived = [swapped(x[j].astype(BF16), "dev", offsets[j]) for j in range(1, len(offsets))]
        x = x[0]
        for part in arrived:
            x = x + part
        sums.append(x)
    x = jnp.concatenate(sums, axis=2)
    hop = 1
    while hop < n_grp:
        x = x.astype(BF16)
        back = swapped(x, "grp", hop)
        x = x.astype(F32) + back.astype(F32)
        hop *= 2
    far = swapped(x[1], "dev", 1)
    near = x[0]
    pieces = []
    for part in range(2):
        for side in range(CORES):
            for head in range(HEADS):
                at = (head * 2 + part) * DH
                pieces.append(
                    jnp.where(core == side, near[:, at : at + DH], far[:, at : at + DH])
                )
    root_grad = jnp.concatenate(pieces, axis=1)

    dq, dq_far, db, db_far = outs
    dq_got = swapped(dq_far, "dev", 1)
    db_got = swapped(db_far, "dev", 1)
    query_grad = lax.dynamic_update_slice_in_dim(dq, dq_got, (1 - core) * (qcols // CORES), 2)
    wide = HEADS * DH
    branch_grad = db
    for part in range(2):
        branch_grad = lax.dynamic_update_slice_in_dim(
            branch_grad,
            db_got[:, :, part * wide : (part + 1) * wide],
            (part * CORES + 1 - core) * wide,
            2,
        )
    return (query_grad, branch_grad, root_grad)


def solution(mesh):
    placed = (
        P(("grp", "dev"), None, None),
        P(("grp", "dev"), None, None),
        P(("grp", "dev"), None, None),
        P("dev", None),
        P(("grp", "dev")),
        P(("grp", "dev")),
    )

    return jax.shard_map(
        local,
        mesh=mesh,
        in_specs=placed,
        out_specs=(P(("grp", "dev"), None, None), P(("grp", "dev"), None, None), P("dev", None)),
        check_vma=False,
    )
```

time: 90.8 us -> 83.9 us (0.924)
  waiting for transfers between devices: 13.8 us -> 25 us
  starting transfers between devices: 42.1 us -> 31.1 us
  Pallas kernels: 22.1 us -> 14.9 us
    ppermute x25, waiting for transfers between devices: 13.8 us -> 25 us  [swapped(): return lax.ppermute(block, axis, route)]
    ppermute x25, starting transfers between devices: 42.1 us -> 31.1 us  [swapped(): return lax.ppermute(block, axis, route)]
    pallas_call x2, Pallas kernels: 22.1 us -> 14.9 us  [head_grads(): pl.pallas_call(functools.partial(head_kernel, head, offsets), in_specs=in...]
    dynamic_update_slice x0 -> x2, local copies, waits for them, and re-layouts: none -> 1.33 us  [local(): lax.dynamic_update_slice_in_dim(branch_grad, db_got[:, :, part * wide:(pa...]
    select_n x1 -> x0, other arithmetic: 1.08 us -> none  [local(): branch_grad = jnp.where(col // (HEADS * DH) % CORES == core, db, db_got)]
    unnamed x34 -> x20, local copies, waits for them, and re-layouts: 4.31 us -> 3.47 us
  transfers between devices with their start and end apart: 25 -> 25, of which waited for: 10 -> 13; matrix products, arithmetic and copies ran while one was open for 7% -> 9% of each run, Pallas kernels for 24% -> 18%
where the time goes in v3:
time: 83.9 us; the launch traced here: 83.7 us
  starting transfers between devices  31.1 us (37%)
  waiting for transfers between devices  25 us (30%)
  Pallas kernels  14.9 us (18%)
  local copies, waits for them, and re-layouts  9.5 us (11%)
  other arithmetic  2.24 us (3%)
  between operations  0.98 us (1%)
    ppermute x25, starting transfers between devices, swapped(): return lax.ppermute(block, axis, route)  31.1 us
    ppermute x25, waiting for transfers between devices, swapped(): return lax.ppermute(block, axis, route)  25 us
    pallas_call x2, Pallas kernels, head_grads(): pl.pallas_call(functools.partial(head_kernel, head, offsets), in_specs=in...  14.9 us
    dynamic_slice x4, local copies, waits for them, and re-layouts, cols(): lax.dynamic_slice_in_dim(x, p * part + which * wide, wide, axis)  4.32 us
    unnamed x20, local copies, waits for them, and re-layouts  3.47 us
  transfers between devices with their start and end apart: 25, of which 13 were waited for; matrix products, arithmetic and copies ran while one was open for 9% of the time, Pallas kernels for 18%

profile of v3, /device:TPU:0, one launch (start us, length us, event | category | flops | bytes accessed | tf_op | source)
XLA Modules:
  0.0 83.7 jit_solution(7027623952871267869)
XLA Ops:
  0.6 0.8 constant_dynamic-slice_fusion.3
  1.4 0.6 collective-permute-start.4
  2.0 2.5 %constant_dynamic-slice_fusion.9 = bf16[2,128,2048]{2,1,0:T(8,128)(2,1)} fusion(bf16[2,128,4096]{2,1,0:T(8,128)(2,1)} %refs_0_.3, s32[]{:T(128)S(6)} %select_n.69), kind=kLoop, calls=%fused_computation.52 | loop fusion | bytes 2097156 | tf_op jit(solution)/shard_map/dynamic_slice | solution.py:319
  4.5 1.0 %constant_dynamic-slice_fusion.8 = bf16[2,128,2048]{2,1,0:T(8,128)(2,1)} fusion(bf16[2,128,4096]{2,1,0:T(8,128)(2,1)S(1)} %copy-done.1, s32[]{:T(128)S(6)} %select_n.69), kind=kLoop, calls=%fused_computation.51 | loop fusion | bytes 2097156 | tf_op jit(solution)/shard_map/dynamic_slice | solution.py:319
  5.6 0.5 collective-permute-start.2
  6.1 0.1 pad_add_fusion.1
  6.2 0.1 reshape.18
  6.2 0.7 pad_maximum_fusion
  7.1 3.7 %collective-permute-start.10 = (bf16[1,2,64,256]{3,2,1,0:T(8,128)(2,1)S(1)}, bf16[1,2,64,256]{3,2,1,0:T(8,128)(2,1)S(1)}, u32[]{:S(2)}, u32[]{:S(2)}) collective-permute-start(bf16[1,2,64,256]{3,2,1,0:T(8,128)(2,1)S(1)} %maximum_bitcast_fusion.1), channel_id=1, source_target_pairs={{8,0},{9,1},{10,2},{11,3},{12,4},{13,5},{14,6},{15,7},{0,8},{1,9},... | collective-permute-start | bytes 196616 | tf_op jit(solution)/shard_map/ppermute | solution.py:28
  10.8 1.3 %collective-permute-start.11 = (bf16[1,2,64,256]{3,2,1,0:T(8,128)(2,1)S(1)}, bf16[1,2,64,256]{3,2,1,0:T(8,128)(2,1)S(1)}, u32[]{:S(2)}, u32[]{:S(2)}) collective-permute-start(bf16[1,2,64,256]{3,2,1,0:T(8,128)(2,1)S(1)} %maximum_bitcast_fusion.1), channel_id=1, source_target_pairs={{12,0},{13,1},{14,2},{15,3},{8,4},{9,5},{10,6},{11,7},{4,8},{5,9},... | collective-permute-start | bytes 196616 | tf_op jit(solution)/shard_map/ppermute | solution.py:28
  12.1 0.2 collective-permute-start.9
  12.4 2.7 %collective-permute-done.10 = bf16[1,2,64,256]{3,2,1,0:T(8,128)(2,1)S(1)} collective-permute-done((bf16[1,2,64,256]{3,2,1,0:T(8,128)(2,1)S(1)}, bf16[1,2,64,256]{3,2,1,0:T(8,128)(2,1)S(1)}, u32[]{:S(2)}, u32[]{:S(2)}) %collective-permute-start.10) | collective-permute-done | bytes 65568 | tf_op jit(solution)/shard_map/ppermute | solution.py:28
  15.1 2.3 %collective-permute-done.11 = bf16[1,2,64,256]{3,2,1,0:T(8,128)(2,1)S(1)} collective-permute-done((bf16[1,2,64,256]{3,2,1,0:T(8,128)(2,1)S(1)}, bf16[1,2,64,256]{3,2,1,0:T(8,128)(2,1)S(1)}, u32[]{:S(2)}, u32[]{:S(2)}) %collective-permute-start.11) | collective-permute-done | bytes 65568 | tf_op jit(solution)/shard_map/ppermute | solution.py:28
  17.4 0.2 collective-permute-done.9
  17.7 0.9 %collective-permute-start.5 = (bf16[1,2,64,256]{3,2,1,0:T(8,128)(2,1)S(1)}, bf16[1,2,64,256]{3,2,1,0:T(8,128)(2,1)S(1)}, u32[]{:S(2)}, u32[]{:S(2)}) collective-permute-start(bf16[1,2,64,256]{3,2,1,0:T(8,128)(2,1)S(1)} %maximum_bitcast_fusion), channel_id=1, source_target_pairs={{4,0},{5,1},{6,2},{7,3},{0,4},{1,5},{2,6},{3,7},{12,8},{13,9},{14,... | collective-permute-start | bytes 196616 | tf_op jit(solution)/shard_map/ppermute | solution.py:28
  18.6 3.1 %collective-permute-start.6 = (bf16[1,2,64,256]{3,2,1,0:T(8,128)(2,1)S(1)}, bf16[1,2,64,256]{3,2,1,0:T(8,128)(2,1)}, u32[]{:S(2)}, u32[]{:S(2)}) collective-permute-start(bf16[1,2,64,256]{3,2,1,0:T(8,128)(2,1)S(1)} %maximum_bitcast_fusion), channel_id=1, source_target_pairs={{8,0},{9,1},{10,2},{11,3},{12,4},{13,5},{14,6},{15,7},{0,8},{1,9},... | collective-permute-start | bytes 196616 | tf_op jit(solution)/shard_map/ppermute | solution.py:28
  21.7 0.2 collective-permute-done.5
  21.9 1.6 %collective-permute-start.12 = (bf16[4,2,64,256]{3,2,1,0:T(8,128)(2,1)S(1)}, bf16[4,2,64,256]{3,2,1,0:T(8,128)(2,1)S(1)}, u32[]{:S(2)}, u32[]{:S(2)}) collective-permute-start(bf16[4,2,64,256]{3,2,1,0:T(8,128)(2,1)S(1)} %pad_maximum_fusion.2.refs_6_), channel_id=1, source_target_pairs={{2,0},{3,1},{0,2},{1,3},{6,4},{7,5},{4,6},{5,7},{10,8},{11,9},{8,1... | collective-permute-start | bytes 786440 | tf_op jit(solution)/shard_map/ppermute | solution.py:28
  23.6 0.1 reshape.19
  23.7 0.6 collective-permute-done.6
  24.2 4.3 %collective-permute-start.7 = (bf16[1,2,64,256]{3,2,1,0:T(8,128)(2,1)S(1)}, bf16[1,2,64,256]{3,2,1,0:T(8,128)(2,1)S(1)}, u32[]{:S(2)}, u32[]{:S(2)}) collective-permute-start(bf16[1,2,64,256]{3,2,1,0:T(8,128)(2,1)S(1)} %maximum_bitcast_fusion), channel_id=1, source_target_pairs={{12,0},{13,1},{14,2},{15,3},{8,4},{9,5},{10,6},{11,7},{4,8},{5,9},... | collective-permute-start | bytes 196616 | tf_op jit(solution)/shard_map/ppermute | solution.py:28
  28.6 0.1 pad_add_fusion.2.info
  28.7 2.2 %collective-permute-done.7 = bf16[1,2,64,256]{3,2,1,0:T(8,128)(2,1)S(1)} collective-permute-done((bf16[1,2,64,256]{3,2,1,0:T(8,128)(2,1)S(1)}, bf16[1,2,64,256]{3,2,1,0:T(8,128)(2,1)S(1)}, u32[]{:S(2)}, u32[]{:S(2)}) %collective-permute-start.7) | collective-permute-done | bytes 65568 | tf_op jit(solution)/shard_map/ppermute | solution.py:28
  30.8 0.9 %pad_maximum_fusion.1.refs_6_ = bf16[4,2,64,256]{3,2,1,0:T(8,128)(2,1)S(1)} fusion(bf16[1,2,64,256]{3,2,1,0:T(8,128)(2,1)S(1)} %collective-permute-done.7, bf16[1,2,64,256]{3,2,1,0:T(8,128)(2,1)} %collective-permute-done.6, bf16[1,2,64,256]{3,2,1,0:T(8,128)(2,1)S(1)} %collective-permute-done.5, bf16[1,2,64,256]{3,2,1,0:T(8,128)(2,1)S(1)} %maximum_bitcast_fusion), kind=kLoop, calls=%fused_computation.3 | loop fusion | flops 393216 | bytes 524288 | tf_op jit(solution)/shard_map/concatenate | solution.py:337
  31.7 1.6 %collective-permute-start.8 = (bf16[4,2,64,256]{3,2,1,0:T(8,128)(2,1)S(1)}, bf16[4,2,64,256]{3,2,1,0:T(8,128)(2,1)S(1)}, u32[]{:S(2)}, u32[]{:S(2)}) collective-permute-start(bf16[4,2,64,256]{3,2,1,0:T(8,128)(2,1)S(1)} %pad_maximum_fusion.1.refs_6_), channel_id=1, source_target_pairs={{2,0},{3,1},{0,2},{1,3},{6,4},{7,5},{4,6},{5,7},{10,8},{11,9},{8,1... | collective-permute-start | bytes 786440 | tf_op jit(solution)/shard_map/ppermute | solution.py:28
  33.3 1.6 %copy-done.2 = bf16[2,128,4096]{2,1,0:T(8,128)(2,1)S(1)} copy-done((bf16[2,128,4096]{2,1,0:T(8,128)(2,1)S(1)}, bf16[2,128,4096]{2,1,0:T(8,128)(2,1)}, u32[]{:S(2)}) %copy-start.2) | copy-done | bytes 2097176
  34.9 7.4 %shard_map.85 = (bf16[2,128,4096]{2,1,0:T(8,128)(2,1)}, bf16[2,128,2048]{2,1,0:T(8,128)(2,1)S(1)}, bf16[2,128,1024]{2,1,0:T(8,128)(2,1)}, bf16[2,128,512]{2,1,0:...) custom-call(s32[10]{0:T(128)S(1)} %pad_add_fusion.2.info, ...), custom_call_target="tpu_custom_call" | custom-call | flops 3019898880 | bytes 2097152 | tf_op jit(solution)/shard_map/pallas_call | solution.py:290
  42.3 4.2 %collective-permute-start.15 = (bf16[4,2,64,256]{3,2,1,0:T(8,128)(2,1)S(1)}, bf16[4,2,64,256]{3,2,1,0:T(8,128)(2,1)S(1)}, u32[]{:S(2)}, u32[]{:S(2)}) collective-permute-start(bf16[4,2,64,256]{3,2,1,0:T(8,128)(2,1)S(1)} %get-tuple-element.24), channel_id=1, source_target_pairs={{2,0},{3,1},{0,2},{1,3},{6,4},{7,5},{4,6},{5,7},{10,8},{11,9},{8,1... | collective-permute-start | bytes 786440 | tf_op jit(solution)/shard_map/ppermute | solution.py:28
  46.5 7.5 %shard_map.86 = (bf16[2,128,4096]{2,1,0:T(8,128)(2,1)}, bf16[2,128,2048]{2,1,0:T(8,128)(2,1)S(1)}, bf16[2,128,1024]{2,1,0:T(8,128)(2,1)}, bf16[2,128,512]{2,1,0:...) custom-call(s32[10]{0:T(128)S(1)} %pad_add_fusion.2.info, ...), custom_call_target="tpu_custom_call", output_to_operand_aliasing={{0}: (9, {}), {1}: (10, {}), {2}: (11, {}), {3}: (12, {})} | custom-call | flops 3019898880 | bytes 2097152 | tf_op jit(solution)/shard_map/pallas_call | solution.py:290
  54.1 3.7 %collective-permute-start.19 = (bf16[4,2,64,256]{3,2,1,0:T(8,128)(2,1)S(1)}, bf16[4,2,64,256]{3,2,1,0:T(8,128)(2,1)S(1)}, u32[]{:S(2)}, u32[]{:S(2)}) collective-permute-start(bf16[4,2,64,256]{3,2,1,0:T(8,128)(2,1)S(1)} %get-tuple-element.26), channel_id=1, source_target_pairs={{2,0},{3,1},{0,2},{1,3},{6,4},{7,5},{4,6},{5,7},{10,8},{11,9},{8,1... | collective-permute-start | bytes 786440 | tf_op jit(solution)/shard_map/ppermute | solution.py:28
  57.8 0.5 collective-permute-start.13
  58.4 1.2 %collective-permute-start.16 = (bf16[2,64,256]{2,1,0:T(8,128)(2,1)S(1)}, bf16[2,64,256]{2,1,0:T(8,128)(2,1)S(1)}, u32[]{:S(2)}, u32[]{:S(2)}) collective-permute-start(bf16[2,64,256]{2,1,0:T(8,128)(2,1)S(1)} %get-tuple-element.35), channel_id=1, source_target_pairs={{4,0},{5,1},{6,2},{7,3},{0,4},{1,5},{2,6},{3,7},{12,8},{13,9},{14,... | collective-permute-start | bytes 196616 | tf_op jit(solution)/shard_map/ppermute | solution.py:28
  59.6 3.2 %collective-permute-done.19 = bf16[4,2,64,256]{3,2,1,0:T(8,128)(2,1)S(1)} collective-permute-done((bf16[4,2,64,256]{3,2,1,0:T(8,128)(2,1)S(1)}, bf16[4,2,64,256]{3,2,1,0:T(8,128)(2,1)S(1)}, u32[]{:S(2)}, u32[]{:S(2)}) %collective-permute-start.19) | collective-permute-done | bytes 262176 | tf_op jit(solution)/shard_map/ppermute | solution.py:28
  63.0 1.3 %collective-permute-start.20 = (bf16[2,64,256]{2,1,0:T(8,128)(2,1)S(1)}, bf16[2,64,256]{2,1,0:T(8,128)(2,1)S(1)}, u32[]{:S(2)}, u32[]{:S(2)}) collective-permute-start(bf16[2,64,256]{2,1,0:T(8,128)(2,1)S(1)} %get-tuple-element.38), channel_id=1, source_target_pairs={{4,0},{5,1},{6,2},{7,3},{0,4},{1,5},{2,6},{3,7},{12,8},{13,9},{14,... | collective-permute-start | bytes 196616 | tf_op jit(solution)/shard_map/ppermute | solution.py:28
  64.3 2.6 %collective-permute-done.17 = bf16[2,64,256]{2,1,0:T(8,128)(2,1)S(1)} collective-permute-done((bf16[2,64,256]{2,1,0:T(8,128)(2,1)S(1)}, bf16[2,64,256]{2,1,0:T(8,128)(2,1)S(1)}, u32[]{:S(2)}, u32[]{:S(2)}) %collective-permute-start.17) | collective-permute-done | bytes 65568 | tf_op jit(solution)/shard_map/ppermute | solution.py:28
  66.9 0.5 collective-permute-start.21
  67.4 1.5 %collective-permute-done.18 = bf16[2,64,256]{2,1,0:T(8,128)(2,1)S(1)} collective-permute-done((bf16[2,64,256]{2,1,0:T(8,128)(2,1)S(1)}, bf16[2,64,256]{2,1,0:T(8,128)(2,1)S(1)}, u32[]{:S(2)}, u32[]{:S(2)}) %collective-permute-start.18) | collective-permute-done | bytes 65568 | tf_op jit(solution)/shard_map/ppermute | solution.py:28
  68.9 0.2 collective-permute-start.22
  69.1 3.6 %collective-permute-done.21 = bf16[2,64,256]{2,1,0:T(8,128)(2,1)S(1)} collective-permute-done((bf16[2,64,256]{2,1,0:T(8,128)(2,1)S(1)}, bf16[2,64,256]{2,1,0:T(8,128)(2,1)S(1)}, u32[]{:S(2)}, u32[]{:S(2)}) %collective-permute-start.21) | collective-permute-done | bytes 65568 | tf_op jit(solution)/shard_map/ppermute | solution.py:28
  72.7 2.3 %collective-permute-done.22 = bf16[2,64,256]{2,1,0:T(8,128)(2,1)S(1)} collective-permute-done((bf16[2,64,256]{2,1,0:T(8,128)(2,1)S(1)}, bf16[2,64,256]{2,1,0:T(8,128)(2,1)S(1)}, u32[]{:S(2)}, u32[]{:S(2)}) %collective-permute-start.22) | collective-permute-done | bytes 65568 | tf_op jit(solution)/shard_map/ppermute | solution.py:28
  75.0 1.5 %collective-permute-start.23 = (bf16[2,64,512]{2,1,0:T(8,128)(2,1)S(1)}, bf16[2,64,512]{2,1,0:T(8,128)(2,1)S(1)}, u32[]{:S(2)}, u32[]{:S(2)}) collective-permute-start(bf16[2,64,512]{2,1,0:T(8,128)(2,1)S(1)} %pad_maximum_fusion.3), channel_id=1, source_target_pairs={{16,0},{0,16},{17,1},{1,17},{18,2},{2,18},{19,3},{3,19},{20,4},{4,... | collective-permute-start | bytes 393224 | tf_op jit(solution)/shard_map/ppermute | solution.py:28
  76.5 0.7 slice_dynamic-update-slice_fusion.1
  77.1 2.9 %collective-permute-done.23 = bf16[2,64,512]{2,1,0:T(8,128)(2,1)S(1)} collective-permute-done((bf16[2,64,512]{2,1,0:T(8,128)(2,1)S(1)}, bf16[2,64,512]{2,1,0:T(8,128)(2,1)S(1)}, u32[]{:S(2)}, u32[]{:S(2)}) %collective-permute-start.23) | collective-permute-done | bytes 131104 | tf_op jit(solution)/shard_map/ppermute | solution.py:28
  80.2 0.7 slice_dynamic-update-slice_fusion
  80.8 0.7 collective-permute-done.24
  81.7 0.1 constant_dynamic-update-slice_fusion
  81.8 0.5 copy-done.7
  82.4 1.3 %copy-done.5 = bf16[2,128,4096]{2,1,0:T(8,128)(2,1)} copy-done((bf16[2,128,4096]{2,1,0:T(8,128)(2,1)}, bf16[2,128,4096]{2,1,0:T(8,128)(2,1)S(1)}, u32[]{:S(2)}) %copy-start.5) | copy-done | bytes 2097176
  (63 shorter events, 0.9 us)
Async XLA Ops:
  1.4 5.6 %collective-permute-start.4 = (bf16[64,512]{1,0:T(8,128)(2,1)S(1)}, bf16[64,512]{1,0:T(8,128)(2,1)S(1)}, u32[]{:S(2)}, u32[]{:S(2)}) collective-permute-start(bf16[64,512]{1,0:T(8,128)(2,1)S(1)} %pad_maximum_fusion.4), channel_id=1, source_target_pairs={{1,0},{0,1},{3,2},{2,3},{5,4},{4,5},{7,6},{6,7},{9,8},{8,9},{11,10... | collective-permute-start | bytes 196616 | tf_op jit(solution)/shard_map/ppermute | solution.py:28
  2.0 2.5 %copy-start.1 = (bf16[2,128,4096]{2,1,0:T(8,128)(2,1)S(1)}, bf16[2,128,4096]{2,1,0:T(8,128)(2,1)}, u32[]{:S(2)}) copy-start(bf16[2,128,4096]{2,1,0:T(8,128)(2,1)} %refs_2_.3) | copy-start | bytes 6291460
  2.0 4.0 %copy-start.3 = (bf16[2,128,1024]{2,1,0:T(8,128)(2,1)S(1)}, bf16[2,128,1024]{2,1,0:T(8,128)(2,1)}, u32[]{:S(2)}) copy-start(bf16[2,128,1024]{2,1,0:T(8,128)(2,1)} %refs_4_.3) | copy-start | bytes 1572868
  2.0 4.1 %copy-start.8 = (s32[2]{0:T(128)S(1)}, s32[2]{0:T(128)}, u32[]{:S(2)}) copy-start(s32[2]{0:T(128)} %param.11) | copy-start | bytes 28
  2.0 4.1 %copy-start.9 = (s32[2]{0:T(128)S(1)}, s32[2]{0:T(128)}, u32[]{:S(2)}) copy-start(s32[2]{0:T(128)} %param.10) | copy-start | bytes 28
  4.5 2.5 %copy-start.6 = (bf16[64,1024]{1,0:T(8,128)(2,1)S(1)}, bf16[64,1024]{1,0:T(8,128)(2,1)}, u32[]{:S(2)}) copy-start(bf16[64,1024]{1,0:T(8,128)(2,1)} %param.9) | copy-start | bytes 393220
  4.5 28.8 %copy-start = (bf16[2,128,4096]{2,1,0:T(8,128)(2,1)S(1)}, bf16[2,128,4096]{2,1,0:T(8,128)(2,1)}, u32[]{:S(2)}) copy-start(bf16[2,128,4096]{2,1,0:T(8,128)(2,1)} %refs_0_.3) | copy-start | bytes 6291460
  4.5 28.8 %collective-permute-start.1 = (bf16[2,128,2048]{2,1,0:T(8,128)(2,1)}, bf16[2,128,2048]{2,1,0:T(8,128)(2,1)}, u32[]{:S(2)}, u32[]{:S(2)}) collective-permute-start(bf16[2,128,2048]{2,1,0:T(8,128)(2,1)} %constant_dynamic-slice_fusion.9), channel_id=1, source_target_pairs={{1,0},{0,1},{3,2},{2,3},{5,4},{4,5},{7,6},{6,7},{9,8},{8,9},{11,10... | collective-permute-start | bytes 3145736 | tf_op jit(solution)/shard_map/ppermute | solution.py:28
  5.6 27.7 %collective-permute-start.2 = (bf16[2,128,2048]{2,1,0:T(8,128)(2,1)}, bf16[2,128,2048]{2,1,0:T(8,128)(2,1)}, u32[]{:S(2)}, u32[]{:S(2)}) collective-permute-start(bf16[2,128,2048]{2,1,0:T(8,128)(2,1)} %constant_dynamic-slice_fusion.8), channel_id=1, source_target_pairs={{1,0},{0,1},{3,2},{2,3},{5,4},{4,5},{7,6},{6,7},{9,8},{8,9},{11,10... | collective-permute-start | bytes 3145736 | tf_op jit(solution)/shard_map/ppermute | solution.py:28
  7.1 8.0 %collective-permute-start.10 = (bf16[1,2,64,256]{3,2,1,0:T(8,128)(2,1)S(1)}, bf16[1,2,64,256]{3,2,1,0:T(8,128)(2,1)S(1)}, u32[]{:S(2)}, u32[]{:S(2)}) collective-permute-start(bf16[1,2,64,256]{3,2,1,0:T(8,128)(2,1)S(1)} %maximum_bitcast_fusion.1), channel_id=1, source_target_pairs={{8,0},{9,1},{10,2},{11,3},{12,4},{13,5},{14,6},{15,7},{0,8},{1,9},... | collective-permute-start | bytes 196616 | tf_op jit(solution)/shard_map/ppermute | solution.py:28
  10.8 6.7 %collective-permute-start.11 = (bf16[1,2,64,256]{3,2,1,0:T(8,128)(2,1)S(1)}, bf16[1,2,64,256]{3,2,1,0:T(8,128)(2,1)S(1)}, u32[]{:S(2)}, u32[]{:S(2)}) collective-permute-start(bf16[1,2,64,256]{3,2,1,0:T(8,128)(2,1)S(1)} %maximum_bitcast_fusion.1), channel_id=1, source_target_pairs={{12,0},{13,1},{14,2},{15,3},{8,4},{9,5},{10,6},{11,7},{4,8},{5,9},... | collective-permute-start | bytes 196616 | tf_op jit(solution)/shard_map/ppermute | solution.py:28
  12.1 5.6 %collective-permute-start.9 = (bf16[1,2,64,256]{3,2,1,0:T(8,128)(2,1)S(1)}, bf16[1,2,64,256]{3,2,1,0:T(8,128)(2,1)S(1)}, u32[]{:S(2)}, u32[]{:S(2)}) collective-permute-start(bf16[1,2,64,256]{3,2,1,0:T(8,128)(2,1)S(1)} %maximum_bitcast_fusion.1), channel_id=1, source_target_pairs={{4,0},{5,1},{6,2},{7,3},{0,4},{1,5},{2,6},{3,7},{12,8},{13,9},{14,... | collective-permute-start | bytes 196616 | tf_op jit(solution)/shard_map/ppermute | solution.py:28
  15.1 18.2 %collective-permute-start.3 = (bf16[2,128,512]{2,1,0:T(8,128)(2,1)}, bf16[2,128,512]{2,1,0:T(8,128)(2,1)S(1)}, u32[]{:S(2)}, u32[]{:S(2)}) collective-permute-start(bf16[2,128,512]{2,1,0:T(8,128)(2,1)} %pad_maximum_fusion), channel_id=1, source_target_pairs={{1,0},{0,1},{3,2},{2,3},{5,4},{4,5},{7,6},{6,7},{9,8},{8,9},{11,10... | collective-permute-start | bytes 786440 | tf_op jit(solution)/shard_map/ppermute | solution.py:28
  17.4 1.2 %collective-permute-start = (s32[2,2]{1,0:T(2,128)S(1)}, s32[2,2]{1,0:T(2,128)S(1)}, u32[]{:S(2)}, u32[]{:S(2)}) collective-permute-start(s32[2,2]{1,0:T(2,128)S(1)} %reshape.18), channel_id=1, source_target_pairs={{1,0},{0,1},{3,2},{2,3},{5,4},{4,5},{7,6},{6,7},{9,8},{8,9},{11,10... | collective-permute-start | bytes 56 | tf_op jit(solution)/shard_map/ppermute | solution.py:28
  17.7 4.3 %collective-permute-start.5 = (bf16[1,2,64,256]{3,2,1,0:T(8,128)(2,1)S(1)}, bf16[1,2,64,256]{3,2,1,0:T(8,128)(2,1)S(1)}, u32[]{:S(2)}, u32[]{:S(2)}) collective-permute-start(bf16[1,2,64,256]{3,2,1,0:T(8,128)(2,1)S(1)} %maximum_bitcast_fusion), channel_id=1, source_target_pairs={{4,0},{5,1},{6,2},{7,3},{0,4},{1,5},{2,6},{3,7},{12,8},{13,9},{14,... | collective-permute-start | bytes 196616 | tf_op jit(solution)/shard_map/ppermute | solution.py:28
  18.6 5.7 %collective-permute-start.6 = (bf16[1,2,64,256]{3,2,1,0:T(8,128)(2,1)S(1)}, bf16[1,2,64,256]{3,2,1,0:T(8,128)(2,1)}, u32[]{:S(2)}, u32[]{:S(2)}) collective-permute-start(bf16[1,2,64,256]{3,2,1,0:T(8,128)(2,1)S(1)} %maximum_bitcast_fusion), channel_id=1, source_target_pairs={{8,0},{9,1},{10,2},{11,3},{12,4},{13,5},{14,6},{15,7},{0,8},{1,9},... | collective-permute-start | bytes 196616 | tf_op jit(solution)/shard_map/ppermute | solution.py:28
  21.9 11.4 %collective-permute-start.12 = (bf16[4,2,64,256]{3,2,1,0:T(8,128)(2,1)S(1)}, bf16[4,2,64,256]{3,2,1,0:T(8,128)(2,1)S(1)}, u32[]{:S(2)}, u32[]{:S(2)}) collective-permute-start(bf16[4,2,64,256]{3,2,1,0:T(8,128)(2,1)S(1)} %pad_maximum_fusion.2.refs_6_), channel_id=1, source_target_pairs={{2,0},{3,1},{0,2},{1,3},{6,4},{7,5},{4,6},{5,7},{10,8},{11,9},{8,1... | collective-permute-start | bytes 786440 | tf_op jit(solution)/shard_map/ppermute | solution.py:28
  24.2 6.6 %collective-permute-start.7 = (bf16[1,2,64,256]{3,2,1,0:T(8,128)(2,1)S(1)}, bf16[1,2,64,256]{3,2,1,0:T(8,128)(2,1)S(1)}, u32[]{:S(2)}, u32[]{:S(2)}) collective-permute-start(bf16[1,2,64,256]{3,2,1,0:T(8,128)(2,1)S(1)} %maximum_bitcast_fusion), channel_id=1, source_target_pairs={{12,0},{13,1},{14,2},{15,3},{8,4},{9,5},{10,6},{11,7},{4,8},{5,9},... | collective-permute-start | bytes 196616 | tf_op jit(solution)/shard_map/ppermute | solution.py:28
  31.7 14.8 %collective-permute-start.8 = (bf16[4,2,64,256]{3,2,1,0:T(8,128)(2,1)S(1)}, bf16[4,2,64,256]{3,2,1,0:T(8,128)(2,1)S(1)}, u32[]{:S(2)}, u32[]{:S(2)}) collective-permute-start(bf16[4,2,64,256]{3,2,1,0:T(8,128)(2,1)S(1)} %pad_maximum_fusion.1.refs_6_), channel_id=1, source_target_pairs={{2,0},{3,1},{0,2},{1,3},{6,4},{7,5},{4,6},{5,7},{10,8},{11,9},{8,1... | collective-permute-start | bytes 786440 | tf_op jit(solution)/shard_map/ppermute | solution.py:28
  33.3 1.6 %copy-start.2 = (bf16[2,128,4096]{2,1,0:T(8,128)(2,1)S(1)}, bf16[2,128,4096]{2,1,0:T(8,128)(2,1)}, u32[]{:S(2)}) copy-start(bf16[2,128,4096]{2,1,0:T(8,128)(2,1)} %refs_2_.3) | copy-start | bytes 6291460
  42.3 16.0 %collective-permute-start.15 = (bf16[4,2,64,256]{3,2,1,0:T(8,128)(2,1)S(1)}, bf16[4,2,64,256]{3,2,1,0:T(8,128)(2,1)S(1)}, u32[]{:S(2)}, u32[]{:S(2)}) collective-permute-start(bf16[4,2,64,256]{3,2,1,0:T(8,128)(2,1)S(1)} %get-tuple-element.24), channel_id=1, source_target_pairs={{2,0},{3,1},{0,2},{1,3},{6,4},{7,5},{4,6},{5,7},{10,8},{11,9},{8,1... | collective-permute-start | bytes 786440 | tf_op jit(solution)/shard_map/ppermute | solution.py:28
  54.1 8.8 %collective-permute-start.19 = (bf16[4,2,64,256]{3,2,1,0:T(8,128)(2,1)S(1)}, bf16[4,2,64,256]{3,2,1,0:T(8,128)(2,1)S(1)}, u32[]{:S(2)}, u32[]{:S(2)}) collective-permute-start(bf16[4,2,64,256]{3,2,1,0:T(8,128)(2,1)S(1)} %get-tuple-element.26), channel_id=1, source_target_pairs={{2,0},{3,1},{0,2},{1,3},{6,4},{7,5},{4,6},{5,7},{10,8},{11,9},{8,1... | collective-permute-start | bytes 786440 | tf_op jit(solution)/shard_map/ppermute | solution.py:28
  57.8 18.7 %collective-permute-start.14 = (bf16[2,128,512]{2,1,0:T(8,128)(2,1)S(1)}, bf16[2,128,512]{2,1,0:T(8,128)(2,1)S(1)}, u32[]{:S(2)}, u32[]{:S(2)}) collective-permute-start(bf16[2,128,512]{2,1,0:T(8,128)(2,1)S(1)} %get-tuple-element.22), channel_id=1, source_target_pairs={{1,0},{0,1},{3,2},{2,3},{5,4},{4,5},{7,6},{6,7},{9,8},{8,9},{11,10... | collective-permute-start | bytes 786440 | tf_op jit(solution)/shard_map/ppermute | solution.py:28
  57.8 23.9 %collective-permute-start.13 = (bf16[2,128,2048]{2,1,0:T(8,128)(2,1)S(1)}, bf16[2,128,2048]{2,1,0:T(8,128)(2,1)S(1)}, u32[]{:S(2)}, u32[]{:S(2)}) collective-permute-start(bf16[2,128,2048]{2,1,0:T(8,128)(2,1)S(1)} %get-tuple-element.20), channel_id=1, source_target_pairs={{1,0},{0,1},{3,2},{2,3},{5,4},{4,5},{7,6},{6,7},{9,8},{8,9},{11,10... | collective-permute-start | bytes 3145736 | tf_op jit(solution)/shard_map/ppermute | solution.py:28
  58.4 4.6 %collective-permute-start.16 = (bf16[2,64,256]{2,1,0:T(8,128)(2,1)S(1)}, bf16[2,64,256]{2,1,0:T(8,128)(2,1)S(1)}, u32[]{:S(2)}, u32[]{:S(2)}) collective-permute-start(bf16[2,64,256]{2,1,0:T(8,128)(2,1)S(1)} %get-tuple-element.35), channel_id=1, source_target_pairs={{4,0},{5,1},{6,2},{7,3},{0,4},{1,5},{2,6},{3,7},{12,8},{13,9},{14,... | collective-permute-start | bytes 196616 | tf_op jit(solution)/shard_map/ppermute | solution.py:28
  59.6 7.3 %collective-permute-start.17 = (bf16[2,64,256]{2,1,0:T(8,128)(2,1)S(1)}, bf16[2,64,256]{2,1,0:T(8,128)(2,1)S(1)}, u32[]{:S(2)}, u32[]{:S(2)}) collective-permute-start(bf16[2,64,256]{2,1,0:T(8,128)(2,1)S(1)} %get-tuple-element.37), channel_id=1, source_target_pairs={{8,0},{9,1},{10,2},{11,3},{12,4},{13,5},{14,6},{15,7},{0,8},{1,9},... | collective-permute-start | bytes 196616 | tf_op jit(solution)/shard_map/ppermute | solution.py:28
  62.8 6.1 %collective-permute-start.18 = (bf16[2,64,256]{2,1,0:T(8,128)(2,1)S(1)}, bf16[2,64,256]{2,1,0:T(8,128)(2,1)S(1)}, u32[]{:S(2)}, u32[]{:S(2)}) collective-permute-start(bf16[2,64,256]{2,1,0:T(8,128)(2,1)S(1)} %get-tuple-element.36), channel_id=1, source_target_pairs={{12,0},{13,1},{14,2},{15,3},{8,4},{9,5},{10,6},{11,7},{4,8},{5,9},... | collective-permute-start | bytes 196616 | tf_op jit(solution)/shard_map/ppermute | solution.py:28
  62.9 18.8 %copy-start.4 = (bf16[2,128,4096]{2,1,0:T(8,128)(2,1)S(1)}, bf16[2,128,4096]{2,1,0:T(8,128)(2,1)}, u32[]{:S(2)}) copy-start(bf16[2,128,4096]{2,1,0:T(8,128)(2,1)} %get-tuple-element.19) | copy-start | bytes 6291460
  63.0 6.1 %collective-permute-start.20 = (bf16[2,64,256]{2,1,0:T(8,128)(2,1)S(1)}, bf16[2,64,256]{2,1,0:T(8,128)(2,1)S(1)}, u32[]{:S(2)}, u32[]{:S(2)}) collective-permute-start(bf16[2,64,256]{2,1,0:T(8,128)(2,1)S(1)} %get-tuple-element.38), channel_id=1, source_target_pairs={{4,0},{5,1},{6,2},{7,3},{0,4},{1,5},{2,6},{3,7},{12,8},{13,9},{14,... | collective-permute-start | bytes 196616 | tf_op jit(solution)/shard_map/ppermute | solution.py:28
  66.9 5.8 %collective-permute-start.21 = (bf16[2,64,256]{2,1,0:T(8,128)(2,1)S(1)}, bf16[2,64,256]{2,1,0:T(8,128)(2,1)S(1)}, u32[]{:S(2)}, u32[]{:S(2)}) collective-permute-start(bf16[2,64,256]{2,1,0:T(8,128)(2,1)S(1)} %get-tuple-element.40), channel_id=1, source_target_pairs={{8,0},{9,1},{10,2},{11,3},{12,4},{13,5},{14,6},{15,7},{0,8},{1,9},... | collective-permute-start | bytes 196616 | tf_op jit(solution)/shard_map/ppermute | solution.py:28
  68.9 6.1 %collective-permute-start.22 = (bf16[2,64,256]{2,1,0:T(8,128)(2,1)S(1)}, bf16[2,64,256]{2,1,0:T(8,128)(2,1)S(1)}, u32[]{:S(2)}, u32[]{:S(2)}) collective-permute-start(bf16[2,64,256]{2,1,0:T(8,128)(2,1)S(1)} %get-tuple-element.39), channel_id=1, source_target_pairs={{12,0},{13,1},{14,2},{15,3},{8,4},{9,5},{10,6},{11,7},{4,8},{5,9},... | collective-permute-start | bytes 196616 | tf_op jit(solution)/shard_map/ppermute | solution.py:28
  75.0 5.0 %collective-permute-start.23 = (bf16[2,64,512]{2,1,0:T(8,128)(2,1)S(1)}, bf16[2,64,512]{2,1,0:T(8,128)(2,1)S(1)}, u32[]{:S(2)}, u32[]{:S(2)}) collective-permute-start(bf16[2,64,512]{2,1,0:T(8,128)(2,1)S(1)} %pad_maximum_fusion.3), channel_id=1, source_target_pairs={{16,0},{0,16},{17,1},{1,17},{18,2},{2,18},{19,3},{3,19},{20,4},{4,... | collective-permute-start | bytes 393224 | tf_op jit(solution)/shard_map/ppermute | solution.py:28
  80.1 1.4 %collective-permute-start.24 = (f32[64,512]{1,0:T(8,128)S(1)}, f32[64,512]{1,0:T(8,128)S(1)}, u32[]{:S(2)}, u32[]{:S(2)}) collective-permute-start(f32[64,512]{1,0:T(8,128)S(1)} %get-tuple-element.34), channel_id=1, source_target_pairs={{1,0},{0,1},{3,2},{2,3},{5,4},{4,5},{7,6},{6,7},{9,8},{8,9},{11,10... | collective-permute-start | bytes 393224 | tf_op jit(solution)/shard_map/ppermute | solution.py:28
  81.7 0.7 copy-start.7
  82.4 1.3 %copy-start.5 = (bf16[2,128,4096]{2,1,0:T(8,128)(2,1)}, bf16[2,128,4096]{2,1,0:T(8,128)(2,1)S(1)}, u32[]{:S(2)}) copy-start(bf16[2,128,4096]{2,1,0:T(8,128)(2,1)S(1)} %constant_dynamic-update-slice_fusion) | copy-start | bytes 6291460

commit v4 on v3

--- a/solution.py
+++ b/solution.py
@@ -251,6 +251,7 @@
     span = roots + rows
     vmem = pl.BlockSpec(memory_space=pltpu.VMEM)
     hbm = pl.BlockSpec(memory_space=pltpu.HBM)
+    q, g, b = (pltpu.with_memory_space_constraint(x, pltpu.HBM) for x in (q, g, b))
     args = [q, q_far, g, g_far, b, b_far, near, nxt]
     in_specs = [pl.BlockSpec(memory_space=pltpu.SMEM)] + [hbm] * len(args)
     aliases = {}
@@ -361,7 +362,9 @@
         for part in arrived:
             x = x + part
         sums.append(x)
-    x = jnp.concatenate(sums, axis=2)
+    x = jnp.concatenate(
+        [s[:, :, part * DH : (part + 1) * DH] for part in range(2) for s in sums], axis=2
+    )
     hop = 1
     while hop < n_grp:
         x = x.astype(BF16)
@@ -370,21 +373,18 @@
         hop *= 2
     far = swapped(x[1], "dev", 1)
     near = x[0]
+    wide = HEADS * DH
     pieces = []
     for part in range(2):
+        at = slice(part * wide, (part + 1) * wide)
         for side in range(CORES):
-            for head in range(HEADS):
-                at = (head * 2 + part) * DH
-                pieces.append(
-                    jnp.where(core == side, near[:, at : at + DH], far[:, at : at + DH])
-                )
+            pieces.append(jnp.where(core == side, near[:, at], far[:, at]))
     root_grad = jnp.concatenate(pieces, axis=1)
 
     dq, dq_far, db, db_far = outs
     dq_got = swapped(dq_far, "dev", 1)
     db_got = swapped(db_far, "dev", 1)
     query_grad = lax.dynamic_update_slice_in_dim(dq, dq_got, (1 - core) * (qcols // CORES), 2)
-    wide = HEADS * DH
     branch_grad = db
     for part in range(2):
         branch_grad = lax.dynamic_update_slice_in_dim(

time: 83.9 us -> 83 us (0.989)
  Pallas kernels: 14.9 us -> 16.1 us
  local copies, waits for them, and re-layouts: 9.5 us -> 8.41 us
  waiting for transfers between devices: 25 us -> 24 us
  starting transfers between devices: 31.1 us -> 32 us
  other arithmetic: 2.24 us -> 1.38 us
    unnamed x20 -> x12, local copies, waits for them, and re-layouts: 3.47 us -> 1.34 us
    pallas_call x2, Pallas kernels: 14.9 us -> 16.1 us  [head_grads(): pl.pallas_call(functools.partial(head_kernel, head, offsets), in_specs=in...]
    dynamic_slice x4, local copies, waits for them, and re-layouts: 4.32 us -> 5.33 us  [cols(): lax.dynamic_slice_in_dim(x, p * part + which * wide, wide, axis)]
    ppermute x25, waiting for transfers between devices: 25 us -> 24 us  [swapped(): return lax.ppermute(block, axis, route)]
    ppermute x25, starting transfers between devices: 31.1 us -> 32 us  [swapped(): return lax.ppermute(block, axis, route)]
  transfers between devices with their start and end apart: 25 -> 25, of which waited for: 13 -> 13; matrix products, arithmetic and copies ran while one was open for 9% -> 9% of each run, Pallas kernels for 18% -> 19%
where the time goes in v4:
time: 83 us; the launch traced here: 82.8 us
  starting transfers between devices  32 us (39%)
  waiting for transfers between devices  24 us (29%)
  Pallas kernels  16.1 us (19%)
  local copies, waits for them, and re-layouts  8.41 us (10%)
  other arithmetic  1.38 us (2%)
  between operations  0.93 us (1%)
    ppermute x25, starting transfers between devices, swapped(): return lax.ppermute(block, axis, route)  32 us
    ppermute x25, waiting for transfers between devices, swapped(): return lax.ppermute(block, axis, route)  24 us
    pallas_call x2, Pallas kernels, head_grads(): pl.pallas_call(functools.partial(head_kernel, head, offsets), in_specs=in...  16.1 us
    dynamic_slice x4, local copies, waits for them, and re-layouts, cols(): lax.dynamic_slice_in_dim(x, p * part + which * wide, wide, axis)  5.33 us
  transfers between devices with their start and end apart: 25, of which 13 were waited for; matrix products, arithmetic and copies ran while one was open for 9% of the time, Pallas kernels for 19%

profile of v4, /device:TPU:0, one launch (start us, length us, event | category | flops | bytes accessed | tf_op | source)
XLA Modules:
  0.0 82.8 jit_solution(17716506505855791973)
XLA Ops:
  0.7 0.9 %constant_dynamic-slice_fusion.3 = (bf16[64,256]{1,0:T(8,128)(2,1)S(1)}, bf16[64,256]{1,0:T(8,128)(2,1)S(1)}) fusion(bf16[64,1024]{1,0:T(8,128)(2,1)} %param.9, s32[]{:T(128)S(6)} %select_n.54, s32[]{:T(128)S(6)} %select_n.55), kind=kLoop, calls=%fused_computation.43 | loop fusion | bytes 131080 | tf_op jit(solution)/shard_map/dynamic_slice | solution.py:320
  1.6 0.6 collective-permute-start.4
  2.2 2.3 %constant_dynamic-slice_fusion.9 = bf16[2,128,2048]{2,1,0:T(8,128)(2,1)} fusion(bf16[2,128,4096]{2,1,0:T(8,128)(2,1)} %refs_0_.3, s32[]{:T(128)S(6)} %select_n.53), kind=kLoop, calls=%fused_computation.49 | loop fusion | bytes 2097156 | tf_op jit(solution)/shard_map/dynamic_slice | solution.py:320
  4.5 1.1 %constant_dynamic-slice_fusion.8 = bf16[2,128,2048]{2,1,0:T(8,128)(2,1)} fusion(bf16[2,128,4096]{2,1,0:T(8,128)(2,1)S(1)} %copy-done, s32[]{:T(128)S(6)} %select_n.53), kind=kLoop, calls=%fused_computation.48 | loop fusion | bytes 2097156 | tf_op jit(solution)/shard_map/dynamic_slice | solution.py:320
  5.6 0.5 collective-permute-start.2
  6.1 1.0 %constant_dynamic-slice_fusion.7 = (bf16[2,128,256]{2,1,0:T(8,128)(2,1)S(1)}, bf16[2,128,256]{2,1,0:T(8,128)(2,1)S(1)}) fusion(bf16[2,128,1024]{2,1,0:T(8,128)(2,1)} %refs_4_.3, s32[]{:T(128)S(6)} %select_n.54, s32[]{:T(128)S(6)} %select_n.55), kind=kLoop, calls=%fused_computation.47 | loop fusion | bytes 524296 | tf_op jit(solution)/shard_map/dynamic_slice | solution.py:320
  7.1 0.1 pad_add_fusion.1
  7.2 0.1 reshape.18
  7.4 3.7 %collective-permute-start.10 = (bf16[1,2,64,256]{3,2,1,0:T(8,128)(2,1)S(1)}, bf16[1,2,64,256]{3,2,1,0:T(8,128)(2,1)S(1)}, u32[]{:S(2)}, u32[]{:S(2)}) collective-permute-start(bf16[1,2,64,256]{3,2,1,0:T(8,128)(2,1)S(1)} %maximum_bitcast_fusion.1), channel_id=1, source_target_pairs={{8,0},{9,1},{10,2},{11,3},{12,4},{13,5},{14,6},{15,7},{0,8},{1,9},... | collective-permute-start | bytes 196616 | tf_op jit(solution)/shard_map/ppermute | solution.py:28
  11.1 1.3 %collective-permute-start.11 = (bf16[1,2,64,256]{3,2,1,0:T(8,128)(2,1)S(1)}, bf16[1,2,64,256]{3,2,1,0:T(8,128)(2,1)S(1)}, u32[]{:S(2)}, u32[]{:S(2)}) collective-permute-start(bf16[1,2,64,256]{3,2,1,0:T(8,128)(2,1)S(1)} %maximum_bitcast_fusion.1), channel_id=1, source_target_pairs={{12,0},{13,1},{14,2},{15,3},{8,4},{9,5},{10,6},{11,7},{4,8},{5,9},... | collective-permute-start | bytes 196616 | tf_op jit(solution)/shard_map/ppermute | solution.py:28
  12.4 0.2 collective-permute-start.9
  12.7 2.7 %collective-permute-done.10 = bf16[1,2,64,256]{3,2,1,0:T(8,128)(2,1)S(1)} collective-permute-done((bf16[1,2,64,256]{3,2,1,0:T(8,128)(2,1)S(1)}, bf16[1,2,64,256]{3,2,1,0:T(8,128)(2,1)S(1)}, u32[]{:S(2)}, u32[]{:S(2)}) %collective-permute-start.10) | collective-permute-done | bytes 65568 | tf_op jit(solution)/shard_map/ppermute | solution.py:28
  15.4 2.4 %collective-permute-done.11 = bf16[1,2,64,256]{3,2,1,0:T(8,128)(2,1)S(1)} collective-permute-done((bf16[1,2,64,256]{3,2,1,0:T(8,128)(2,1)S(1)}, bf16[1,2,64,256]{3,2,1,0:T(8,128)(2,1)S(1)}, u32[]{:S(2)}, u32[]{:S(2)}) %collective-permute-start.11) | collective-permute-done | bytes 65568 | tf_op jit(solution)/shard_map/ppermute | solution.py:28
  17.8 0.2 collective-permute-done.9
  18.0 0.9 %collective-permute-start.5 = (bf16[1,2,64,256]{3,2,1,0:T(8,128)(2,1)S(1)}, bf16[1,2,64,256]{3,2,1,0:T(8,128)(2,1)S(1)}, u32[]{:S(2)}, u32[]{:S(2)}) collective-permute-start(bf16[1,2,64,256]{3,2,1,0:T(8,128)(2,1)S(1)} %maximum_bitcast_fusion), channel_id=1, source_target_pairs={{4,0},{5,1},{6,2},{7,3},{0,4},{1,5},{2,6},{3,7},{12,8},{13,9},{14,... | collective-permute-start | bytes 196616 | tf_op jit(solution)/shard_map/ppermute | solution.py:28
  18.9 3.1 %collective-permute-start.6 = (bf16[1,2,64,256]{3,2,1,0:T(8,128)(2,1)S(1)}, bf16[1,2,64,256]{3,2,1,0:T(8,128)(2,1)S(1)}, u32[]{:S(2)}, u32[]{:S(2)}) collective-permute-start(bf16[1,2,64,256]{3,2,1,0:T(8,128)(2,1)S(1)} %maximum_bitcast_fusion), channel_id=1, source_target_pairs={{8,0},{9,1},{10,2},{11,3},{12,4},{13,5},{14,6},{15,7},{0,8},{1,9},... | collective-permute-start | bytes 196616 | tf_op jit(solution)/shard_map/ppermute | solution.py:28
  22.1 0.2 collective-permute-done.5
  22.3 1.6 %collective-permute-start.12 = (bf16[4,2,64,256]{3,2,1,0:T(8,128)(2,1)S(1)}, bf16[4,2,64,256]{3,2,1,0:T(8,128)(2,1)S(1)}, u32[]{:S(2)}, u32[]{:S(2)}) collective-permute-start(bf16[4,2,64,256]{3,2,1,0:T(8,128)(2,1)S(1)} %pad_maximum_fusion.2.refs_6_), channel_id=1, source_target_pairs={{2,0},{3,1},{0,2},{1,3},{6,4},{7,5},{4,6},{5,7},{10,8},{11,9},{8,1... | collective-permute-start | bytes 786440 | tf_op jit(solution)/shard_map/ppermute | solution.py:28
  23.9 0.1 reshape.19
  24.0 0.5 collective-permute-done.6
  24.5 4.3 %collective-permute-start.7 = (bf16[1,2,64,256]{3,2,1,0:T(8,128)(2,1)S(1)}, bf16[1,2,64,256]{3,2,1,0:T(8,128)(2,1)S(1)}, u32[]{:S(2)}, u32[]{:S(2)}) collective-permute-start(bf16[1,2,64,256]{3,2,1,0:T(8,128)(2,1)S(1)} %maximum_bitcast_fusion), channel_id=1, source_target_pairs={{12,0},{13,1},{14,2},{15,3},{8,4},{9,5},{10,6},{11,7},{4,8},{5,9},... | collective-permute-start | bytes 196616 | tf_op jit(solution)/shard_map/ppermute | solution.py:28
  28.9 2.2 %collective-permute-done.7 = bf16[1,2,64,256]{3,2,1,0:T(8,128)(2,1)S(1)} collective-permute-done((bf16[1,2,64,256]{3,2,1,0:T(8,128)(2,1)S(1)}, bf16[1,2,64,256]{3,2,1,0:T(8,128)(2,1)S(1)}, u32[]{:S(2)}, u32[]{:S(2)}) %collective-permute-start.7) | collective-permute-done | bytes 65568 | tf_op jit(solution)/shard_map/ppermute | solution.py:28
  31.1 1.6 %collective-permute-start.8 = (bf16[4,2,64,256]{3,2,1,0:T(8,128)(2,1)S(1)}, bf16[4,2,64,256]{3,2,1,0:T(8,128)(2,1)S(1)}, u32[]{:S(2)}, u32[]{:S(2)}) collective-permute-start(bf16[4,2,64,256]{3,2,1,0:T(8,128)(2,1)S(1)} %pad_maximum_fusion.1.refs_6_), channel_id=1, source_target_pairs={{2,0},{3,1},{0,2},{1,3},{6,4},{7,5},{4,6},{5,7},{10,8},{11,9},{8,1... | collective-permute-start | bytes 786440 | tf_op jit(solution)/shard_map/ppermute | solution.py:28
  32.7 8.0 %shard_map.85 = (bf16[2,128,4096]{2,1,0:T(8,128)(2,1)}, bf16[2,128,2048]{2,1,0:T(8,128)(2,1)S(1)}, bf16[2,128,1024]{2,1,0:T(8,128)(2,1)}, bf16[2,128,512]{2,1,0:...) custom-call(s32[10]{0:T(128)S(1)} %pad_add_fusion.2.info, ...), custom_call_target="tpu_custom_call" | custom-call | flops 3019898880 | bytes 2097152 | tf_op jit(solution)/shard_map/pallas_call | solution.py:291
  40.7 4.2 %collective-permute-start.15 = (bf16[4,2,64,256]{3,2,1,0:T(8,128)(2,1)S(1)}, bf16[4,2,64,256]{3,2,1,0:T(8,128)(2,1)S(1)}, u32[]{:S(2)}, u32[]{:S(2)}) collective-permute-start(bf16[4,2,64,256]{3,2,1,0:T(8,128)(2,1)S(1)} %get-tuple-element.24), channel_id=1, source_target_pairs={{2,0},{3,1},{0,2},{1,3},{6,4},{7,5},{4,6},{5,7},{10,8},{11,9},{8,1... | collective-permute-start | bytes 786440 | tf_op jit(solution)/shard_map/ppermute | solution.py:28
  44.9 8.0 %shard_map.86 = (bf16[2,128,4096]{2,1,0:T(8,128)(2,1)}, bf16[2,128,2048]{2,1,0:T(8,128)(2,1)S(1)}, bf16[2,128,1024]{2,1,0:T(8,128)(2,1)}, bf16[2,128,512]{2,1,0:...) custom-call(s32[10]{0:T(128)S(1)} %pad_add_fusion.2.info, ...), custom_call_target="tpu_custom_call", output_to_operand_aliasing={{0}: (9, {}), {1}: (10, {}), {2}: (11, {}), {3}: (12, {})} | custom-call | flops 3019898880 | bytes 2097152 | tf_op jit(solution)/shard_map/pallas_call | solution.py:291
  53.0 3.7 %collective-permute-start.19 = (bf16[4,2,64,256]{3,2,1,0:T(8,128)(2,1)S(1)}, bf16[4,2,64,256]{3,2,1,0:T(8,128)(2,1)S(1)}, u32[]{:S(2)}, u32[]{:S(2)}) collective-permute-start(bf16[4,2,64,256]{3,2,1,0:T(8,128)(2,1)S(1)} %get-tuple-element.26), channel_id=1, source_target_pairs={{2,0},{3,1},{0,2},{1,3},{6,4},{7,5},{4,6},{5,7},{10,8},{11,9},{8,1... | collective-permute-start | bytes 786440 | tf_op jit(solution)/shard_map/ppermute | solution.py:28
  56.7 0.5 collective-permute-start.13
  57.2 0.1 fusion.8
  57.3 1.2 %collective-permute-start.16 = (bf16[2,64,256]{2,1,0:T(8,128)(2,1)S(1)}, bf16[2,64,256]{2,1,0:T(8,128)(2,1)S(1)}, u32[]{:S(2)}, u32[]{:S(2)}) collective-permute-start(bf16[2,64,256]{2,1,0:T(8,128)(2,1)S(1)} %get-tuple-element.39), channel_id=1, source_target_pairs={{4,0},{5,1},{6,2},{7,3},{0,4},{1,5},{2,6},{3,7},{12,8},{13,9},{14,... | collective-permute-start | bytes 196616 | tf_op jit(solution)/shard_map/ppermute | solution.py:28
  58.6 3.1 %collective-permute-done.19 = bf16[4,2,64,256]{3,2,1,0:T(8,128)(2,1)S(1)} collective-permute-done((bf16[4,2,64,256]{3,2,1,0:T(8,128)(2,1)S(1)}, bf16[4,2,64,256]{3,2,1,0:T(8,128)(2,1)S(1)}, u32[]{:S(2)}, u32[]{:S(2)}) %collective-permute-start.19) | collective-permute-done | bytes 262176 | tf_op jit(solution)/shard_map/ppermute | solution.py:28
  61.6 0.1 collective-permute-start.18
  61.8 0.1 fusion.9
  61.9 1.4 %collective-permute-start.20 = (bf16[2,64,256]{2,1,0:T(8,128)(2,1)S(1)}, bf16[2,64,256]{2,1,0:T(8,128)(2,1)S(1)}, u32[]{:S(2)}, u32[]{:S(2)}) collective-permute-start(bf16[2,64,256]{2,1,0:T(8,128)(2,1)S(1)} %get-tuple-element.42), channel_id=1, source_target_pairs={{4,0},{5,1},{6,2},{7,3},{0,4},{1,5},{2,6},{3,7},{12,8},{13,9},{14,... | collective-permute-start | bytes 196616 | tf_op jit(solution)/shard_map/ppermute | solution.py:28
  63.3 2.6 %collective-permute-done.17 = bf16[2,64,256]{2,1,0:T(8,128)(2,1)S(1)} collective-permute-done((bf16[2,64,256]{2,1,0:T(8,128)(2,1)S(1)}, bf16[2,64,256]{2,1,0:T(8,128)(2,1)S(1)}, u32[]{:S(2)}, u32[]{:S(2)}) %collective-permute-start.17) | collective-permute-done | bytes 65568 | tf_op jit(solution)/shard_map/ppermute | solution.py:28
  65.8 0.4 collective-permute-start.21
  66.2 1.5 %collective-permute-done.18 = bf16[2,64,256]{2,1,0:T(8,128)(2,1)S(1)} collective-permute-done((bf16[2,64,256]{2,1,0:T(8,128)(2,1)S(1)}, bf16[2,64,256]{2,1,0:T(8,128)(2,1)S(1)}, u32[]{:S(2)}, u32[]{:S(2)}) %collective-permute-start.18) | collective-permute-done | bytes 65568 | tf_op jit(solution)/shard_map/ppermute | solution.py:28
  67.7 0.3 collective-permute-start.22
  68.0 3.7 %collective-permute-done.21 = bf16[2,64,256]{2,1,0:T(8,128)(2,1)S(1)} collective-permute-done((bf16[2,64,256]{2,1,0:T(8,128)(2,1)S(1)}, bf16[2,64,256]{2,1,0:T(8,128)(2,1)S(1)}, u32[]{:S(2)}, u32[]{:S(2)}) %collective-permute-start.21) | collective-permute-done | bytes 65568 | tf_op jit(solution)/shard_map/ppermute | solution.py:28
  71.7 2.1 %collective-permute-done.22 = bf16[2,64,256]{2,1,0:T(8,128)(2,1)S(1)} collective-permute-done((bf16[2,64,256]{2,1,0:T(8,128)(2,1)S(1)}, bf16[2,64,256]{2,1,0:T(8,128)(2,1)S(1)}, u32[]{:S(2)}, u32[]{:S(2)}) %collective-permute-start.22) | collective-permute-done | bytes 65568 | tf_op jit(solution)/shard_map/ppermute | solution.py:28
  73.9 2.3 %collective-permute-start.23 = (bf16[2,64,512]{2,1,0:T(8,128)(2,1)S(1)}, bf16[2,64,512]{2,1,0:T(8,128)(2,1)S(1)}, u32[]{:S(2)}, u32[]{:S(2)}) collective-permute-start(bf16[2,64,512]{2,1,0:T(8,128)(2,1)S(1)} %pad_maximum_fusion.4), channel_id=1, source_target_pairs={{16,0},{0,16},{17,1},{1,17},{18,2},{2,18},{19,3},{3,19},{20,4},{4,... | collective-permute-start | bytes 393224 | tf_op jit(solution)/shard_map/ppermute | solution.py:28
  76.2 0.7 slice_dynamic-update-slice_fusion.1
  76.9 2.3 %collective-permute-done.23 = bf16[2,64,512]{2,1,0:T(8,128)(2,1)S(1)} collective-permute-done((bf16[2,64,512]{2,1,0:T(8,128)(2,1)S(1)}, bf16[2,64,512]{2,1,0:T(8,128)(2,1)S(1)}, u32[]{:S(2)}, u32[]{:S(2)}) %collective-permute-start.23) | collective-permute-done | bytes 131104 | tf_op jit(solution)/shard_map/ppermute | solution.py:28
  79.3 0.7 slice_dynamic-update-slice_fusion
  79.9 0.7 collective-permute-done.24
  80.6 0.7 pad_maximum_fusion.3
  81.4 0.1 constant_dynamic-update-slice_fusion
  81.5 1.3 %copy-done.2 = bf16[2,128,4096]{2,1,0:T(8,128)(2,1)} copy-done((bf16[2,128,4096]{2,1,0:T(8,128)(2,1)}, bf16[2,128,4096]{2,1,0:T(8,128)(2,1)S(1)}, u32[]{:S(2)}) %copy-start.2) | copy-done | bytes 2097176
  (51 shorter events, 0.7 us)
Async XLA Ops:
  0.6 3.9 %copy-start = (bf16[2,128,4096]{2,1,0:T(8,128)(2,1)S(1)}, bf16[2,128,4096]{2,1,0:T(8,128)(2,1)}, u32[]{:S(2)}) copy-start(bf16[2,128,4096]{2,1,0:T(8,128)(2,1)} %refs_2_.3) | copy-start | bytes 6291460
  1.6 5.7 %collective-permute-start.4 = (bf16[64,512]{1,0:T(8,128)(2,1)S(1)}, bf16[64,512]{1,0:T(8,128)(2,1)S(1)}, u32[]{:S(2)}, u32[]{:S(2)}) collective-permute-start(bf16[64,512]{1,0:T(8,128)(2,1)S(1)} %pad_maximum_fusion.5), channel_id=1, source_target_pairs={{1,0},{0,1},{3,2},{2,3},{5,4},{4,5},{7,6},{6,7},{9,8},{8,9},{11,10... | collective-permute-start | bytes 196616 | tf_op jit(solution)/shard_map/ppermute | solution.py:28
  2.2 4.9 %copy-start.4 = (s32[2]{0:T(128)S(1)}, s32[2]{0:T(128)}, u32[]{:S(2)}) copy-start(s32[2]{0:T(128)} %param.11) | copy-start | bytes 28
  2.2 4.9 %copy-start.5 = (s32[2]{0:T(128)S(1)}, s32[2]{0:T(128)}, u32[]{:S(2)}) copy-start(s32[2]{0:T(128)} %param.10) | copy-start | bytes 28
  4.5 2.8 %copy-start.3 = (bf16[64,1024]{1,0:T(8,128)(2,1)S(1)}, bf16[64,1024]{1,0:T(8,128)(2,1)}, u32[]{:S(2)}) copy-start(bf16[64,1024]{1,0:T(8,128)(2,1)} %param.9) | copy-start | bytes 393220
  4.5 28.2 %collective-permute-start.1 = (bf16[2,128,2048]{2,1,0:T(8,128)(2,1)}, bf16[2,128,2048]{2,1,0:T(8,128)(2,1)S(1)}, u32[]{:S(2)}, u32[]{:S(2)}) collective-permute-start(bf16[2,128,2048]{2,1,0:T(8,128)(2,1)} %constant_dynamic-slice_fusion.9), channel_id=1, source_target_pairs={{1,0},{0,1},{3,2},{2,3},{5,4},{4,5},{7,6},{6,7},{9,8},{8,9},{11,10... | collective-permute-start | bytes 3145736 | tf_op jit(solution)/shard_map/ppermute | solution.py:28
  5.6 27.1 %collective-permute-start.2 = (bf16[2,128,2048]{2,1,0:T(8,128)(2,1)}, bf16[2,128,2048]{2,1,0:T(8,128)(2,1)S(1)}, u32[]{:S(2)}, u32[]{:S(2)}) collective-permute-start(bf16[2,128,2048]{2,1,0:T(8,128)(2,1)} %constant_dynamic-slice_fusion.8), channel_id=1, source_target_pairs={{1,0},{0,1},{3,2},{2,3},{5,4},{4,5},{7,6},{6,7},{9,8},{8,9},{11,10... | collective-permute-start | bytes 3145736 | tf_op jit(solution)/shard_map/ppermute | solution.py:28
  7.4 8.0 %collective-permute-start.10 = (bf16[1,2,64,256]{3,2,1,0:T(8,128)(2,1)S(1)}, bf16[1,2,64,256]{3,2,1,0:T(8,128)(2,1)S(1)}, u32[]{:S(2)}, u32[]{:S(2)}) collective-permute-start(bf16[1,2,64,256]{3,2,1,0:T(8,128)(2,1)S(1)} %maximum_bitcast_fusion.1), channel_id=1, source_target_pairs={{8,0},{9,1},{10,2},{11,3},{12,4},{13,5},{14,6},{15,7},{0,8},{1,9},... | collective-permute-start | bytes 196616 | tf_op jit(solution)/shard_map/ppermute | solution.py:28
  11.1 6.7 %collective-permute-start.11 = (bf16[1,2,64,256]{3,2,1,0:T(8,128)(2,1)S(1)}, bf16[1,2,64,256]{3,2,1,0:T(8,128)(2,1)S(1)}, u32[]{:S(2)}, u32[]{:S(2)}) collective-permute-start(bf16[1,2,64,256]{3,2,1,0:T(8,128)(2,1)S(1)} %maximum_bitcast_fusion.1), channel_id=1, source_target_pairs={{12,0},{13,1},{14,2},{15,3},{8,4},{9,5},{10,6},{11,7},{4,8},{5,9},... | collective-permute-start | bytes 196616 | tf_op jit(solution)/shard_map/ppermute | solution.py:28
  12.4 5.6 %collective-permute-start.9 = (bf16[1,2,64,256]{3,2,1,0:T(8,128)(2,1)S(1)}, bf16[1,2,64,256]{3,2,1,0:T(8,128)(2,1)S(1)}, u32[]{:S(2)}, u32[]{:S(2)}) collective-permute-start(bf16[1,2,64,256]{3,2,1,0:T(8,128)(2,1)S(1)} %maximum_bitcast_fusion.1), channel_id=1, source_target_pairs={{4,0},{5,1},{6,2},{7,3},{0,4},{1,5},{2,6},{3,7},{12,8},{13,9},{14,... | collective-permute-start | bytes 196616 | tf_op jit(solution)/shard_map/ppermute | solution.py:28
  15.4 17.3 %collective-permute-start.3 = (bf16[2,128,512]{2,1,0:T(8,128)(2,1)S(1)}, bf16[2,128,512]{2,1,0:T(8,128)(2,1)S(1)}, u32[]{:S(2)}, u32[]{:S(2)}) collective-permute-start(bf16[2,128,512]{2,1,0:T(8,128)(2,1)S(1)} %pad_maximum_fusion), channel_id=1, source_target_pairs={{1,0},{0,1},{3,2},{2,3},{5,4},{4,5},{7,6},{6,7},{9,8},{8,9},{11,10... | collective-permute-start | bytes 786440 | tf_op jit(solution)/shard_map/ppermute | solution.py:28
  17.8 1.2 %collective-permute-start = (s32[2,2]{1,0:T(2,128)S(1)}, s32[2,2]{1,0:T(2,128)S(1)}, u32[]{:S(2)}, u32[]{:S(2)}) collective-permute-start(s32[2,2]{1,0:T(2,128)S(1)} %reshape.18), channel_id=1, source_target_pairs={{1,0},{0,1},{3,2},{2,3},{5,4},{4,5},{7,6},{6,7},{9,8},{8,9},{11,10... | collective-permute-start | bytes 56 | tf_op jit(solution)/shard_map/ppermute | solution.py:28
  18.0 4.3 %collective-permute-start.5 = (bf16[1,2,64,256]{3,2,1,0:T(8,128)(2,1)S(1)}, bf16[1,2,64,256]{3,2,1,0:T(8,128)(2,1)S(1)}, u32[]{:S(2)}, u32[]{:S(2)}) collective-permute-start(bf16[1,2,64,256]{3,2,1,0:T(8,128)(2,1)S(1)} %maximum_bitcast_fusion), channel_id=1, source_target_pairs={{4,0},{5,1},{6,2},{7,3},{0,4},{1,5},{2,6},{3,7},{12,8},{13,9},{14,... | collective-permute-start | bytes 196616 | tf_op jit(solution)/shard_map/ppermute | solution.py:28
  18.9 5.6 %collective-permute-start.6 = (bf16[1,2,64,256]{3,2,1,0:T(8,128)(2,1)S(1)}, bf16[1,2,64,256]{3,2,1,0:T(8,128)(2,1)S(1)}, u32[]{:S(2)}, u32[]{:S(2)}) collective-permute-start(bf16[1,2,64,256]{3,2,1,0:T(8,128)(2,1)S(1)} %maximum_bitcast_fusion), channel_id=1, source_target_pairs={{8,0},{9,1},{10,2},{11,3},{12,4},{13,5},{14,6},{15,7},{0,8},{1,9},... | collective-permute-start | bytes 196616 | tf_op jit(solution)/shard_map/ppermute | solution.py:28
  22.3 10.4 %collective-permute-start.12 = (bf16[4,2,64,256]{3,2,1,0:T(8,128)(2,1)S(1)}, bf16[4,2,64,256]{3,2,1,0:T(8,128)(2,1)S(1)}, u32[]{:S(2)}, u32[]{:S(2)}) collective-permute-start(bf16[4,2,64,256]{3,2,1,0:T(8,128)(2,1)S(1)} %pad_maximum_fusion.2.refs_6_), channel_id=1, source_target_pairs={{2,0},{3,1},{0,2},{1,3},{6,4},{7,5},{4,6},{5,7},{10,8},{11,9},{8,1... | collective-permute-start | bytes 786440 | tf_op jit(solution)/shard_map/ppermute | solution.py:28
  24.5 6.6 %collective-permute-start.7 = (bf16[1,2,64,256]{3,2,1,0:T(8,128)(2,1)S(1)}, bf16[1,2,64,256]{3,2,1,0:T(8,128)(2,1)S(1)}, u32[]{:S(2)}, u32[]{:S(2)}) collective-permute-start(bf16[1,2,64,256]{3,2,1,0:T(8,128)(2,1)S(1)} %maximum_bitcast_fusion), channel_id=1, source_target_pairs={{12,0},{13,1},{14,2},{15,3},{8,4},{9,5},{10,6},{11,7},{4,8},{5,9},... | collective-permute-start | bytes 196616 | tf_op jit(solution)/shard_map/ppermute | solution.py:28
  31.1 13.8 %collective-permute-start.8 = (bf16[4,2,64,256]{3,2,1,0:T(8,128)(2,1)S(1)}, bf16[4,2,64,256]{3,2,1,0:T(8,128)(2,1)S(1)}, u32[]{:S(2)}, u32[]{:S(2)}) collective-permute-start(bf16[4,2,64,256]{3,2,1,0:T(8,128)(2,1)S(1)} %pad_maximum_fusion.1.refs_6_), channel_id=1, source_target_pairs={{2,0},{3,1},{0,2},{1,3},{6,4},{7,5},{4,6},{5,7},{10,8},{11,9},{8,1... | collective-permute-start | bytes 786440 | tf_op jit(solution)/shard_map/ppermute | solution.py:28
  40.7 16.5 %collective-permute-start.15 = (bf16[4,2,64,256]{3,2,1,0:T(8,128)(2,1)S(1)}, bf16[4,2,64,256]{3,2,1,0:T(8,128)(2,1)S(1)}, u32[]{:S(2)}, u32[]{:S(2)}) collective-permute-start(bf16[4,2,64,256]{3,2,1,0:T(8,128)(2,1)S(1)} %get-tuple-element.24), channel_id=1, source_target_pairs={{2,0},{3,1},{0,2},{1,3},{6,4},{7,5},{4,6},{5,7},{10,8},{11,9},{8,1... | collective-permute-start | bytes 786440 | tf_op jit(solution)/shard_map/ppermute | solution.py:28
  53.0 8.7 %collective-permute-start.19 = (bf16[4,2,64,256]{3,2,1,0:T(8,128)(2,1)S(1)}, bf16[4,2,64,256]{3,2,1,0:T(8,128)(2,1)S(1)}, u32[]{:S(2)}, u32[]{:S(2)}) collective-permute-start(bf16[4,2,64,256]{3,2,1,0:T(8,128)(2,1)S(1)} %get-tuple-element.26), channel_id=1, source_target_pairs={{2,0},{3,1},{0,2},{1,3},{6,4},{7,5},{4,6},{5,7},{10,8},{11,9},{8,1... | collective-permute-start | bytes 786440 | tf_op jit(solution)/shard_map/ppermute | solution.py:28
  56.7 19.5 %collective-permute-start.14 = (bf16[2,128,512]{2,1,0:T(8,128)(2,1)S(1)}, bf16[2,128,512]{2,1,0:T(8,128)(2,1)S(1)}, u32[]{:S(2)}, u32[]{:S(2)}) collective-permute-start(bf16[2,128,512]{2,1,0:T(8,128)(2,1)S(1)} %get-tuple-element.22), channel_id=1, source_target_pairs={{1,0},{0,1},{3,2},{2,3},{5,4},{4,5},{7,6},{6,7},{9,8},{8,9},{11,10... | collective-permute-start | bytes 786440 | tf_op jit(solution)/shard_map/ppermute | solution.py:28
  56.7 24.7 %collective-permute-start.13 = (bf16[2,128,2048]{2,1,0:T(8,128)(2,1)S(1)}, bf16[2,128,2048]{2,1,0:T(8,128)(2,1)S(1)}, u32[]{:S(2)}, u32[]{:S(2)}) collective-permute-start(bf16[2,128,2048]{2,1,0:T(8,128)(2,1)S(1)} %get-tuple-element.20), channel_id=1, source_target_pairs={{1,0},{0,1},{3,2},{2,3},{5,4},{4,5},{7,6},{6,7},{9,8},{8,9},{11,10... | collective-permute-start | bytes 3145736 | tf_op jit(solution)/shard_map/ppermute | solution.py:28
  57.3 4.6 %collective-permute-start.16 = (bf16[2,64,256]{2,1,0:T(8,128)(2,1)S(1)}, bf16[2,64,256]{2,1,0:T(8,128)(2,1)S(1)}, u32[]{:S(2)}, u32[]{:S(2)}) collective-permute-start(bf16[2,64,256]{2,1,0:T(8,128)(2,1)S(1)} %get-tuple-element.39), channel_id=1, source_target_pairs={{4,0},{5,1},{6,2},{7,3},{0,4},{1,5},{2,6},{3,7},{12,8},{13,9},{14,... | collective-permute-start | bytes 196616 | tf_op jit(solution)/shard_map/ppermute | solution.py:28
  58.6 7.3 %collective-permute-start.17 = (bf16[2,64,256]{2,1,0:T(8,128)(2,1)S(1)}, bf16[2,64,256]{2,1,0:T(8,128)(2,1)S(1)}, u32[]{:S(2)}, u32[]{:S(2)}) collective-permute-start(bf16[2,64,256]{2,1,0:T(8,128)(2,1)S(1)} %get-tuple-element.41), channel_id=1, source_target_pairs={{8,0},{9,1},{10,2},{11,3},{12,4},{13,5},{14,6},{15,7},{0,8},{1,9},... | collective-permute-start | bytes 196616 | tf_op jit(solution)/shard_map/ppermute | solution.py:28
  61.6 6.1 %collective-permute-start.18 = (bf16[2,64,256]{2,1,0:T(8,128)(2,1)S(1)}, bf16[2,64,256]{2,1,0:T(8,128)(2,1)S(1)}, u32[]{:S(2)}, u32[]{:S(2)}) collective-permute-start(bf16[2,64,256]{2,1,0:T(8,128)(2,1)S(1)} %get-tuple-element.40), channel_id=1, source_target_pairs={{12,0},{13,1},{14,2},{15,3},{8,4},{9,5},{10,6},{11,7},{4,8},{5,9},... | collective-permute-start | bytes 196616 | tf_op jit(solution)/shard_map/ppermute | solution.py:28
  61.9 19.5 %copy-start.1 = (bf16[2,128,4096]{2,1,0:T(8,128)(2,1)S(1)}, bf16[2,128,4096]{2,1,0:T(8,128)(2,1)}, u32[]{:S(2)}) copy-start(bf16[2,128,4096]{2,1,0:T(8,128)(2,1)} %get-tuple-element.19) | copy-start | bytes 6291460
  61.9 6.1 %collective-permute-start.20 = (bf16[2,64,256]{2,1,0:T(8,128)(2,1)S(1)}, bf16[2,64,256]{2,1,0:T(8,128)(2,1)S(1)}, u32[]{:S(2)}, u32[]{:S(2)}) collective-permute-start(bf16[2,64,256]{2,1,0:T(8,128)(2,1)S(1)} %get-tuple-element.42), channel_id=1, source_target_pairs={{4,0},{5,1},{6,2},{7,3},{0,4},{1,5},{2,6},{3,7},{12,8},{13,9},{14,... | collective-permute-start | bytes 196616 | tf_op jit(solution)/shard_map/ppermute | solution.py:28
  65.8 5.9 %collective-permute-start.21 = (bf16[2,64,256]{2,1,0:T(8,128)(2,1)S(1)}, bf16[2,64,256]{2,1,0:T(8,128)(2,1)S(1)}, u32[]{:S(2)}, u32[]{:S(2)}) collective-permute-start(bf16[2,64,256]{2,1,0:T(8,128)(2,1)S(1)} %get-tuple-element.44), channel_id=1, source_target_pairs={{8,0},{9,1},{10,2},{11,3},{12,4},{13,5},{14,6},{15,7},{0,8},{1,9},... | collective-permute-start | bytes 196616 | tf_op jit(solution)/shard_map/ppermute | solution.py:28
  67.7 6.1 %collective-permute-start.22 = (bf16[2,64,256]{2,1,0:T(8,128)(2,1)S(1)}, bf16[2,64,256]{2,1,0:T(8,128)(2,1)S(1)}, u32[]{:S(2)}, u32[]{:S(2)}) collective-permute-start(bf16[2,64,256]{2,1,0:T(8,128)(2,1)S(1)} %get-tuple-element.43), channel_id=1, source_target_pairs={{12,0},{13,1},{14,2},{15,3},{8,4},{9,5},{10,6},{11,7},{4,8},{5,9},... | collective-permute-start | bytes 196616 | tf_op jit(solution)/shard_map/ppermute | solution.py:28
  73.9 5.3 %collective-permute-start.23 = (bf16[2,64,512]{2,1,0:T(8,128)(2,1)S(1)}, bf16[2,64,512]{2,1,0:T(8,128)(2,1)S(1)}, u32[]{:S(2)}, u32[]{:S(2)}) collective-permute-start(bf16[2,64,512]{2,1,0:T(8,128)(2,1)S(1)} %pad_maximum_fusion.4), channel_id=1, source_target_pairs={{16,0},{0,16},{17,1},{1,17},{18,2},{2,18},{19,3},{3,19},{20,4},{4,... | collective-permute-start | bytes 393224 | tf_op jit(solution)/shard_map/ppermute | solution.py:28
  79.2 1.4 %collective-permute-start.24 = (f32[64,512]{1,0:T(8,128)S(1)}, f32[64,512]{1,0:T(8,128)S(1)}, u32[]{:S(2)}, u32[]{:S(2)}) collective-permute-start(f32[64,512]{1,0:T(8,128)S(1)} %get-tuple-element.38), channel_id=1, source_target_pairs={{1,0},{0,1},{3,2},{2,3},{5,4},{4,5},{7,6},{6,7},{9,8},{8,9},{11,10... | collective-permute-start | bytes 393224 | tf_op jit(solution)/shard_map/ppermute | solution.py:28
  81.5 1.3 %copy-start.2 = (bf16[2,128,4096]{2,1,0:T(8,128)(2,1)}, bf16[2,128,4096]{2,1,0:T(8,128)(2,1)S(1)}, u32[]{:S(2)}) copy-start(bf16[2,128,4096]{2,1,0:T(8,128)(2,1)S(1)} %constant_dynamic-update-slice_fusion) | copy-start | bytes 6291460
